TPU v7x, 128 devices: a whole 4x4x4 slice. The times are simulated.
128 devices in a mesh: batch: 8 (over x, core), rows: 16 (over z, y).
Axes of the slice: x: 4, y: 4, z: 4, core: 2. Of those that a mesh axis runs over, the one named last changes fastest.
Arguments:
- feat_quarter: bfloat16 [8, 256, 512, 256], P('batch', 'rows'), may hold values from -12 to 12
- feat_eighth: bfloat16 [8, 128, 256, 256], P('batch', 'rows'), may hold values from -12 to 12
- feat_sixteenth: bfloat16 [8, 64, 128, 256], P('batch', 'rows'), may hold values from -12 to 12
- feat_thirty: bfloat16 [8, 32, 64, 256], P('batch', 'rows'), may hold values from -12 to 12
- labels: int32 [8, 256, 512], P('batch', 'rows'), may hold values from 0 to 255, as said below
- first_weights: bfloat16 [4, 3, 3, 256, 128], replicated, may hold values from -0.125 to 0.125
- inner_weights: bfloat16 [3, 3, 3, 128, 128], replicated, may hold values from -0.1875 to 0.1875
- norm_gain: float32 [7, 128], replicated, may hold values from 0.1 to 1.9
- norm_shift: float32 [7, 128], replicated, may hold values from -3 to 3
- class_weight: bfloat16 [128, 19], replicated, may hold values from -0.5 to 0.5
- class_bias: float32 [19], replicated, may hold values from -3 to 3
Outputs:
- logits: bfloat16 [8, 19, 256, 512], P('batch', None, 'rows')
- mean_loss: float32 [], replicated
Inputs may be any that keep to these rules, and one draw needn't show every extreme that they name: `labels`: values 0 to 18 name classes; 255 marks a pixel without a label.
All inputs are finite; a program needn't handle non-finite values.
Results may differ from a plain program's by a relative error of at most 0.008.
Values may be sent and summed in bfloat16 or wider, within the bound.
No kernel may reach another device: no remote copies, remote signals or barrier semaphores. Data moves between devices by JAX's collectives and lax.ppermute only.
A program may use at most 128 MiB of HBM per device.

v0:
```python
import jax
import jax.numpy as jnp
import numpy as np
from jax import lax
from jax.experimental import pallas as pl
from jax.experimental.pallas import tpu as pltpu
from jax.sharding import Mesh
from jax.sharding import PartitionSpec as P

GROUPS = 32
GROUP = 4
HEAD = 128
ROWS = ("rows_0", "rows_1")
EVERY = ("batch_0", "batch_1", "rows_0", "rows_1")
BATCH = ("batch_0", "batch_1")
NORM_FLOOR = 0.05
DEPTHS = (1, 2, 3, 1)
STAT_ROWS = 48
SLOT = 32
F32, BF16 = jnp.float32, jnp.bfloat16
VMEM_LIMIT = 60 * 1024 * 1024


def doubling(cols):
    matrix = np.zeros((2 * cols, cols), np.float32)
    for k in range(cols):
        matrix[2 * k, k] += 0.75
        matrix[2 * k, max(k - 1, 0)] += 0.25
        matrix[2 * k + 1, k] += 0.75
        matrix[2 * k + 1, min(k + 1, cols - 1)] += 0.25
    return matrix


def everyone(pieces, axes):
    return lax.all_to_all(pieces, axes, 0, 0)


def matmul(a, b):
    return jnp.dot(a, b, preferred_element_type=F32)


def matmul_t(a, b):
    return lax.dot_general(a, b, (((1,), (1,)), ((), ())), preferred_element_type=F32)


def fill_pair(w_ref, out_ref, depth):
    zero = jnp.zeros((depth, HEAD), BF16)
    for j in range(4):
        for across in range(3):
            rows = slice(j * depth, (j + 1) * depth)
            at = across * 2 * HEAD
            out_ref[rows, at : at + HEAD] = w_ref[j, across] if j < 3 else zero
            out_ref[rows, at + HEAD : at + 2 * HEAD] = w_ref[j - 1, across] if j else zero


def fill_single(w_ref, out_ref, depth):
    for j in range(3):
        for across in range(3):
            out_ref[j * depth : (j + 1) * depth, across * HEAD : (across + 1) * HEAD] = w_ref[j, across]


def across_taps(z, width):
    pixels = z.shape[0]
    index = lax.broadcasted_iota(jnp.int32, (pixels, width), 0)
    left = jnp.where(index == 0, 0.0, pltpu.roll(z[:, :width], 1, 0))
    right = jnp.where(index == pixels - 1, 0.0, pltpu.roll(z[:, 2 * width :], pixels - 1, 0))
    return z[:, width : 2 * width] + left + right


def conv_pair(rows, w_ref):
    return across_taps(matmul(jnp.concatenate(rows, axis=1), w_ref[...]), 2 * HEAD)


def sums(y):
    total = jnp.sum(y, axis=0, keepdims=True)
    centred = y - total * (1.0 / y.shape[0])
    return total, jnp.sum(centred * centred, axis=0, keepdims=True)


def merge(parts, pixels):
    total = sum(p[0] for p in parts)
    mean = total * (1.0 / (pixels * len(parts)))
    square = sum(p[1] + pixels * jnp.square(p[0] * (1.0 / pixels) - mean) for p in parts)
    return total, square


def halves(pair):
    total, square = pair
    return [(total[:, :HEAD], square[:, :HEAD]), (total[:, HEAD:], square[:, HEAD:])]


def group_sum(v):
    lane = lax.broadcasted_iota(jnp.int32, v.shape, 1)
    v = v + jnp.where(lane % 2 == 0, pltpu.roll(v, HEAD - 1, 1), pltpu.roll(v, 1, 1))
    return v + jnp.where(lane % 4 < 2, pltpu.roll(v, HEAD - 2, 1), pltpu.roll(v, 2, 1))


def normed(y, mean, factor, shift):
    return jnp.maximum((y - mean) * factor + shift, 0.0).astype(BF16)


def split_rows(values):
    high = values.astype(BF16).astype(F32)
    rest = values - high
    middle = rest.astype(BF16).astype(F32)
    return [high, middle, rest - middle]


def edges_kernel(quarter, eighth, sixteenth, thirty, before, after, sems):
    copies, at = [], 0
    for level, feat in enumerate((quarter, eighth, sixteenth, thirty)):
        rows, cols, _ = feat.shape
        for i in range(DEPTHS[level]):
            spot = pl.ds(at + i * cols, cols)
            copies.append((feat.at[rows - DEPTHS[level] + i], before.at[spot]))
            copies.append((feat.at[i], after.at[spot]))
        at += DEPTHS[level] * cols
    started = [pltpu.make_async_copy(a, b, sems.at[i]) for i, (a, b) in enumerate(copies)]
    for copy in started:
        copy.start()
    for copy in started:
        copy.wait()


def inside_kernel(quarter, eighth, w0, w1, y0, y1, stats, wide0, wide1):
    fill_pair(w0, wide0, 2 * HEAD)
    fill_pair(w1, wide1, 2 * HEAD)
    stats[...] = jnp.zeros_like(stats)

    def work(x, wide, y, first):
        def step(p, carry):
            out = conv_pair([x[2 * p + j] for j in range(4)], wide)
            y[2 * p] = out[:, :HEAD]
            y[2 * p + 1] = out[:, HEAD:]
            total, square = sums(out)
            stats[first + p, 0:1] = total
            stats[first + p, 1:2] = square
            return carry

        lax.fori_loop(0, y.shape[0] // 2, step, 0)

    work(quarter, wide0, y0, 0)
    work(eighth, wide1, y1, y0.shape[0] // 2)


def outside_kernel(
    before, after, q_low, q_high, e_low, e_high, sixteenth, thirty, w0, w1, w2, w3, stats_in,
    y0, y1, y2, pieces, single0, wide1, wide2, wide3,
):
    depth = 2 * HEAD
    fill_single(w0, single0, depth)
    fill_pair(w1, wide1, depth)
    fill_pair(w2, wide2, depth)
    fill_pair(w3, wide3, depth)
    spots, at = [], 0
    cols = (q_low.shape[1], e_low.shape[1], sixteenth.shape[1], thirty.shape[1])
    for level in range(4):
        spots.append([slice(at + i * cols[level], at + (i + 1) * cols[level]) for i in range(DEPTHS[level])])
        at += DEPTHS[level] * cols[level]
    inside0 = 7
    quarter_parts, eighth_parts = [], []
    for p in range(inside0):
        quarter_parts += halves((stats_in[p, 0:1], stats_in[p, 1:2]))
    for p in range(inside0, inside0 + 3):
        eighth_parts += halves((stats_in[p, 0:1], stats_in[p, 1:2]))
    row_sets = (
        [before[spots[0][0]], q_low[0], q_low[1]],
        [q_high[0], q_high[1], after[spots[0][0]]],
    )
    for i, rows in enumerate(row_sets):
        out = across_taps(matmul(jnp.concatenate(rows, axis=1), single0[...]), HEAD)
        y0[i] = out
        quarter_parts.append(sums(out))
    row_sets = (
        [before[spots[1][0]], before[spots[1][1]], e_low[0], e_low[1]],
        [e_high[0], e_high[1], after[spots[1][0]], after[spots[1][1]]],
    )
    for i, rows in enumerate(row_sets):
        out = conv_pair(rows, wide1)
        y1[2 * i] = out[:, :HEAD]
        y1[2 * i + 1] = out[:, HEAD:]
        eighth_parts.append(halves(sums(out))[1 - i])
    rows = [before[s] for s in spots[2]]
    rows += [sixteenth[i] for i in range(sixteenth.shape[0])]
    rows += [after[s] for s in spots[2]]
    sixteenth_parts = []
    for p in range(y2.shape[0] // 2):
        out = conv_pair(rows[2 * p : 2 * p + 4], wide2)
        y2[2 * p] = out[:, :HEAD]
        y2[2 * p + 1] = out[:, HEAD:]
        if 0 < p < y2.shape[0] // 2 - 1:
            sixteenth_parts += halves(sums(out))
    out = conv_pair([before[spots[3][0]], thirty[0], thirty[1], after[spots[3][0]]], wide3)
    coarse = jnp.concatenate([out[:, :HEAD], out[:, HEAD:]], axis=0).astype(BF16)
    merged = [
        merge(quarter_parts, cols[0]), merge(eighth_parts, cols[1]), merge(sixteenth_parts, cols[2])
    ]
    pad = [jnp.zeros((5, HEAD), F32)]
    total = jnp.concatenate([m[0] for m in merged] + pad, axis=0)
    square = jnp.concatenate([m[1] for m in merged] + pad, axis=0)
    head = jnp.concatenate(split_rows(total) + split_rows(square), axis=0).astype(BF16)
    for i in range(pieces.shape[0]):
        pieces[i, :STAT_ROWS] = head
        pieces[i, STAT_ROWS:] = coarse


def between_kernel(
    place, got, y2, weights, gain, shift, up_small, up_big,
    y4, y6, params, pieces, fine, coarse, field5, stats5, wide0, wide1, wide2,
):
    members = got.shape[0]
    position = place[0]
    first, last = position == 0, position == members - 1
    for i, wide in enumerate((wide0, wide1, wide2)):
        fill_pair(weights.at[i], wide, HEAD)
    row = lax.broadcasted_iota(jnp.int32, (8, HEAD), 0)
    pixels = jnp.where(row == 0, 8192.0, jnp.where(row == 1, 2048.0, 512.0))

    def parts(i):
        block = got[i, :STAT_ROWS].astype(F32)
        return block[0:8] + block[8:16] + block[16:24], block[24:32] + block[32:40] + block[40:48]

    each = [parts(i) for i in range(members)]
    total = sum(p[0] for p in each)
    mean = group_sum(total) / (pixels * (members * GROUP))
    square = sum(p[1] + pixels * jnp.square(p[0] / pixels - mean) for p in each)
    var = group_sum(square) / (pixels * (members * GROUP))
    params[0] = mean
    params[1] = gain[...] * lax.rsqrt(var + NORM_FLOOR)
    params[2] = shift[...]

    def one(i, j):
        return params[i, j : j + 1]

    def local_norm(total, square, pixels, layer):
        total, square = (jnp.broadcast_to(v, (8, HEAD)) for v in (total, square))
        mean = group_sum(total) / (pixels * GROUP)
        square = square + pixels * jnp.square(total / pixels - mean)
        var = group_sum(square) / (pixels * GROUP)
        factor = gain[layer : layer + 1] * lax.rsqrt(var[0:1] + NORM_FLOOR)
        return mean[0:1], factor, shift[layer : layer + 1]

    def up_conv(acts, wide, out):
        count = len(acts)
        doubled = []
        for k in range(0, count, 2):
            both = matmul(up_big[...], jnp.concatenate([acts[k], acts[k + 1]], axis=1))
            doubled += [both[:, :HEAD], both[:, HEAD:]]
        lines = 2 * (count - 2)
        for k in range(1, count - 1):
            for half, other in ((0, k - 1), (1, k + 1)):
                line = 0.75 * doubled[k] + 0.25 * doubled[other]
                at = 2 * (k - 1) + half
                if at < 2:
                    line = jnp.where(first, 0.0, line)
                if at >= lines - 2:
                    line = jnp.where(last, 0.0, line)
                fine[at] = line.astype(BF16)
        own = []
        for p in range(lines // 2 - 1):
            y = conv_pair([fine[2 * p + j] for j in range(4)], wide)
            out[2 * p] = y[:, :HEAD]
            out[2 * p + 1] = y[:, HEAD:]
            two = halves(sums(y))
            own += two[1:] if p == 0 else two[:1] if p == lines // 2 - 2 else two
        return merge(own, y.shape[0])

    acts = [normed(y2[i], one(0, 2), one(1, 2), one(2, 2)) for i in range(y2.shape[0])]
    count = len(acts)
    acts[1] = jnp.where(first, acts[2], acts[1])
    acts[count - 2] = jnp.where(last, acts[count - 3], acts[count - 2])
    merged4 = up_conv(acts, wide0, y4)
    lines, cols = coarse.shape[0] - 2, coarse.shape[1]
    small = cols // 2
    total3 = jnp.zeros((1, HEAD), F32)
    for i in range(members):
        total3 = total3 + jnp.sum(got[i, STAT_ROWS:].astype(F32), axis=0, keepdims=True)
    count3 = members * 2 * small
    middle3 = total3 * (1.0 / count3)
    square3 = jnp.zeros((1, HEAD), F32)
    for i in range(members):
        square3 = square3 + jnp.sum(
            jnp.square(got[i, STAT_ROWS:].astype(F32) - middle3), axis=0, keepdims=True
        )
    norm3 = local_norm(total3, square3, count3, 3)
    doubled = []
    for i in range(members):
        a = normed(got[i, STAT_ROWS:].astype(F32), *norm3)
        both = matmul(up_small[...], jnp.concatenate([a[:small], a[small:]], axis=1))
        doubled += [both[:, :HEAD], both[:, HEAD:]]
    coarse[0] = jnp.zeros((cols, HEAD), BF16)
    coarse[lines + 1] = jnp.zeros((cols, HEAD), BF16)
    for k in range(len(doubled)):
        for half, other in ((0, max(k - 1, 0)), (1, min(k + 1, len(doubled) - 1))):
            coarse[1 + 2 * k + half] = (0.75 * doubled[k] + 0.25 * doubled[other]).astype(BF16)

    def step(p, carry):
        y = conv_pair([coarse[2 * p + j] for j in range(4)], wide1)
        field5[2 * p] = y[:, :HEAD]
        field5[2 * p + 1] = y[:, HEAD:]
        total, square = sums(y)
        stats5[p, 0:1] = total
        stats5[p, 1:2] = square
        return carry

    lax.fori_loop(0, lines // 2, step, 0)
    parts5 = []
    for p in range(lines // 2):
        parts5 += halves((stats5[p, 0:1], stats5[p, 1:2]))
    total5, square5 = merge(parts5, cols)
    norm5 = local_norm(total5, square5, lines * cols, 5)
    band = lines // members
    acts = []
    for i in range(band + 4):
        at = jnp.clip(position * band + (i - 2), 0, lines - 1)
        acts.append(normed(field5[at], *norm5))
    merged6 = up_conv(acts, wide2, y6)
    block = jnp.concatenate(
        [merged4[0], merged6[0], jnp.zeros((6, HEAD), F32), merged4[1], merged6[1], jnp.zeros((6, HEAD), F32)],
        axis=0,
    )
    for i in range(members):
        pieces[i] = block


def final_kernel(
    place, bias, got, params, gain, shift, y0, y0_edge, y1, y1_edge, y4, y6, labels, class_t, class_t3, up_cols,
    logits, pieces, lines, scores,
):
    members = got.shape[0]
    first, last = place[0] == 0, place[0] == members - 1
    pixels = 2048.0
    total = sum(got[i, 0:8] for i in range(members))
    mean = group_sum(total) / (pixels * members * GROUP)
    square = sum(got[i, 8:16] + pixels * jnp.square(got[i, 0:8] / pixels - mean) for i in range(members))
    var = group_sum(square) / (pixels * members * GROUP)
    scale = lax.rsqrt(var + NORM_FLOOR)
    norm4 = (mean[0:1], gain[4:5] * scale[0:1], shift[4:5])
    norm6 = (mean[1:2], gain[6:7] * scale[1:2], shift[6:7])
    norm0 = tuple(params[i, 0:1] for i in range(3))
    norm1 = tuple(params[i, 1:2] for i in range(3))
    count = y4.shape[0]
    for i in range(count):
        field1 = y1_edge[i] if i < 2 else y1_edge[i - count + 4] if i >= count - 2 else y1[i - 2]
        acts = jnp.concatenate(
            [normed(field1, *norm1), normed(y4[i], *norm4), normed(y6[i], *norm6)], axis=1
        )
        lines[i] = matmul_t(class_t3[...], acts)
    lines[0] = jnp.where(first, lines[1], lines[0])
    lines[count - 1] = jnp.where(last, lines[count - 2], lines[count - 1])
    doubled = []
    for i in range(count):
        value = lines[i]
        high = value.astype(BF16)
        low = (value - high.astype(F32)).astype(BF16)
        doubled.append(matmul(jnp.concatenate([high, low], axis=0), up_cols[...]))
    doubled = [d[:SLOT] + d[SLOT:] for d in doubled]
    rows = labels.shape[0]
    for r in range(rows):
        field0 = y0_edge[0] if r == 0 else y0_edge[1] if r == rows - 1 else y0[r - 1]
        k = r // 2 + 1
        other = k - 1 if r % 2 == 0 else k + 1
        value = matmul_t(class_t[...], normed(field0, *norm0))
        value = value + (0.75 * doubled[k] + 0.25 * doubled[other])
        for i in range(scores.shape[0]):
            scores[i, r * SLOT : (r + 1) * SLOT] = value[:, i * HEAD : (i + 1) * HEAD]
    label_map = labels[...]
    exps = jnp.zeros(label_map.shape, F32)
    picked = jnp.zeros(label_map.shape, F32)
    for c in range(logits.shape[0]):
        tiles = [scores.at[i][pl.ds(c, rows, stride=SLOT), :] for i in range(scores.shape[0])]
        score = jnp.concatenate(tiles, axis=1) + bias[c]
        logits[c] = score.astype(BF16)
        exps = exps + jnp.exp(score)
        picked = picked + jnp.where(label_map == c, score, 0.0)
    usable = label_map != 255
    terms = jnp.where(usable, jnp.log(exps) - picked, 0.0)
    counts = jnp.where(usable, 1.0, 0.0)
    out = []
    for v in (terms, counts):
        v = jnp.sum(v, axis=0, keepdims=True)
        out.append(sum(v[:, i * HEAD : (i + 1) * HEAD] for i in range(v.shape[1] // HEAD)))
    block = jnp.concatenate(out, axis=0)
    for i in range(pieces.shape[0]):
        pieces[i] = block


def params_of(**kw):
    return pltpu.CompilerParams(vmem_limit_bytes=VMEM_LIMIT, **kw)


def shaped(shape, dtype):
    return jax.ShapeDtypeStruct(shape, dtype)


VM = pl.BlockSpec(memory_space=pltpu.VMEM)
SM = pl.BlockSpec(memory_space=pltpu.SMEM)
ANY = pl.BlockSpec(memory_space=pl.ANY)


def block(shape, index):
    return pl.BlockSpec(shape, lambda i: index)


def per_device(
    feat_quarter,
    feat_eighth,
    feat_sixteenth,
    feat_thirty,
    labels,
    first_weights,
    inner_weights,
    norm_gain,
    norm_shift,
    class_weight,
    class_bias,
):
    position = lax.axis_index(ROWS)
    bands = lax.axis_size(ROWS)
    devices = bands * lax.axis_size(BATCH)
    place = position.astype(jnp.int32).reshape(1)
    up_pairs = [(i, i + 1) for i in range(bands - 1)]
    down_pairs = [(j, i) for i, j in up_pairs]
    feats = [feat_quarter[0], feat_eighth[0], feat_sixteenth[0], feat_thirty[0]]
    depth = feats[0].shape[2]
    halo = sum(d * f.shape[1] for d, f in zip(DEPTHS, feats))
    before, after = pl.pallas_call(
        edges_kernel,
        out_shape=[shaped((halo, depth), BF16)] * 2,
        in_specs=[ANY] * 4,
        out_specs=[ANY] * 2,
        scratch_shapes=[pltpu.SemaphoreType.DMA((2 * sum(DEPTHS),))],
        name="edges",
    )(*feats)
    before = lax.ppermute(before, ROWS, up_pairs)
    after = lax.ppermute(after, ROWS, down_pairs)
    q_rows, q_cols, _ = feats[0].shape
    e_rows, e_cols, _ = feats[1].shape
    s_rows, s_cols, _ = feats[2].shape
    t_rows, t_cols, _ = feats[3].shape
    wide = pltpu.VMEM((4 * depth, 6 * HEAD), BF16)
    y0, y1, stats = pl.pallas_call(
        inside_kernel,
        out_shape=[
            shaped((q_rows - 2, q_cols, HEAD), F32),
            shaped((e_rows - 2, e_cols, HEAD), F32),
            shaped(((q_rows + e_rows) // 2 - 2, 8, 2 * HEAD), F32),
        ],
        in_specs=[VM] * 4,
        out_specs=[VM] * 3,
        scratch_shapes=[wide, wide],
        compiler_params=params_of(),
        name="inside",
    )(feats[0], feats[1], first_weights[0], first_weights[1])
    whole = lambda a: block(a.shape, (0,) * a.ndim)
    args = [before, after, feats[0], feats[0], feats[1], feats[1], feats[2], feats[3]]
    specs = [
        whole(before), whole(after),
        block((2, q_cols, depth), (0, 0, 0)), block((2, q_cols, depth), (q_rows // 2 - 1, 0, 0)),
        block((2, e_cols, depth), (0, 0, 0)), block((2, e_cols, depth), (e_rows // 2 - 1, 0, 0)),
        whole(feats[2]), whole(feats[3]),
    ]
    for level in range(4):
        args.append(first_weights)
        specs.append(block((None,) + first_weights.shape[1:], (level, 0, 0, 0, 0)))
    args.append(stats)
    specs.append(whole(stats))
    piece = STAT_ROWS + t_rows * t_cols
    out_shape = [
        shaped((2, q_cols, HEAD), F32),
        shaped((4, e_cols, HEAD), F32),
        shaped((s_rows + 4, s_cols, HEAD), F32),
        shaped((bands, piece, HEAD), BF16),
    ]
    y0_edge, y1_edge, y2, pieces = pl.pallas_call(
        outside_kernel,
        grid=(1,),
        out_shape=out_shape,
        in_specs=specs,
        out_specs=[whole(s) for s in out_shape],
        scratch_shapes=[pltpu.VMEM((3 * depth, 3 * HEAD), BF16), wide, wide, wide],
        compiler_params=params_of(),
        name="outside",
    )(*args)
    got = everyone(pieces, ROWS)
    up_small = jnp.asarray(doubling(t_cols), BF16)
    up_big = jnp.asarray(doubling(s_cols), BF16)
    up_cols = jnp.asarray(doubling(e_cols).T, BF16)
    pad = ((0, 1), (0, 0))
    gain8, shift8 = jnp.pad(norm_gain, pad), jnp.pad(norm_shift, pad)
    narrow = pltpu.VMEM((4 * HEAD, 6 * HEAD), BF16)
    y4, y6, params, pieces = pl.pallas_call(
        between_kernel,
        out_shape=[
            shaped((e_rows + 2, e_cols, HEAD), F32),
            shaped((e_rows + 2, e_cols, HEAD), F32),
            shaped((3, 8, HEAD), F32),
            shaped((bands, 16, HEAD), F32),
        ],
        in_specs=[SM] + [VM] * 7,
        out_specs=[VM] * 4,
        scratch_shapes=[
            pltpu.VMEM((e_rows + 4, e_cols, HEAD), BF16),
            pltpu.VMEM((2 * t_rows * bands + 2, 2 * t_cols, HEAD), BF16),
            pltpu.VMEM((2 * t_rows * bands, 2 * t_cols, HEAD), F32),
            pltpu.VMEM((t_rows * bands, 8, 2 * HEAD), F32),
            narrow, narrow, narrow,
        ],
        compiler_params=params_of(),
        name="between",
    )(place, got, y2, inner_weights, gain8, shift8, up_small, up_big)
    got = everyone(pieces, ROWS)
    classes = class_weight.shape[1]
    class_t = jnp.pad(class_weight.T, ((0, SLOT - classes), (0, 0)))
    class_t3 = jnp.concatenate([class_t] * 3, axis=1)
    logits, pieces = pl.pallas_call(
        final_kernel,
        out_shape=[shaped((classes, q_rows, q_cols), BF16), shaped((devices, 2, HEAD), F32)],
        in_specs=[SM, SM] + [VM] * 14,
        out_specs=[VM] * 2,
        scratch_shapes=[
            pltpu.VMEM((e_rows + 2, SLOT, e_cols), F32),
            pltpu.VMEM((q_cols // HEAD, q_rows * SLOT, HEAD), F32),
        ],
        compiler_params=params_of(),
        name="final",
    )(
        place, class_bias, got, params, gain8, shift8, y0, y0_edge, y1, y1_edge, y4, y6, labels[0],
        class_t, class_t3, up_cols,
    )
    loss_total, valid_count = jnp.sum(everyone(pieces, EVERY), axis=(0, 2))
    mean_loss = loss_total / jnp.maximum(valid_count, 1.0)
    return (logits[None], mean_loss)


def solution(mesh):
    split = Mesh(mesh.devices.reshape(4, 2, 4, 4), ("batch_0", "batch_1", "rows_0", "rows_1"))
    in_specs = (
        P(BATCH, ROWS, None, None),
        P(BATCH, ROWS, None, None),
        P(BATCH, ROWS, None, None),
        P(BATCH, ROWS, None, None),
        P(BATCH, ROWS, None),
        P(),
        P(),
        P(),
        P(),
        P(),
        P(),
    )
    out_specs = (P(BATCH, None, ROWS, None), P())
    return jax.shard_map(
        per_device, mesh=split, in_specs=in_specs, out_specs=out_specs, check_vma=False
    )
```

profile of v0, /device:TPU:1, one launch (start us, length us, event | category | flops | bytes accessed | tf_op | source)
XLA Modules:
  0.0 158.0 jit_solution(978789698779675883)
XLA Ops:
  0.6 0.0 copy-start
  0.6 46.9 %edges.1 = (bf16[1472,256]{1,0:T(8,128)(2,1)}, bf16[1472,256]{1,0:T(8,128)(2,1)}) custom-call(bf16[16,512,256]{2,1,0:T(8,128)(2,1)} %bitcast.13, bf16[8,256,256]{2,1,0:T(8,128)(2,1)} %bitcast.17, bf16[4,128,256]{2,1,0:T(8,128)(2,1)} %bitcast.21, bf16[2,64,256]{2,1,0:T(8,128)(2,1)} %bitcast.23), custom_call_target="tpu_custom_call" | custom-call | tf_op jit(solution)/shard_map/edges/pallas_call | solution.py:427
  47.5 4.1 %collective-permute-start = (bf16[1472,256]{1,0:T(8,128)(2,1)}, bf16[1472,256]{1,0:T(8,128)(2,1)S(1)}, u32[]{:S(2)}, u32[]{:S(2)}) collective-permute-start(bf16[1472,256]{1,0:T(8,128)(2,1)} %get-tuple-element.17), channel_id=1, source_target_pairs={{0,1},{1,2},{2,3},{3,4},{4,5},{5,6},{6,7},{7,8},{8,9},{9,10},{10,1... | collective-permute-start | bytes 2261000 | tf_op jit(solution)/shard_map/ppermute | solution.py:435
  51.6 1.3 collective-permute-start.1
  52.9 0.0 copy-done
  52.9 1.2 slice_bitcast_fusion
  54.1 14.2 %inside.1 = (f32[14,512,128]{2,1,0:T(8,128)}, f32[6,256,128]{2,1,0:T(8,128)}, f32[10,8,256]{2,1,0:T(8,128)}) custom-call(bf16[16,512,256]{2,1,0:T(8,128)(2,1)} %bitcast.14, bf16[8,256,256]{2,1,0:T(8,128)(2,1)} %bitcast.18, bf16[3,3,256,128]{3,2,1,0:T(8,128)(2,1)} %get-tuple-element.33.w0, bf16[3,3,256,128]{3,2,1,0:T(8,128)(2,1)} %get-tuple-element.32.w1), custom_call_target="tpu_custom_call" | custom-call | tf_op jit(solution)/shard_map/inside/pallas_call | solution.py:442
  68.3 0.0 collective-permute-done.before
  68.3 0.0 copy-start.2
  68.3 3.0 %collective-permute-done.1.after = bf16[1472,256]{1,0:T(8,128)(2,1)} collective-permute-done((bf16[1472,256]{1,0:T(8,128)(2,1)}, bf16[1472,256]{1,0:T(8,128)(2,1)}, u32[]{:S(2)}, u32[]{:S(2)}) %collective-permute-start.1) | collective-permute-done | bytes 753696 | tf_op jit(solution)/shard_map/ppermute | solution.py:436
  71.3 0.0 copy-done.2
  71.3 0.0 copy-start.6
  71.3 0.0 copy-start.7
  71.3 6.8 %outside.1 = (f32[2,512,128]{2,1,0:T(8,128)}, f32[4,256,128]{2,1,0:T(8,128)}, f32[8,128,128]{2,1,0:T(8,128)}, bf16[16,176,128]{2,1,0:T(8,128)(2,1)}) custom-call(bf16[1472,256]{1,0:T(8,128)(2,1)} %copy-done.2, bf16[1472,256]{1,0:T(8,128)(2,1)} %collective-permute-done.1.after, bf16[16,512,256]{2,1,0:T(8,128)(2,1)} %bitcast.15, ...), custom_call_target="tpu_custom_call" | custom-call | tf_op jit(solution)/shard_map/outside/pallas_call | solution.py:475
  78.0 0.0 copy-start.5
  78.0 9.3 %all-to-all-start = ((bf16[16,176,128]{2,1,0:T(8,128)(2,1)}), bf16[16,176,128]{2,1,0:T(8,128)(2,1)S(1)}, u32[]{:S(2)}, u32[]{:S(2)}) async-start(bf16[16,176,128]{2,1,0:T(8,128)(2,1)} %get-tuple-element.20), calls=%async_computation | async-start | bytes 1441792 | tf_op jit(solution)/shard_map/all_to_all | solution.py:35
  87.4 0.0 copy-done.6
  87.4 0.6 pad.11.gain
  88.0 0.0 copy-done.7
  88.0 0.6 pad.12.shift
  88.6 10.5 %all-to-all-done.got = bf16[16,176,128]{2,1,0:T(8,128)(2,1)S(1)} async-done(((bf16[16,176,128]{2,1,0:T(8,128)(2,1)}), bf16[16,176,128]{2,1,0:T(8,128)(2,1)S(1)}, u32[]{:S(2)}, u32[]{:S(2)}) %all-to-all-start) | async-done | bytes 720928 | tf_op jit(solution)/shard_map/all_to_all | solution.py:35
  99.1 0.0 copy-start.1
  99.1 0.9 copy-done.1
  100.0 17.3 %between.1 = (f32[10,256,128]{2,1,0:T(8,128)}, f32[10,256,128]{2,1,0:T(8,128)}, f32[3,8,128]{2,1,0:T(8,128)}, f32[16,16,128]{2,1,0:T(8,128)}) custom-call(s32[1]{0:T(128)} %bitcast.place, bf16[16,176,128]{2,1,0:T(8,128)(2,1)} %copy-done.1, f32[8,128,128]{2,1,0:T(8,128)} %get-tuple-element.21.y2, bf16[3,3,3,128,128]{4,3,2,1,0:T(8,128)(2,1)} %weights.1, ...), custom_call_target="tpu_custom_call" | custom-call | tf_op jit(solution)/shard_map/between/pallas_call | solution.py:492
  117.3 3.7 %all-to-all-start.1 = ((f32[16,16,128]{2,1,0:T(8,128)}), f32[16,16,128]{2,1,0:T(8,128)S(1)}, u32[]{:S(2)}, u32[]{:S(2)}) async-start(f32[16,16,128]{2,1,0:T(8,128)} %get-tuple-element.22), calls=%async_computation.1 | async-start | bytes 262144 | tf_op jit(solution)/shard_map/all_to_all | solution.py:35
  121.0 0.0 copy-done.5
  121.0 0.0 copy-start.4
  121.0 0.6 pad_maximum_fusion.class_t3
  121.6 6.0 %all-to-all-done.1.got = f32[16,16,128]{2,1,0:T(8,128)S(1)} async-done(((f32[16,16,128]{2,1,0:T(8,128)}), f32[16,16,128]{2,1,0:T(8,128)S(1)}, u32[]{:S(2)}, u32[]{:S(2)}) %all-to-all-start.1) | async-done | bytes 131104 | tf_op jit(solution)/shard_map/all_to_all | solution.py:35
  127.6 0.0 copy-start.3
  127.6 0.0 copy-done.4
  127.6 0.6 copy-done.3
  128.3 7.0 %final.1 = (bf16[19,16,512]{2,1,0:T(8,128)(2,1)}, f32[128,2,128]{2,1,0:T(2,128)}) custom-call(s32[1]{0:T(128)} %bitcast.place, f32[19]{0:T(128)} %bias.1, f32[16,16,128]{2,1,0:T(8,128)} %copy-done.3, f32[3,8,128]{2,1,0:T(8,128)} %get-tuple-element.23.params, f32[8,128]{1,0:T(8,128)} %pad.11.gain, f32[8,128]{1,0:T(8,128)} %pad.12.shift, ...), custom_call_target="tpu_custom_call" | custom-call | tf_op jit(solution)/shard_map/final/pallas_call | solution.py:516
  135.3 19.4 %all_to_all.15 = f32[128,2,128]{2,1,0:T(2,128)S(1)} all-to-all(f32[128,2,128]{2,1,0:T(2,128)} %get-tuple-element.31), channel_id=1, replica_groups=mesh['batch_0'=4,'batch_1'=2,'rows_0'=4,'rows_1'=4] {'batch_0','batch_1'..., dimensions={0} | all-to-all | bytes 262144 | tf_op jit(solution)/shard_map/all_to_all | solution.py:35
  154.7 0.3 reduce_sum.9
  155.0 0.6 fusion
  (1 shorter events, 0.0 us)
Async XLA Ops:
  0.6 52.3 %copy-start = (bf16[4,3,3,256,128]{4,3,2,1,0:T(8,128)(2,1)S(1)}, bf16[4,3,3,256,128]{4,3,2,1,0:T(8,128)(2,1)}, u32[]{:S(2)}) copy-start(bf16[4,3,3,256,128]{4,3,2,1,0:T(8,128)(2,1)} %w3.1) | copy-start | bytes 7077892
  47.5 20.8 %collective-permute-start = (bf16[1472,256]{1,0:T(8,128)(2,1)}, bf16[1472,256]{1,0:T(8,128)(2,1)S(1)}, u32[]{:S(2)}, u32[]{:S(2)}) collective-permute-start(bf16[1472,256]{1,0:T(8,128)(2,1)} %get-tuple-element.17), channel_id=1, source_target_pairs={{0,1},{1,2},{2,3},{3,4},{4,5},{5,6},{6,7},{7,8},{8,9},{9,10},{10,1... | collective-permute-start | bytes 2261000 | tf_op jit(solution)/shard_map/ppermute | solution.py:435
  51.6 19.7 %collective-permute-start.1 = (bf16[1472,256]{1,0:T(8,128)(2,1)}, bf16[1472,256]{1,0:T(8,128)(2,1)}, u32[]{:S(2)}, u32[]{:S(2)}) collective-permute-start(bf16[1472,256]{1,0:T(8,128)(2,1)} %get-tuple-element.18), channel_id=1, source_target_pairs={{1,0},{2,1},{3,2},{4,3},{5,4},{6,5},{7,6},{8,7},{9,8},{10,9},{11,1... | collective-permute-start | bytes 2261000 | tf_op jit(solution)/shard_map/ppermute | solution.py:436
  68.3 3.0 %copy-start.2 = (bf16[1472,256]{1,0:T(8,128)(2,1)}, bf16[1472,256]{1,0:T(8,128)(2,1)S(1)}, u32[]{:S(2)}) copy-start(bf16[1472,256]{1,0:T(8,128)(2,1)S(1)} %collective-permute-done.before) | copy-start | bytes 2260996
  71.3 16.1 %copy-start.6 = (f32[7,128]{1,0:T(8,128)S(1)}, f32[7,128]{1,0:T(8,128)}, u32[]{:S(2)}) copy-start(f32[7,128]{1,0:T(8,128)} %param.21) | copy-start | bytes 10756
  71.3 16.7 %copy-start.7 = (f32[7,128]{1,0:T(8,128)S(1)}, f32[7,128]{1,0:T(8,128)}, u32[]{:S(2)}) copy-start(f32[7,128]{1,0:T(8,128)} %param.22) | copy-start | bytes 10756
  78.0 42.9 %copy-start.5 = (bf16[128,19]{0,1:T(8,128)(2,1)S(1)}, bf16[128,19]{0,1:T(8,128)(2,1)}, u32[]{:S(2)}) copy-start(bf16[128,19]{0,1:T(8,128)(2,1)} %param.23) | copy-start | bytes 14596
  78.0 21.1 %all-to-all-start = ((bf16[16,176,128]{2,1,0:T(8,128)(2,1)}), bf16[16,176,128]{2,1,0:T(8,128)(2,1)S(1)}, u32[]{:S(2)}, u32[]{:S(2)}) async-start(bf16[16,176,128]{2,1,0:T(8,128)(2,1)} %get-tuple-element.20), calls=%async_computation | async-start | bytes 1441792 | tf_op jit(solution)/shard_map/all_to_all | solution.py:35
  99.1 0.9 copy-start.1
  117.3 10.3 %all-to-all-start.1 = ((f32[16,16,128]{2,1,0:T(8,128)}), f32[16,16,128]{2,1,0:T(8,128)S(1)}, u32[]{:S(2)}, u32[]{:S(2)}) async-start(f32[16,16,128]{2,1,0:T(8,128)} %get-tuple-element.22), calls=%async_computation.1 | async-start | bytes 262144 | tf_op jit(solution)/shard_map/all_to_all | solution.py:35
  121.0 6.6 %copy-start.4 = (bf16[32,128]{1,0:T(8,128)(2,1)}, bf16[32,128]{1,0:T(8,128)(2,1)S(1)}, u32[]{:S(2)}) copy-start(bf16[32,128]{1,0:T(8,128)(2,1)S(1)} %pad.13.class_t) | copy-start | bytes 24580
  127.6 0.7 copy-start.3
where the time goes:
time: 158 us
  Pallas kernels  92.2 us (58%)
  waiting for transfers between devices  19.5 us (12%)
  blocking collectives  19.4 us (12%)
  starting transfers between devices  18.4 us (12%)
  local copies, waits for them, and re-layouts  4.49 us (3%)
  between operations  3.2 us (2%)
    pallas_call x1, Pallas kernels, per_device(): pl.pallas_call(edges_kernel, out_shape=[shaped((halo, depth), BF16)] * 2,...  46.9 us
    all_to_all x1, blocking collectives, everyone(): return lax.all_to_all(pieces, axes, 0, 0)  19.4 us
    pallas_call x1, Pallas kernels, per_device(): pl.pallas_call(between_kernel, out_shape=[shaped((e_rows + 2, e_cols, HEA...  17.3 us
    all_to_all x2, waiting for transfers between devices, everyone(): return lax.all_to_all(pieces, axes, 0, 0)  16.5 us
    pallas_call x1, Pallas kernels, per_device(): pl.pallas_call(inside_kernel, out_shape=[shaped((q_rows - 2, q_cols, HEAD...  14.2 us
    all_to_all x2, starting transfers between devices, everyone(): return lax.all_to_all(pieces, axes, 0, 0)  13 us
    pallas_call x1, Pallas kernels, per_device(): pl.pallas_call(final_kernel, out_shape=[shaped((classes, q_rows, q_cols),...  7.05 us
    pallas_call x1, Pallas kernels, per_device(): pl.pallas_call(outside_kernel, grid=(1,), out_shape=out_shape, in_specs=s...  6.77 us
  transfers between devices with their start and end apart: 4, of which 3 were waited for; matrix products, arithmetic and copies ran while one was open for 2% of the time, Pallas kernels for 9%

commit v1 on v0

v1 whole, which is shorter than its diff:
```python
import jax
import jax.numpy as jnp
import numpy as np
from jax import lax
from jax.experimental import pallas as pl
from jax.experimental.pallas import tpu as pltpu
from jax.sharding import Mesh
from jax.sharding import PartitionSpec as P

GROUP = 4
HEAD = 128
ROWS = ("rows_0", "rows_1")
EVERY = ("batch_0", "batch_1", "rows_0", "rows_1")
BATCH = ("batch_0", "batch_1")
NORM_FLOOR = 0.05
SMALL = (3, 1)
BIG = (1, 2)
STAT_ROWS = 32
EARLY = 3
SLOT = 32
F32, BF16 = jnp.float32, jnp.bfloat16
VMEM_LIMIT = 60 * 1024 * 1024


def doubling(cols):
    matrix = np.zeros((2 * cols, cols), np.float32)
    for k in range(cols):
        matrix[2 * k, k] += 0.75
        matrix[2 * k, max(k - 1, 0)] += 0.25
        matrix[2 * k + 1, k] += 0.75
        matrix[2 * k + 1, min(k + 1, cols - 1)] += 0.25
    return matrix


def everyone(pieces, axes):
    return lax.all_to_all(pieces, axes, 0, 0)


def matmul(a, b):
    return jnp.dot(a, b, preferred_element_type=F32)


def matmul_t(a, b):
    return lax.dot_general(a, b, (((1,), (1,)), ((), ())), preferred_element_type=F32)


def fill_pair(w_ref, out_ref, depth):
    zero = jnp.zeros((depth, HEAD), BF16)
    for j in range(4):
        for across in range(3):
            rows = slice(j * depth, (j + 1) * depth)
            at = across * 2 * HEAD
            out_ref[rows, at : at + HEAD] = w_ref[j, across] if j < 3 else zero
            out_ref[rows, at + HEAD : at + 2 * HEAD] = w_ref[j - 1, across] if j else zero


def across_taps(z, width, cols):
    pixels = z.shape[0]
    index = lax.broadcasted_iota(jnp.int32, (pixels, width), 0) % cols
    left = jnp.where(index == 0, 0.0, pltpu.roll(z[:, :width], 1, 0))
    right = jnp.where(index == cols - 1, 0.0, pltpu.roll(z[:, 2 * width :], pixels - 1, 0))
    return z[:, width : 2 * width] + left + right


def conv_pair(rows, w_ref):
    return across_taps(matmul(jnp.concatenate(rows, axis=1), w_ref[...]), 2 * HEAD, rows[0].shape[0])


def sums(y):
    total = jnp.sum(y, axis=0, keepdims=True)
    centred = y - total * (1.0 / y.shape[0])
    return total, jnp.sum(centred * centred, axis=0, keepdims=True)


def merge(parts, pixels):
    total = sum(p[0] for p in parts)
    mean = total * (1.0 / (pixels * len(parts)))
    square = sum(p[1] + pixels * jnp.square(p[0] * (1.0 / pixels) - mean) for p in parts)
    return total, square


def halves(pair):
    total, square = pair
    return [(total[:, :HEAD], square[:, :HEAD]), (total[:, HEAD:], square[:, HEAD:])]


def group_sum(v):
    lane = lax.broadcasted_iota(jnp.int32, v.shape, 1)
    v = v + jnp.where(lane % 2 == 0, pltpu.roll(v, HEAD - 1, 1), pltpu.roll(v, 1, 1))
    return v + jnp.where(lane % 4 < 2, pltpu.roll(v, HEAD - 2, 1), pltpu.roll(v, 2, 1))


def normed(y, mean, factor, shift):
    return jnp.maximum((y - mean) * factor + shift, 0.0).astype(BF16)


def split_rows(values):
    high = values.astype(BF16).astype(F32)
    rest = values - high
    middle = rest.astype(BF16).astype(F32)
    return [high, middle, rest - middle]


def edges_kernel(quarter, eighth, sixteenth, thirty, small_before, small_after, big_before, big_after, sems):
    copies = []
    groups = (
        (SMALL, (sixteenth, thirty), small_before, small_after),
        (BIG, (quarter, eighth), big_before, big_after),
    )
    for depths, feats, before, after in groups:
        at = 0
        for depth, feat in zip(depths, feats):
            rows, cols, _ = feat.shape
            for i in range(depth):
                spot = pl.ds(at, cols)
                copies.append((feat.at[rows - depth + i], before.at[spot]))
                copies.append((feat.at[i], after.at[spot]))
                at += cols
    started = [pltpu.make_async_copy(a, b, sems.at[i]) for i, (a, b) in enumerate(copies)]
    for copy in started:
        copy.start()
    for copy in started:
        copy.wait()


def store_pair(out, y, stats, step):
    y[0] = out[:, :HEAD]
    y[1] = out[:, HEAD:]
    total, square = sums(out)
    stats[step, 0:1] = total
    stats[step, 1:2] = square


def quarter_early_kernel(low, middle, high, w, y, stats, wide):
    step = pl.program_id(0)

    @pl.when(step == 0)
    def _():
        fill_pair(w, wide, 2 * HEAD)

    store_pair(conv_pair([low[0], middle[0], middle[1], high[0]], wide), y, stats, step)


def quarter_late_kernel(low, middle, high, before, after, w, _, __, y, stats, wide):
    step = pl.program_id(0)

    @pl.when(step == 0)
    def _():
        fill_pair(w, wide, 2 * HEAD)

    above = jnp.where(step == 0, before[...], low[0])
    below = jnp.where(step == pl.num_programs(0) - 1, after[...], high[0])
    store_pair(conv_pair([above, middle[0], middle[1], below], wide), y, stats, step)


def eighth_kernel(low, high, before, after, w, _, y, stats, wide):
    step = pl.program_id(0)
    cols = low.shape[1]

    @pl.when(step == 0)
    def _():
        fill_pair(w, wide, 2 * HEAD)

    at_first, at_last = step == 0, step == pl.num_programs(0) - 1
    rows = [jnp.where(at_first, before[i * cols : (i + 1) * cols], low[i]) for i in range(2)]
    rows += [jnp.where(at_last, after[i * cols : (i + 1) * cols], high[i]) for i in range(2)]
    store_pair(conv_pair(rows, wide), y, stats, step)


def coarse_kernel(before, after, sixteenth, thirty, w2, w3, _, y2, pieces, wide2, wide3):
    depth = 2 * HEAD
    fill_pair(w2, wide2, depth)
    fill_pair(w3, wide3, depth)
    own, cols, _ = sixteenth.shape
    ring = SMALL[0]
    rows = [before[i * cols : (i + 1) * cols] for i in range(ring)]
    rows += [sixteenth[i] for i in range(own)]
    rows += [after[i * cols : (i + 1) * cols] for i in range(ring)]
    parts = []
    for p in range(y2.shape[0] // 2):
        out = conv_pair(rows[2 * p : 2 * p + 4], wide2)
        y2[2 * p] = out[:, :HEAD]
        y2[2 * p + 1] = out[:, HEAD:]
        if 0 < p < y2.shape[0] // 2 - 1:
            parts += halves(sums(out))
    at = ring * cols
    out = conv_pair([before[at:], thirty[0], thirty[1], after[at:]], wide3)
    coarse = jnp.concatenate([out[:, :HEAD], out[:, HEAD:]], axis=0).astype(BF16)
    total, square = merge(parts, cols)
    values = jnp.concatenate([total, square, jnp.zeros((6, HEAD), F32)], axis=0)
    head = jnp.concatenate(split_rows(values) + [jnp.zeros((8, HEAD), F32)], axis=0).astype(BF16)
    for i in range(pieces.shape[0]):
        pieces[i, :STAT_ROWS] = head
        pieces[i, STAT_ROWS:] = coarse


def between_kernel(
    place, got, y2, weights, gain, shift, up_small, up_big, stats_early, stats_late, stats_eighth,
    y4, y6, pieces, fine, coarse, field5, stats5, wide0, wide1, wide2,
):
    members = got.shape[0]
    position = place[0]
    first, last = position == 0, position == members - 1
    for i, wide in enumerate((wide0, wide1, wide2)):
        fill_pair(weights.at[i], wide, HEAD)

    def merged_norm(each, pixels, layer):
        count = pixels * len(each) * GROUP
        mean = group_sum(jnp.broadcast_to(sum(p[0] for p in each), (8, HEAD)))[0:1] * (1.0 / count)
        square = sum(p[1] + pixels * jnp.square(p[0] * (1.0 / pixels) - mean) for p in each)
        var = group_sum(jnp.broadcast_to(square, (8, HEAD)))[0:1] * (1.0 / count)
        return mean, gain[layer : layer + 1] * lax.rsqrt(var + NORM_FLOOR), shift[layer : layer + 1]

    def up_conv(acts, wide, out):
        count = len(acts)
        doubled = []
        for k in range(0, count, 2):
            both = matmul(up_big[...], jnp.concatenate([acts[k], acts[k + 1]], axis=1))
            doubled += [both[:, :HEAD], both[:, HEAD:]]
        lines = 2 * (count - 2)
        for k in range(1, count - 1):
            for half, other in ((0, k - 1), (1, k + 1)):
                line = 0.75 * doubled[k] + 0.25 * doubled[other]
                at = 2 * (k - 1) + half
                if at < 2:
                    line = jnp.where(first, 0.0, line)
                if at >= lines - 2:
                    line = jnp.where(last, 0.0, line)
                fine[at] = line.astype(BF16)
        own = []
        for p in range(lines // 2 - 1):
            y = conv_pair([fine[2 * p + j] for j in range(4)], wide)
            out[2 * p] = y[:, :HEAD]
            out[2 * p + 1] = y[:, HEAD:]
            two = halves(sums(y))
            own += two[1:] if p == 0 else two[:1] if p == lines // 2 - 2 else two
        return merge(own, y.shape[0])

    lines, cols = coarse.shape[0] - 2, coarse.shape[1]
    small = cols // 2
    each3 = [sums(got[i, STAT_ROWS:].astype(F32)) for i in range(members)]
    norm3 = merged_norm(each3, 2 * small, 3)
    doubled = []
    for i in range(members):
        a = normed(got[i, STAT_ROWS:].astype(F32), *norm3)
        both = matmul(up_small[...], jnp.concatenate([a[:small], a[small:]], axis=1))
        doubled += [both[:, :HEAD], both[:, HEAD:]]
    coarse[0] = jnp.zeros((cols, HEAD), BF16)
    coarse[lines + 1] = jnp.zeros((cols, HEAD), BF16)
    for k in range(len(doubled)):
        for half, other in ((0, max(k - 1, 0)), (1, min(k + 1, len(doubled) - 1))):
            coarse[1 + 2 * k + half] = (0.75 * doubled[k] + 0.25 * doubled[other]).astype(BF16)
    fold = 4

    def step(q, carry):
        base = q * (2 * fold)
        lhs = jnp.concatenate(
            [
                jnp.concatenate([coarse[base + 2 * i + j] for j in range(4)], axis=1)
                for i in range(fold)
            ],
            axis=0,
        )
        y = across_taps(matmul(lhs, wide1[...]), 2 * HEAD, cols)
        for i in range(fold):
            field5[base + 2 * i] = y[i * cols : (i + 1) * cols, :HEAD]
            field5[base + 2 * i + 1] = y[i * cols : (i + 1) * cols, HEAD:]
        total, square = sums(y)
        stats5[q, 0:1] = total
        stats5[q, 1:2] = square
        return carry

    lax.fori_loop(0, lines // (2 * fold), step, 0, unroll=2)
    blocks = [got[i, :STAT_ROWS].astype(F32) for i in range(members)]
    blocks = [b[0:8] + b[8:16] + b[16:24] for b in blocks]
    norm2 = merged_norm([(b[0:1], b[1:2]) for b in blocks], y2.shape[1] * (y2.shape[0] - 4), 2)
    acts = [normed(y2[i], *norm2) for i in range(y2.shape[0])]
    count = len(acts)
    acts[1] = jnp.where(first, acts[2], acts[1])
    acts[count - 2] = jnp.where(last, acts[count - 3], acts[count - 2])
    merged4 = up_conv(acts, wide0, y4)
    parts5 = []
    for q in range(lines // (2 * fold)):
        parts5 += halves((stats5[q, 0:1], stats5[q, 1:2]))
    norm5 = merged_norm(parts5, cols * fold, 5)
    band = lines // members
    acts = []
    for i in range(band + 4):
        at = jnp.clip(position * band + (i - 2), 0, lines - 1)
        acts.append(normed(field5[at], *norm5))
    merged6 = up_conv(acts, wide2, y6)
    parts0, parts1 = [], []
    for stats in (stats_early, stats_late):
        for p in range(stats.shape[0]):
            parts0 += halves((stats[p, 0:1], stats[p, 1:2]))
    for p in range(stats_eighth.shape[0]):
        two = halves((stats_eighth[p, 0:1], stats_eighth[p, 1:2]))
        parts1 += two[1:] if p == 0 else two[:1] if p == stats_eighth.shape[0] - 1 else two
    eighth_cols = y4.shape[1]
    merged = [merge(parts0, 2 * eighth_cols), merge(parts1, eighth_cols), merged4, merged6]
    pad = [jnp.zeros((4, HEAD), F32)]
    block = jnp.concatenate([m[0] for m in merged] + pad + [m[1] for m in merged] + pad, axis=0)
    for i in range(members):
        pieces[i] = block


def final_kernel(
    place, bias, got, gain, shift, y0, y1, y4, y6, labels, class_t, class_t3, up_cols,
    logits, pieces, lines, doubled, scores, norms,
):
    members = got.shape[0]
    step = pl.program_id(0)
    count = y4.shape[0]

    @pl.when(step == 0)
    def _():
        first, last = place[0] == 0, place[0] == members - 1
        row = lax.broadcasted_iota(jnp.int32, (8, HEAD), 0)
        own = float((count - 2) * y4.shape[1])
        pixels = jnp.where(row == 0, 4.0 * own, own)
        total = sum(got[i, 0:8] for i in range(members))
        mean = group_sum(total) / (pixels * (members * GROUP))
        square = sum(got[i, 8:16] + pixels * jnp.square(got[i, 0:8] / pixels - mean) for i in range(members))
        scale = lax.rsqrt(group_sum(square) / (pixels * (members * GROUP)) + NORM_FLOOR)
        layers = (0, 1, 4, 6)
        norm = [
            (mean[j : j + 1], gain[layer : layer + 1] * scale[j : j + 1], shift[layer : layer + 1])
            for j, layer in enumerate(layers)
        ]
        for i in range(3):
            norms[i : i + 1] = norm[0][i]
        for i in range(count):
            acts = [normed(y[i], *norm[1 + j]) for j, y in enumerate((y1, y4, y6))]
            lines[i] = matmul_t(class_t3[...], jnp.concatenate(acts, axis=1))
        lines[0] = jnp.where(first, lines[1], lines[0])
        lines[count - 1] = jnp.where(last, lines[count - 2], lines[count - 1])
        for i in range(count):
            value = lines[i]
            high = value.astype(BF16)
            low = (value - high.astype(F32)).astype(BF16)
            both = matmul(jnp.concatenate([high, low], axis=0), up_cols[...])
            doubled[i] = both[:SLOT] + both[SLOT:]

    norm0 = tuple(norms[i : i + 1] for i in range(3))
    centre = 0.75 * doubled[step + 1]
    for half in range(2):
        value = matmul_t(class_t[...], normed(y0[half], *norm0))
        value = value + (centre + 0.25 * doubled[step + 2 * half])
        at = pl.multiple_of((2 * step + half) * SLOT, SLOT)
        for i in range(scores.shape[0]):
            scores[i, pl.ds(at, SLOT)] = value[:, i * HEAD : (i + 1) * HEAD]

    @pl.when(step == pl.num_programs(0) - 1)
    def _():
        label_map = labels[...]
        rows = label_map.shape[0]
        exps = jnp.zeros(label_map.shape, F32)
        picked = jnp.zeros(label_map.shape, F32)
        for c in range(logits.shape[0]):
            tiles = [scores.at[i][pl.ds(c, rows, stride=SLOT), :] for i in range(scores.shape[0])]
            score = jnp.concatenate(tiles, axis=1) + bias[c]
            logits[c] = score.astype(BF16)
            exps = exps + jnp.exp(score)
            picked = picked + jnp.where(label_map == c, score, 0.0)
        usable = label_map != 255
        terms = jnp.where(usable, jnp.log(exps) - picked, 0.0)
        counts = jnp.where(usable, 1.0, 0.0)
        out = []
        for v in (terms, counts):
            v = jnp.sum(v, axis=0, keepdims=True)
            out.append(sum(v[:, i * HEAD : (i + 1) * HEAD] for i in range(v.shape[1] // HEAD)))
        both = jnp.concatenate(out, axis=0)
        for i in range(pieces.shape[0]):
            pieces[i] = both


def params_of(**kw):
    return pltpu.CompilerParams(vmem_limit_bytes=VMEM_LIMIT, **kw)


def shaped(shape, dtype):
    return jax.ShapeDtypeStruct(shape, dtype)


VM = pl.BlockSpec(memory_space=pltpu.VMEM)
SM = pl.BlockSpec(memory_space=pltpu.SMEM)
ANY = pl.BlockSpec(memory_space=pl.ANY)


def device_step(
    feat_quarter,
    feat_eighth,
    feat_sixteenth,
    feat_thirty,
    labels,
    first_weights,
    inner_weights,
    norm_gain,
    norm_shift,
    class_weight,
    class_bias,
):
    position = lax.axis_index(ROWS)
    bands = lax.axis_size(ROWS)
    devices = bands * lax.axis_size(BATCH)
    place = position.astype(jnp.int32).reshape(1)
    up_pairs = [(i, i + 1) for i in range(bands - 1)]
    down_pairs = [(j, i) for i, j in up_pairs]
    feats = [feat_quarter[0], feat_eighth[0], feat_sixteenth[0], feat_thirty[0]]
    quarter, eighth, sixteenth, thirty = feats
    q_rows, q_cols, depth = quarter.shape
    e_rows, e_cols, _ = eighth.shape
    s_rows, s_cols, _ = sixteenth.shape
    t_rows, t_cols, _ = thirty.shape
    small = shaped((SMALL[0] * s_cols + SMALL[1] * t_cols, depth), BF16)
    big = shaped((BIG[0] * q_cols + BIG[1] * e_cols, depth), BF16)
    small_before, small_after, big_before, big_after = pl.pallas_call(
        edges_kernel,
        out_shape=[small, small, big, big],
        in_specs=[ANY] * 4,
        out_specs=[VM] * 4,
        scratch_shapes=[pltpu.SemaphoreType.DMA((2 * (sum(SMALL) + sum(BIG)),))],
        compiler_params=params_of(),
        name="edges",
    )(*feats)
    small_before = lax.ppermute(small_before, ROWS, up_pairs)
    small_after = lax.ppermute(small_after, ROWS, down_pairs)
    big_before = lax.ppermute(big_before, ROWS, up_pairs)
    big_after = lax.ppermute(big_after, ROWS, down_pairs)

    def fixed(a, *index):
        index = index or (0,) * len(a.shape)
        return pl.BlockSpec(a.shape, lambda i: index)

    def weight(level):
        return pl.BlockSpec((None,) + first_weights.shape[1:], lambda i: (level, 0, 0, 0, 0))

    wide = pltpu.VMEM((4 * depth, 6 * HEAD), BF16)
    pairs = q_rows // 2
    line = (1, q_cols, depth)

    def quarter_specs(pair):
        return [
            pl.BlockSpec(line, lambda i: (jnp.maximum(2 * pair(i) - 1, 0), 0, 0)),
            pl.BlockSpec((2, q_cols, depth), lambda i: (pair(i), 0, 0)),
            pl.BlockSpec(line, lambda i: (jnp.minimum(2 * pair(i) + 2, q_rows - 1), 0, 0)),
        ]

    early = lambda i: i + 1
    late = lambda i: jnp.where(i == 0, 0, i + EARLY)
    field = shaped((q_rows, q_cols, HEAD), F32)
    stats_shape = lambda n: shaped((n, 8, 2 * HEAD), F32)
    early_call = pl.pallas_call(
        quarter_early_kernel,
        grid=(EARLY,),
        out_shape=[field, stats_shape(EARLY)],
        in_specs=quarter_specs(early) + [weight(0)],
        out_specs=[
            pl.BlockSpec((2, q_cols, HEAD), lambda i: (early(i), 0, 0)), fixed(stats_shape(EARLY))
        ],
        scratch_shapes=[wide],
        compiler_params=params_of(),
        name="quarter_early",
    )
    y0, stats_early = early_call(quarter, quarter, quarter, first_weights)
    piece = shaped((bands, STAT_ROWS + t_rows * t_cols, HEAD), BF16)
    y2_shape = shaped((s_rows + 4, s_cols, HEAD), F32)
    y2, pieces = pl.pallas_call(
        coarse_kernel,
        grid=(1,),
        out_shape=[y2_shape, piece],
        in_specs=[fixed(small), fixed(small), fixed(sixteenth), fixed(thirty), weight(2), weight(3), ANY],
        out_specs=[fixed(y2_shape), fixed(piece)],
        scratch_shapes=[wide, wide],
        compiler_params=params_of(),
        name="coarse",
    )(small_before, small_after, sixteenth, thirty, first_weights, first_weights, stats_early)
    got = everyone(pieces, ROWS)
    y0, stats_late = pl.pallas_call(
        quarter_late_kernel,
        grid=(pairs - EARLY,),
        out_shape=[field, stats_shape(pairs - EARLY)],
        in_specs=quarter_specs(late)
        + [pl.BlockSpec((q_cols, depth), lambda i: (0, 0))] * 2
        + [weight(0), ANY, ANY],
        out_specs=[
            pl.BlockSpec((2, q_cols, HEAD), lambda i: (late(i), 0, 0)), fixed(stats_shape(pairs - EARLY))
        ],
        input_output_aliases={6: 0},
        scratch_shapes=[wide],
        compiler_params=params_of(),
        name="quarter_late",
    )(quarter, quarter, quarter, big_before, big_after, first_weights, y0, y2)
    steps = e_rows // 2 + 1
    halo = pl.BlockSpec((BIG[1] * e_cols, depth), lambda i: (BIG[0] * q_cols // (BIG[1] * e_cols), 0))
    two = (2, e_cols, depth)
    y1, stats_eighth = pl.pallas_call(
        eighth_kernel,
        grid=(steps,),
        out_shape=[shaped((e_rows + 2, e_cols, HEAD), F32), stats_shape(steps)],
        in_specs=[
            pl.BlockSpec(two, lambda i: (jnp.maximum(i - 1, 0), 0, 0)),
            pl.BlockSpec(two, lambda i: (jnp.minimum(i, steps - 2), 0, 0)),
            halo, halo, weight(1), ANY,
        ],
        out_specs=[pl.BlockSpec((2, e_cols, HEAD), lambda i: (i, 0, 0)), fixed(stats_shape(steps))],
        scratch_shapes=[wide],
        compiler_params=params_of(),
        name="eighth",
    )(eighth, eighth, big_before, big_after, first_weights, y2)
    up_small = jnp.asarray(doubling(t_cols), BF16)
    up_big = jnp.asarray(doubling(s_cols), BF16)
    up_cols = jnp.asarray(doubling(e_cols).T, BF16)
    narrow = pltpu.VMEM((4 * HEAD, 6 * HEAD), BF16)
    y4, y6, pieces = pl.pallas_call(
        between_kernel,
        out_shape=[
            shaped((e_rows + 2, e_cols, HEAD), F32),
            shaped((e_rows + 2, e_cols, HEAD), F32),
            shaped((bands, 16, HEAD), F32),
        ],
        in_specs=[SM] + [VM] * 10,
        out_specs=[VM] * 3,
        scratch_shapes=[
            pltpu.VMEM((e_rows + 4, e_cols, HEAD), BF16),
            pltpu.VMEM((2 * t_rows * bands + 2, 2 * t_cols, HEAD), BF16),
            pltpu.VMEM((2 * t_rows * bands, 2 * t_cols, HEAD), F32),
            pltpu.VMEM((t_rows * bands, 8, 2 * HEAD), F32),
            narrow, narrow, narrow,
        ],
        compiler_params=params_of(),
        name="between",
    )(
        place, got, y2, inner_weights, norm_gain, norm_shift, up_small, up_big,
        stats_early, stats_late, stats_eighth,
    )
    got = everyone(pieces, ROWS)
    classes = class_weight.shape[1]
    class_t = jnp.pad(class_weight.T, ((0, SLOT - classes), (0, 0)))
    class_t3 = jnp.concatenate([class_t] * 3, axis=1)
    out_shape = [shaped((classes, q_rows, q_cols), BF16), shaped((devices, 2, HEAD), F32)]
    args = [got, norm_gain, norm_shift, y0, y1, y4, y6, labels[0], class_t, class_t3, up_cols]
    specs = [fixed(a) for a in args]
    specs[3] = pl.BlockSpec((2, q_cols, HEAD), lambda i: (i, 0, 0))
    logits, pieces = pl.pallas_call(
        final_kernel,
        grid=(pairs,),
        out_shape=out_shape,
        in_specs=[SM, SM] + specs,
        out_specs=[fixed(a) for a in out_shape],
        scratch_shapes=[
            pltpu.VMEM((e_rows + 2, SLOT, e_cols), F32),
            pltpu.VMEM((e_rows + 2, SLOT, q_cols), F32),
            pltpu.VMEM((q_cols // HEAD, q_rows * SLOT, HEAD), F32),
            pltpu.VMEM((8, HEAD), F32),
        ],
        compiler_params=params_of(),
        name="final",
    )(place, class_bias, *args)
    loss_total, valid_count = jnp.sum(everyone(pieces, EVERY), axis=(0, 2))
    mean_loss = loss_total / jnp.maximum(valid_count, 1.0)
    return (logits[None], mean_loss)


def solution(mesh):
    split = Mesh(mesh.devices.reshape(4, 2, 4, 4), ("batch_0", "batch_1", "rows_0", "rows_1"))
    in_specs = (
        P(BATCH, ROWS, None, None),
        P(BATCH, ROWS, None, None),
        P(BATCH, ROWS, None, None),
        P(BATCH, ROWS, None, None),
        P(BATCH, ROWS, None),
        P(),
        P(),
        P(),
        P(),
        P(),
        P(),
    )
    out_specs = (P(BATCH, None, ROWS, None), P())
    return jax.shard_map(
        device_step, mesh=split, in_specs=in_specs, out_specs=out_specs, check_vma=False
    )
```

time: 158 us -> 124 us (0.78)
  Pallas kernels: 92.2 us -> 48.5 us
  starting transfers between devices: 18.4 us -> 25.6 us
  waiting for transfers between devices: 19.5 us -> 21.8 us
    pallas_call x5 -> x7, Pallas kernels: 92.2 us -> 48.5 us  [the longest x1 11.5 us: device_step(): pl.pallas_call(between_kernel, out_shape=[shaped((e_rows + 2, e_cols, HEA...]
    ppermute x2 -> x4, waiting for transfers between devices: 2.96 us -> 15.6 us  [the longest x1 12 us: device_step(): big_before = lax.ppermute(big_before, ROWS, up_pairs)]
    all_to_all x2, waiting for transfers between devices: 16.5 us -> 6.2 us  [everyone(): return lax.all_to_all(pieces, axes, 0, 0)]
    ppermute x2 -> x4, starting transfers between devices: 5.36 us -> 9.91 us  [the longest x1 4.03 us: device_step(): small_before = lax.ppermute(small_before, ROWS, up_pairs)]
    all_to_all x2, starting transfers between devices: 13 us -> 15.7 us  [everyone(): return lax.all_to_all(pieces, axes, 0, 0)]
  transfers between devices with their start and end apart: 4 -> 6, of which waited for: 3 -> 4; matrix products, arithmetic and copies ran while one was open for 2% -> 0% of each run, Pallas kernels for 9% -> 17%
where the time goes in v1:
time: 124 us; the launch traced here: 123 us
  Pallas kernels  48.5 us (39%)
  starting transfers between devices  25.6 us (21%)
  waiting for transfers between devices  21.8 us (18%)
  blocking collectives  19.6 us (16%)
  local copies, waits for them, and re-layouts  3.6 us (3%)
  between operations  3.17 us (3%)
    all_to_all x1, blocking collectives, everyone(): return lax.all_to_all(pieces, axes, 0, 0)  19.6 us
    all_to_all x2, starting transfers between devices, everyone(): return lax.all_to_all(pieces, axes, 0, 0)  15.7 us
    ppermute x1, waiting for transfers between devices, device_step(): big_before = lax.ppermute(big_before, ROWS, up_pairs)  12 us
    pallas_call x1, Pallas kernels, device_step(): pl.pallas_call(between_kernel, out_shape=[shaped((e_rows + 2, e_cols, HEA...  11.5 us
    pallas_call x1, Pallas kernels, device_step(): pl.pallas_call(final_kernel, grid=(pairs,), out_shape=out_shape, in_specs...  9.67 us
    pallas_call x1, Pallas kernels, device_step(): pl.pallas_call(quarter_late_kernel, grid=(pairs - EARLY,), out_shape=[fie...  8.47 us
    pallas_call x1, Pallas kernels, device_step(): pl.pallas_call(eighth_kernel, grid=(steps,), out_shape=[shaped((e_rows +...  6.26 us
    all_to_all x2, waiting for transfers between devices, everyone(): return lax.all_to_all(pieces, axes, 0, 0)  6.2 us
  transfers between devices with their start and end apart: 6, of which 4 were waited for; matrix products, arithmetic and copies ran while one was open for 0% of the time, Pallas kernels for 17%

profile of v1, /device:TPU:1, one launch (start us, length us, event | category | flops | bytes accessed | tf_op | source)
XLA Modules:
  0.0 123.2 jit_solution(5521442156241700144)
XLA Ops:
  0.6 2.6 %edges.1 = (bf16[448,256]{1,0:T(8,128)(2,1)}, bf16[448,256]{1,0:T(8,128)(2,1)}, bf16[1024,256]{1,0:T(8,128)(2,1)}, bf16[1024,256]{1,0:T(8,128)(2,1)}) custom-call(bf16[16,512,256]{2,1,0:T(8,128)(2,1)} %bitcast.9, bf16[8,256,256]{2,1,0:T(8,128)(2,1)} %bitcast.16, bf16[4,128,256]{2,1,0:T(8,128)(2,1)} %bitcast.19, bf16[2,64,256]{2,1,0:T(8,128)(2,1)} %bitcast.21), custom_call_target="tpu_custom_call" | custom-call | tf_op jit(solution)/shard_map/edges/pallas_call | solution.py:417
  3.3 4.0 %collective-permute-start = (bf16[448,256]{1,0:T(8,128)(2,1)}, bf16[448,256]{1,0:T(8,128)(2,1)S(1)}, u32[]{:S(2)}, u32[]{:S(2)}) collective-permute-start(bf16[448,256]{1,0:T(8,128)(2,1)} %get-tuple-element.19), channel_id=1, source_target_pairs={{0,1},{1,2},{2,3},{3,4},{4,5},{5,6},{6,7},{7,8},{8,9},{9,10},{10,1... | collective-permute-start | bytes 688136 | tf_op jit(solution)/shard_map/ppermute | solution.py:426
  7.3 1.3 %collective-permute-start.1 = (bf16[448,256]{1,0:T(8,128)(2,1)}, bf16[448,256]{1,0:T(8,128)(2,1)S(1)}, u32[]{:S(2)}, u32[]{:S(2)}) collective-permute-start(bf16[448,256]{1,0:T(8,128)(2,1)} %get-tuple-element.20), channel_id=1, source_target_pairs={{1,0},{2,1},{3,2},{4,3},{5,4},{6,5},{7,6},{8,7},{9,8},{10,9},{11,1... | collective-permute-start | bytes 688136 | tf_op jit(solution)/shard_map/ppermute | solution.py:427
  8.6 5.9 %quarter_early.1 = (f32[16,512,128]{2,1,0:T(8,128)}, f32[3,8,256]{2,1,0:T(8,128)}) custom-call(bf16[16,512,256]{2,1,0:T(8,128)(2,1)} %bitcast.10, bf16[16,512,256]{2,1,0:T(8,128)(2,1)} %bitcast.11, bf16[16,512,256]{2,1,0:T(8,128)(2,1)} %bitcast.12, bf16[4,3,3,256,128]{4,3,2,1,0:T(8,128)(2,1)} %w.5), custom_call_target="tpu_custom_call" | custom-call | tf_op jit(solution)/shard_map/quarter_early/pallas_call | solution.py:465
  14.6 0.0 collective-permute-done.before
  14.6 0.0 copy-start.4
  14.6 1.1 collective-permute-done.1.after
  15.6 0.0 copy-start.5
  15.6 0.0 copy-done.4
  15.6 0.7 copy-done.5
  16.3 0.0 copy-start.9
  16.3 0.0 copy-start.8
  16.3 4.0 %coarse.1 = (f32[8,128,128]{2,1,0:T(8,128)}, bf16[16,160,128]{2,1,0:T(8,128)(2,1)}) custom-call(bf16[448,256]{1,0:T(8,128)(2,1)} %copy-done.4, bf16[448,256]{1,0:T(8,128)(2,1)} %copy-done.5, bf16[4,128,256]{2,1,0:T(8,128)(2,1)} %bitcast.20, bf16[2,64,256]{2,1,0:T(8,128)(2,1)} %bitcast.22, bf16[4,3,3,256,128]{4,3,2,1,0:T(8,128)(2,1)} %w.5, ...), custom_call_target="tpu_custom_call" | custom-call | tf_op jit(solution)/shard_map/coarse/pallas_call | solution.py:468
  20.3 9.2 %all-to-all-start = ((bf16[16,160,128]{2,1,0:T(8,128)(2,1)}), bf16[16,160,128]{2,1,0:T(8,128)(2,1)S(1)}, u32[]{:S(2)}, u32[]{:S(2)}) async-start(bf16[16,160,128]{2,1,0:T(8,128)(2,1)} %get-tuple-element.22), calls=%async_computation | async-start | bytes 1310720 | tf_op jit(solution)/shard_map/all_to_all | solution.py:36
  29.6 0.0 copy-done.9
  29.6 3.3 %collective-permute-start.2 = (bf16[1024,256]{1,0:T(8,128)(2,1)S(1)}, bf16[1024,256]{1,0:T(8,128)(2,1)S(1)}, u32[]{:S(2)}, u32[]{:S(2)}) collective-permute-start(bf16[1024,256]{1,0:T(8,128)(2,1)S(1)} %copy-done.9), channel_id=1, source_target_pairs={{0,1},{1,2},{2,3},{3,4},{4,5},{5,6},{6,7},{7,8},{8,9},{9,10},{10,1... | collective-permute-start | bytes 1572872 | tf_op jit(solution)/shard_map/ppermute | solution.py:428
  32.9 0.0 copy-done.8
  32.9 1.3 %collective-permute-start.3 = (bf16[1024,256]{1,0:T(8,128)(2,1)S(1)}, bf16[1024,256]{1,0:T(8,128)(2,1)S(1)}, u32[]{:S(2)}, u32[]{:S(2)}) collective-permute-start(bf16[1024,256]{1,0:T(8,128)(2,1)S(1)} %copy-done.8), channel_id=1, source_target_pairs={{1,0},{2,1},{3,2},{4,3},{5,4},{6,5},{7,6},{8,7},{9,8},{10,9},{11,1... | collective-permute-start | bytes 1572872 | tf_op jit(solution)/shard_map/ppermute | solution.py:429
  34.2 12.0 %collective-permute-done.2.before = bf16[1024,256]{1,0:T(8,128)(2,1)S(1)} collective-permute-done((bf16[1024,256]{1,0:T(8,128)(2,1)S(1)}, bf16[1024,256]{1,0:T(8,128)(2,1)S(1)}, u32[]{:S(2)}, u32[]{:S(2)}) %collective-permute-start.2) | collective-permute-done | bytes 524320 | tf_op jit(solution)/shard_map/ppermute | solution.py:428
  46.2 0.0 copy-start.1
  46.2 2.6 %collective-permute-done.3.after = bf16[1024,256]{1,0:T(8,128)(2,1)S(1)} collective-permute-done((bf16[1024,256]{1,0:T(8,128)(2,1)S(1)}, bf16[1024,256]{1,0:T(8,128)(2,1)S(1)}, u32[]{:S(2)}, u32[]{:S(2)}) %collective-permute-start.3) | collective-permute-done | bytes 524320 | tf_op jit(solution)/shard_map/ppermute | solution.py:429
  48.7 0.0 copy-start.2
  48.8 0.0 copy-done.1
  48.8 0.8 copy-done.2
  49.5 6.3 %eighth.1 = (f32[10,256,128]{2,1,0:T(8,128)}, f32[5,8,256]{2,1,0:T(8,128)}) custom-call(bf16[8,256,256]{2,1,0:T(8,128)(2,1)} %bitcast.17, bf16[8,256,256]{2,1,0:T(8,128)(2,1)} %bitcast.18, bf16[1024,256]{1,0:T(8,128)(2,1)} %copy-done.1, bf16[1024,256]{1,0:T(8,128)(2,1)} %copy-done.2, bf16[4,3,3,256,128]{4,3,2,1,0:T(8,128)(2,1)} %w.5, ...), custom_call_target="tpu_custom_call" | custom-call | tf_op jit(solution)/shard_map/eighth/pallas_call | solution.py:497
  55.8 8.5 %quarter_late.1 = (f32[16,512,128]{2,1,0:T(8,128)}, f32[5,8,256]{2,1,0:T(8,128)}) custom-call(bf16[16,512,256]{2,1,0:T(8,128)(2,1)} %bitcast.13, bf16[16,512,256]{2,1,0:T(8,128)(2,1)} %bitcast.14, bf16[16,512,256]{2,1,0:T(8,128)(2,1)} %bitcast.15, bf16[1024,256]{1,0:T(8,128)(2,1)} %copy-done.1, ...), custom_call_target="tpu_custom_call", output_to_operand_aliasing={{0}: (6, {})} | custom-call | tf_op jit(solution)/shard_map/quarter_late/pallas_call | solution.py:479
  64.3 0.0 copy-start.7
  64.3 0.0 all-to-all-done.got
  64.3 0.0 copy-start
  64.3 0.9 copy-done
  65.2 11.5 %between.1 = (f32[10,256,128]{2,1,0:T(8,128)}, f32[10,256,128]{2,1,0:T(8,128)}, f32[16,16,128]{2,1,0:T(8,128)}) custom-call(s32[1]{0:T(128)} %bitcast.place, bf16[16,160,128]{2,1,0:T(8,128)(2,1)} %copy-done, f32[8,128,128]{2,1,0:T(8,128)} %get-tuple-element.23.__._.y2, bf16[3,3,3,128,128]{4,3,2,1,0:T(8,128)(2,1)} %weights.1, f32[7,128]{1,0:T(8,128)} %gain.3, ...), custom_call_target="tpu_custom_call" | custom-call | tf_op jit(solution)/shard_map/between/pallas_call | solution.py:515
  76.7 6.5 %all-to-all-start.1 = ((f32[16,16,128]{2,1,0:T(8,128)}), f32[16,16,128]{2,1,0:T(8,128)S(1)}, u32[]{:S(2)}, u32[]{:S(2)}) async-start(f32[16,16,128]{2,1,0:T(8,128)} %get-tuple-element.29), calls=%async_computation.1 | async-start | bytes 262144 | tf_op jit(solution)/shard_map/all_to_all | solution.py:36
  83.1 0.0 copy-done.7
  83.2 0.0 copy-start.6
  83.2 0.6 pad_maximum_fusion.class_t3
  83.8 6.2 %all-to-all-done.1.got = f32[16,16,128]{2,1,0:T(8,128)S(1)} async-done(((f32[16,16,128]{2,1,0:T(8,128)}), f32[16,16,128]{2,1,0:T(8,128)S(1)}, u32[]{:S(2)}, u32[]{:S(2)}) %all-to-all-start.1) | async-done | bytes 131104 | tf_op jit(solution)/shard_map/all_to_all | solution.py:36
  90.0 0.0 copy-start.3
  90.0 0.0 copy-done.6
  90.0 0.6 copy-done.3
  90.6 9.7 %final.1 = (bf16[19,16,512]{2,1,0:T(8,128)(2,1)}, f32[128,2,128]{2,1,0:T(2,128)}) custom-call(s32[1]{0:T(128)} %bitcast.place, f32[19]{0:T(128)} %bias.1, f32[16,16,128]{2,1,0:T(8,128)} %copy-done.3, f32[7,128]{1,0:T(8,128)} %gain.3, f32[7,128]{1,0:T(8,128)} %shift.3, f32[16,512,128]{2,1,0:T(8,128)} %get-tuple-element.30.y0, ...), custom_call_target="tpu_custom_call" | custom-call | tf_op jit(solution)/shard_map/final/pallas_call | solution.py:545
  100.3 19.6 %all_to_all.15 = f32[128,2,128]{2,1,0:T(2,128)S(1)} all-to-all(f32[128,2,128]{2,1,0:T(2,128)} %get-tuple-element.35), channel_id=1, replica_groups=mesh['batch_0'=4,'batch_1'=2,'rows_0'=4,'rows_1'=4] {'batch_0','batch_1'..., dimensions={0} | all-to-all | bytes 262144 | tf_op jit(solution)/shard_map/all_to_all | solution.py:36
  119.9 0.3 reduce_sum.9
  120.2 0.6 fusion
  (1 shorter events, 0.0 us)
Async XLA Ops:
  3.3 11.3 %collective-permute-start = (bf16[448,256]{1,0:T(8,128)(2,1)}, bf16[448,256]{1,0:T(8,128)(2,1)S(1)}, u32[]{:S(2)}, u32[]{:S(2)}) collective-permute-start(bf16[448,256]{1,0:T(8,128)(2,1)} %get-tuple-element.19), channel_id=1, source_target_pairs={{0,1},{1,2},{2,3},{3,4},{4,5},{5,6},{6,7},{7,8},{8,9},{9,10},{10,1... | collective-permute-start | bytes 688136 | tf_op jit(solution)/shard_map/ppermute | solution.py:426
  7.3 8.3 %collective-permute-start.1 = (bf16[448,256]{1,0:T(8,128)(2,1)}, bf16[448,256]{1,0:T(8,128)(2,1)S(1)}, u32[]{:S(2)}, u32[]{:S(2)}) collective-permute-start(bf16[448,256]{1,0:T(8,128)(2,1)} %get-tuple-element.20), channel_id=1, source_target_pairs={{1,0},{2,1},{3,2},{4,3},{5,4},{6,5},{7,6},{8,7},{9,8},{10,9},{11,1... | collective-permute-start | bytes 688136 | tf_op jit(solution)/shard_map/ppermute | solution.py:427
  14.6 1.1 copy-start.4
  15.6 0.7 copy-start.5
  16.3 13.3 %copy-start.9 = (bf16[1024,256]{1,0:T(8,128)(2,1)S(1)}, bf16[1024,256]{1,0:T(8,128)(2,1)}, u32[]{:S(2)}) copy-start(bf16[1024,256]{1,0:T(8,128)(2,1)} %get-tuple-element.24) | copy-start | bytes 1572868
  16.3 16.6 %copy-start.8 = (bf16[1024,256]{1,0:T(8,128)(2,1)S(1)}, bf16[1024,256]{1,0:T(8,128)(2,1)}, u32[]{:S(2)}) copy-start(bf16[1024,256]{1,0:T(8,128)(2,1)} %get-tuple-element.25) | copy-start | bytes 1572868
  20.3 43.9 %all-to-all-start = ((bf16[16,160,128]{2,1,0:T(8,128)(2,1)}), bf16[16,160,128]{2,1,0:T(8,128)(2,1)S(1)}, u32[]{:S(2)}, u32[]{:S(2)}) async-start(bf16[16,160,128]{2,1,0:T(8,128)(2,1)} %get-tuple-element.22), calls=%async_computation | async-start | bytes 1310720 | tf_op jit(solution)/shard_map/all_to_all | solution.py:36
  29.6 16.6 %collective-permute-start.2 = (bf16[1024,256]{1,0:T(8,128)(2,1)S(1)}, bf16[1024,256]{1,0:T(8,128)(2,1)S(1)}, u32[]{:S(2)}, u32[]{:S(2)}) collective-permute-start(bf16[1024,256]{1,0:T(8,128)(2,1)S(1)} %copy-done.9), channel_id=1, source_target_pairs={{0,1},{1,2},{2,3},{3,4},{4,5},{5,6},{6,7},{7,8},{8,9},{9,10},{10,1... | collective-permute-start | bytes 1572872 | tf_op jit(solution)/shard_map/ppermute | solution.py:428
  32.9 15.8 %collective-permute-start.3 = (bf16[1024,256]{1,0:T(8,128)(2,1)S(1)}, bf16[1024,256]{1,0:T(8,128)(2,1)S(1)}, u32[]{:S(2)}, u32[]{:S(2)}) collective-permute-start(bf16[1024,256]{1,0:T(8,128)(2,1)S(1)} %copy-done.8), channel_id=1, source_target_pairs={{1,0},{2,1},{3,2},{4,3},{5,4},{6,5},{7,6},{8,7},{9,8},{10,9},{11,1... | collective-permute-start | bytes 1572872 | tf_op jit(solution)/shard_map/ppermute | solution.py:429
  46.2 2.6 %copy-start.1 = (bf16[1024,256]{1,0:T(8,128)(2,1)}, bf16[1024,256]{1,0:T(8,128)(2,1)S(1)}, u32[]{:S(2)}) copy-start(bf16[1024,256]{1,0:T(8,128)(2,1)S(1)} %collective-permute-done.2.before) | copy-start | bytes 1572868
  48.7 0.8 copy-start.2
  64.3 18.9 %copy-start.7 = (bf16[128,19]{0,1:T(8,128)(2,1)S(1)}, bf16[128,19]{0,1:T(8,128)(2,1)}, u32[]{:S(2)}) copy-start(bf16[128,19]{0,1:T(8,128)(2,1)} %param.23) | copy-start | bytes 14596
  64.3 0.9 copy-start
  76.7 13.3 %all-to-all-start.1 = ((f32[16,16,128]{2,1,0:T(8,128)}), f32[16,16,128]{2,1,0:T(8,128)S(1)}, u32[]{:S(2)}, u32[]{:S(2)}) async-start(f32[16,16,128]{2,1,0:T(8,128)} %get-tuple-element.29), calls=%async_computation.1 | async-start | bytes 262144 | tf_op jit(solution)/shard_map/all_to_all | solution.py:36
  83.2 6.8 %copy-start.6 = (bf16[32,128]{1,0:T(8,128)(2,1)}, bf16[32,128]{1,0:T(8,128)(2,1)S(1)}, u32[]{:S(2)}) copy-start(bf16[32,128]{1,0:T(8,128)(2,1)S(1)} %pad.4.class_t) | copy-start | bytes 24580
  90.0 0.6 copy-start.3

commit v2 on v1

v2 whole, which is shorter than its diff:
```python
import jax
import jax.numpy as jnp
import numpy as np
from jax import lax
from jax.experimental import pallas as pl
from jax.experimental.pallas import tpu as pltpu
from jax.sharding import Mesh
from jax.sharding import PartitionSpec as P

GROUP = 4
HEAD = 128
ROWS = ("rows_0", "rows_1")
EVERY = ("batch_0", "batch_1", "rows_0", "rows_1")
BATCH = ("batch_0", "batch_1")
NORM_FLOOR = 0.05
SMALL = (3, 1)
BIG = (1, 2)
STAT_ROWS = 32
SLOT = 32
F32, BF16 = jnp.float32, jnp.bfloat16
VMEM_LIMIT = 60 * 1024 * 1024


def doubling(cols):
    matrix = np.zeros((2 * cols, cols), np.float32)
    for k in range(cols):
        matrix[2 * k, k] += 0.75
        matrix[2 * k, max(k - 1, 0)] += 0.25
        matrix[2 * k + 1, k] += 0.75
        matrix[2 * k + 1, min(k + 1, cols - 1)] += 0.25
    return matrix


def everyone(pieces, axes):
    return lax.all_to_all(pieces, axes, 0, 0)


def matmul(a, b):
    return jnp.dot(a, b, preferred_element_type=F32)


def matmul_t(a, b):
    return lax.dot_general(a, b, (((1,), (1,)), ((), ())), preferred_element_type=F32)


def fill_pair(w_ref, out_ref, depth):
    zero = jnp.zeros((depth, HEAD), BF16)
    for j in range(4):
        for across in range(3):
            rows = slice(j * depth, (j + 1) * depth)
            at = across * 2 * HEAD
            out_ref[rows, at : at + HEAD] = w_ref[j, across] if j < 3 else zero
            out_ref[rows, at + HEAD : at + 2 * HEAD] = w_ref[j - 1, across] if j else zero


def across_taps(z, width, cols):
    pixels = z.shape[0]
    index = lax.broadcasted_iota(jnp.int32, (pixels, width), 0) % cols
    left = jnp.where(index == 0, 0.0, pltpu.roll(z[:, :width], 1, 0))
    right = jnp.where(index == cols - 1, 0.0, pltpu.roll(z[:, 2 * width :], pixels - 1, 0))
    return z[:, width : 2 * width] + left + right


def conv_pair(rows, w_ref):
    return across_taps(matmul(jnp.concatenate(rows, axis=1), w_ref[...]), 2 * HEAD, rows[0].shape[0])


def fill_deep(w_ref, out_ref, depth):
    zero = jnp.zeros((depth, HEAD), BF16)
    for j in range(4):
        rows = slice(j * depth, (j + 1) * depth)
        if j < 3:
            out_ref[rows, :HEAD] = w_ref[j, 0]
            out_ref[rows, HEAD : 2 * HEAD] = w_ref[j, 1]
        out_ref[rows, 2 * HEAD : 3 * HEAD] = w_ref[j, 2] if j < 3 else zero
        out_ref[rows, 3 * HEAD :] = w_ref[j - 1, 2] if j else zero


def conv_deep(rows, w_ref):
    cols, depth = rows[0].shape
    wide = jnp.concatenate(rows, axis=1)
    stacked = jnp.concatenate([wide[:, : 3 * depth], wide[:, depth:]], axis=0)
    near = matmul(stacked, w_ref[: 3 * depth, : 2 * HEAD])
    far = matmul(wide, w_ref[:, 2 * HEAD :])
    taps = [jnp.concatenate([near[:cols, at : at + HEAD], near[cols:, at : at + HEAD]], axis=1) for at in (0, HEAD)]
    index = lax.broadcasted_iota(jnp.int32, far.shape, 0)
    left = jnp.where(index == 0, 0.0, pltpu.roll(taps[0], 1, 0))
    right = jnp.where(index == cols - 1, 0.0, pltpu.roll(far, cols - 1, 0))
    return taps[1] + left + right


def centre(y):
    total = jnp.sum(y, axis=0, keepdims=True)
    centred = y - total * (1.0 / y.shape[0])
    return total, jnp.sum(centred * centred, axis=0, keepdims=True), centred


def sums(y):
    return centre(y)[:2]


def merge(parts, pixels):
    total = sum(p[0] for p in parts)
    mean = total * (1.0 / (pixels * len(parts)))
    square = sum(p[1] + pixels * jnp.square(p[0] * (1.0 / pixels) - mean) for p in parts)
    return total, square


def halves(pair):
    total, square = pair
    return [(total[:, :HEAD], square[:, :HEAD]), (total[:, HEAD:], square[:, HEAD:])]


def group_sum(v):
    lane = lax.broadcasted_iota(jnp.int32, v.shape, 1)
    v = v + jnp.where(lane % 2 == 0, pltpu.roll(v, HEAD - 1, 1), pltpu.roll(v, 1, 1))
    return v + jnp.where(lane % 4 < 2, pltpu.roll(v, HEAD - 2, 1), pltpu.roll(v, 2, 1))


def normed(y, mean, factor, shift):
    return jnp.maximum((y - mean) * factor + shift, 0.0).astype(BF16)


def offset(total, pixels, norm):
    mean, factor, shift = norm
    return (total * (1.0 / pixels) - mean) * factor + shift


def lifted(centred, factor, at):
    return jnp.maximum(centred.astype(F32) * factor + at, 0.0).astype(BF16)


def split_rows(values):
    high = values.astype(BF16).astype(F32)
    rest = values - high
    middle = rest.astype(BF16).astype(F32)
    return [high, middle, rest - middle]


def edges_kernel(quarter, eighth, sixteenth, thirty, small_before, small_after, big_before, big_after, sems):
    copies = []
    groups = (
        (SMALL, (sixteenth, thirty), small_before, small_after),
        (BIG, (quarter, eighth), big_before, big_after),
    )
    for depths, feats, before, after in groups:
        at = 0
        for depth, feat in zip(depths, feats):
            rows, cols, _ = feat.shape
            for i in range(depth):
                spot = pl.ds(at, cols)
                copies.append((feat.at[rows - depth + i], before.at[spot]))
                copies.append((feat.at[i], after.at[spot]))
                at += cols
    started = [pltpu.make_async_copy(a, b, sems.at[i]) for i, (a, b) in enumerate(copies)]
    for copy in started:
        copy.start()
    for copy in started:
        copy.wait()


class Copies:
    def __init__(self, sems):
        self.sems, self.used = sems, 0

    def start(self, source, target):
        copy = pltpu.make_async_copy(source, target, self.sems.at[self.used])
        self.used += 1
        copy.start()
        return copy


def keep_pair(y, field, stats, index, pair):
    total, square, centred = centre(y)
    field[2 * pair] = centred[:, :HEAD].astype(BF16)
    field[2 * pair + 1] = centred[:, HEAD:].astype(BF16)
    stats[index, 0:1] = total
    stats[index, 1:2] = square


def inner_kernel(
    quarter, eighth, weights, _, c0_out, c1_out, stats0, stats1, x0, x1, w0, w1, deep0, deep1, c0, c1, sems
):
    copies = Copies(sems)
    inside = stats0.shape[0]
    wait_w0 = copies.start(weights.at[0], w0)
    rows_of = lambda r, n: copies.start(quarter.at[pl.ds(r, n)], x0.at[pl.ds(r, n)])
    waits = [rows_of(1, 4), rows_of(5, 2)]
    wait_w0.wait()
    fill_deep(w0, deep0, 2 * HEAD)
    out = []
    for i in range(inside):
        p = i + 1
        waits[i].wait()
        if i + 2 < inside:
            waits.append(rows_of(2 * p + 5, 2))
        elif i + 2 == inside:
            wait_w1 = copies.start(weights.at[1], w1)
            wait_x1 = copies.start(eighth, x1)
        rows = [x0[2 * p - 1 + j] for j in range(4)]
        keep_pair(conv_deep(rows, deep0), c0, stats0, i, p)
        out.append(copies.start(c0.at[pl.ds(2 * p, 2)], c0_out.at[pl.ds(2 * p, 2)]))
    wait_w1.wait()
    fill_deep(w1, deep1, 2 * HEAD)
    wait_x1.wait()
    for i in range(stats1.shape[0]):
        p = i + 1
        rows = [x1[2 * i + j] for j in range(4)]
        keep_pair(conv_deep(rows, deep1), c1, stats1, i, p)
        out.append(copies.start(c1.at[pl.ds(2 * p, 2)], c1_out.at[pl.ds(2 * p, 2)]))
    for copy in out:
        copy.wait()


def outer_kernel(
    quarter, eighth, before, after, weights, _, __, c0_out, c1_out, stats0, stats1,
    x0, x1, low, high, w0, w1, deep0, deep1, c0, c1, sems,
):
    copies = Copies(sems)
    q_rows, cols, _ = quarter.shape
    e_rows, e_cols, _ = eighth.shape
    wait_w0 = copies.start(weights.at[0], w0)
    waits = [
        copies.start(before, low),
        copies.start(quarter.at[pl.ds(0, 3)], x0.at[pl.ds(0, 3)]),
        copies.start(after, high),
        copies.start(quarter.at[pl.ds(q_rows - 3, 3)], x0.at[pl.ds(3, 3)]),
    ]
    wait_w1 = copies.start(weights.at[1], w1)
    waits1 = [
        copies.start(eighth.at[pl.ds(0, 2)], x1.at[pl.ds(0, 2)]),
        copies.start(eighth.at[pl.ds(e_rows - 2, 2)], x1.at[pl.ds(2, 2)]),
    ]
    wait_w0.wait()
    fill_deep(w0, deep0, 2 * HEAD)
    out = []
    for i in range(2):
        waits[2 * i].wait()
        waits[2 * i + 1].wait()
        rows = [x0[3 * i + j] for j in range(3)]
        rows = rows + [high[:cols]] if i else [low[:cols]] + rows
        keep_pair(conv_deep(rows, deep0), c0, stats0, i, i)
        spot = pl.ds(i * (q_rows - 2), 2)
        out.append(copies.start(c0.at[pl.ds(2 * i, 2)], c0_out.at[spot]))
    wait_w1.wait()
    fill_deep(w1, deep1, 2 * HEAD)
    for i in range(2):
        waits1[i].wait()
        halo = (high if i else low)
        rows = [x1[2 * i + j] for j in range(2)]
        extra = [halo[cols + j * e_cols : cols + (j + 1) * e_cols] for j in range(2)]
        rows = rows + extra if i else extra + rows
        keep_pair(conv_deep(rows, deep1), c1, stats1, i, i)
        spot = pl.ds(i * e_rows, 2)
        out.append(copies.start(c1.at[pl.ds(2 * i, 2)], c1_out.at[spot]))
    for copy in out:
        copy.wait()


def coarse_kernel(before, after, sixteenth, thirty, w2, w3, y2, pieces, wide2, wide3):
    depth = 2 * HEAD
    fill_deep(w2, wide2, depth)
    fill_deep(w3, wide3, depth)
    own, cols, _ = sixteenth.shape
    ring = SMALL[0]
    rows = [before[i * cols : (i + 1) * cols] for i in range(ring)]
    rows += [sixteenth[i] for i in range(own)]
    rows += [after[i * cols : (i + 1) * cols] for i in range(ring)]
    parts = []
    for p in range(y2.shape[0] // 2):
        out = conv_deep(rows[2 * p : 2 * p + 4], wide2)
        y2[2 * p] = out[:, :HEAD]
        y2[2 * p + 1] = out[:, HEAD:]
        if 0 < p < y2.shape[0] // 2 - 1:
            parts += halves(sums(out))
    at = ring * cols
    out = conv_deep([before[at:], thirty[0], thirty[1], after[at:]], wide3)
    total3, square3, coarse = centre(jnp.concatenate([out[:, :HEAD], out[:, HEAD:]], axis=0))
    coarse = coarse.astype(BF16)
    total, square = merge(parts, cols)
    values = jnp.concatenate([total, square, total3, square3, jnp.zeros((4, HEAD), F32)], axis=0)
    head = jnp.concatenate(split_rows(values) + [jnp.zeros((8, HEAD), F32)], axis=0).astype(BF16)
    for i in range(pieces.shape[0]):
        pieces[i, :STAT_ROWS] = head
        pieces[i, STAT_ROWS:] = coarse


def between_kernel(
    place, got, y2_in, weights_in, gain, shift, up_small, up_big, inner0, outer0, inner1, outer1,
    c4_out, c6_out, stats4, stats6, pieces,
    y2, weights, c4, c6, fine, coarse, field5, stats5, wide0, wide1, wide2, sems,
):
    members = got.shape[0]
    position = place[0]
    first, last = position == 0, position == members - 1
    copies = Copies(sems)
    wait_w = copies.start(weights_in, weights)
    wait_y2 = copies.start(y2_in, y2)
    out = []

    def merged_norm(each, pixels, layer):
        count = pixels * len(each) * GROUP
        mean = group_sum(jnp.broadcast_to(sum(p[0] for p in each), (8, HEAD)))[0:1] * (1.0 / count)
        square = sum(p[1] + pixels * jnp.square(p[0] * (1.0 / pixels) - mean) for p in each)
        var = group_sum(jnp.broadcast_to(square, (8, HEAD)))[0:1] * (1.0 / count)
        return mean, gain[layer : layer + 1] * lax.rsqrt(var + NORM_FLOOR), shift[layer : layer + 1]

    def up_conv(acts, wide, kept, kept_out, stats):
        count = len(acts)
        doubled = []
        for k in range(0, count, 2):
            both = matmul(up_big[...], jnp.concatenate([acts[k], acts[k + 1]], axis=1))
            doubled += [both[:, :HEAD], both[:, HEAD:]]
        lines = 2 * (count - 2)
        for k in range(1, count - 1):
            for half, other in ((0, k - 1), (1, k + 1)):
                line = 0.75 * doubled[k] + 0.25 * doubled[other]
                at = 2 * (k - 1) + half
                if at < 2:
                    line = jnp.where(first, 0.0, line)
                if at >= lines - 2:
                    line = jnp.where(last, 0.0, line)
                fine[at] = line.astype(BF16)
        own = []
        for p in range(lines // 2 - 1):
            keep_pair(conv_pair([fine[2 * p + j] for j in range(4)], wide), kept, stats, p, p)
            span = pl.ds(2 * p, 2)
            out.append(copies.start(kept.at[span], kept_out.at[span]))
            two = halves((stats[p, 0:1], stats[p, 1:2]))
            own += two[1:] if p == 0 else two[:1] if p == lines // 2 - 2 else two
        return merge(own, kept.shape[1])

    lines, cols = coarse.shape[0] - 2, coarse.shape[1]
    small = cols // 2
    blocks = [got[i, :STAT_ROWS].astype(F32) for i in range(members)]
    blocks = [b[0:8] + b[8:16] + b[16:24] for b in blocks]
    norm3 = merged_norm([(b[2:3], b[3:4]) for b in blocks], 2 * small, 3)
    doubled = []
    for i in range(members):
        a = lifted(got[i, STAT_ROWS:], norm3[1], offset(blocks[i][2:3], 2 * small, norm3))
        both = matmul(up_small[...], jnp.concatenate([a[:small], a[small:]], axis=1))
        doubled += [both[:, :HEAD], both[:, HEAD:]]
    coarse[0] = jnp.zeros((cols, HEAD), BF16)
    coarse[lines + 1] = jnp.zeros((cols, HEAD), BF16)
    for k in range(len(doubled)):
        for half, other in ((0, max(k - 1, 0)), (1, min(k + 1, len(doubled) - 1))):
            coarse[1 + 2 * k + half] = (0.75 * doubled[k] + 0.25 * doubled[other]).astype(BF16)
    wait_w.wait()
    for i, wide in enumerate((wide0, wide1, wide2)):
        fill_pair(weights.at[i], wide, HEAD)
    fold = 4

    def step(q, carry):
        base = q * (2 * fold)
        lhs = jnp.concatenate(
            [
                jnp.concatenate([coarse[base + 2 * i + j] for j in range(4)], axis=1)
                for i in range(fold)
            ],
            axis=0,
        )
        y = across_taps(matmul(lhs, wide1[...]), 2 * HEAD, cols)
        for i in range(fold):
            field5[base + 2 * i] = y[i * cols : (i + 1) * cols, :HEAD]
            field5[base + 2 * i + 1] = y[i * cols : (i + 1) * cols, HEAD:]
        total, square = sums(y)
        stats5[q, 0:1] = total
        stats5[q, 1:2] = square
        return carry

    lax.fori_loop(0, lines // (2 * fold), step, 0, unroll=2)
    wait_y2.wait()
    norm2 = merged_norm([(b[0:1], b[1:2]) for b in blocks], y2.shape[1] * (y2.shape[0] - 4), 2)
    acts = [normed(y2[i], *norm2) for i in range(y2.shape[0])]
    count = len(acts)
    acts[1] = jnp.where(first, acts[2], acts[1])
    acts[count - 2] = jnp.where(last, acts[count - 3], acts[count - 2])
    merged4 = up_conv(acts, wide0, c4, c4_out, stats4)
    parts5 = []
    for q in range(lines // (2 * fold)):
        parts5 += halves((stats5[q, 0:1], stats5[q, 1:2]))
    norm5 = merged_norm(parts5, cols * fold, 5)
    band = lines // members
    acts = []
    for i in range(band + 4):
        at = jnp.clip(position * band + (i - 2), 0, lines - 1)
        acts.append(normed(field5[at], *norm5))
    merged6 = up_conv(acts, wide2, c6, c6_out, stats6)
    parts0, parts1 = [], []
    for stats in (inner0, outer0):
        for p in range(stats.shape[0]):
            parts0 += halves((stats[p, 0:1], stats[p, 1:2]))
    for p in range(inner1.shape[0]):
        parts1 += halves((inner1[p, 0:1], inner1[p, 1:2]))
    for p in range(2):
        parts1.append(halves((outer1[p, 0:1], outer1[p, 1:2]))[1 - p])
    eighth_cols = c4.shape[1]
    merged = [merge(parts0, 2 * eighth_cols), merge(parts1, eighth_cols), merged4, merged6]
    pad = [jnp.zeros((4, HEAD), F32)]
    block = jnp.concatenate([m[0] for m in merged] + pad + [m[1] for m in merged] + pad, axis=0)
    for i in range(members):
        pieces[i] = block
    for copy in out:
        copy.wait()


def final_kernel(
    place, bias, got, gain, shift, inner0, outer0, inner1, outer1, stats4, stats6, labels, class_t, class_t3, up_cols,
    c0_in, c1_in, c4_in, c6_in, logits, pieces, c0, c1, c4, c6, lines, doubled, scores, sems,
):
    members = got.shape[0]
    copies = Copies(sems)
    waits = [copies.start(a, b) for a, b in ((c1_in, c1), (c4_in, c4), (c6_in, c6))]
    rows = c0.shape[0]
    chunk = rows // 4
    waits0 = [
        copies.start(c0_in.at[pl.ds(i * chunk, chunk)], c0.at[pl.ds(i * chunk, chunk)]) for i in range(4)
    ]
    count = c4.shape[0]
    first, last = place[0] == 0, place[0] == members - 1
    row = lax.broadcasted_iota(jnp.int32, (8, HEAD), 0)
    own = float((count - 2) * c4.shape[1])
    pixels = jnp.where(row == 0, 4.0 * own, own)
    total = sum(got[i, 0:8] for i in range(members))
    mean = group_sum(total) / (pixels * (members * GROUP))
    square = sum(got[i, 8:16] + pixels * jnp.square(got[i, 0:8] / pixels - mean) for i in range(members))
    scale = lax.rsqrt(group_sum(square) / (pixels * (members * GROUP)) + NORM_FLOOR)
    norms = [
        (mean[j : j + 1], gain[layer : layer + 1] * scale[j : j + 1], shift[layer : layer + 1])
        for j, layer in enumerate((0, 1, 4, 6))
    ]

    def lift(field, r, total, norm):
        half = total[:, (r % 2) * HEAD : (r % 2 + 1) * HEAD]
        return lifted(field[r], norm[1], offset(half, field.shape[1], norm))

    def joined(inner, outer):
        pairs = [inner[p, 0:1] for p in range(inner.shape[0])]
        return [outer[0, 0:1]] + pairs + [outer[1, 0:1]]

    totals0, totals1 = joined(inner0, outer0), joined(inner1, outer1)
    for wait in waits:
        wait.wait()
    for i in range(count):
        p = i // 2
        acts = [
            lift(c1, i, totals1[p], norms[1]),
            lift(c4, i, stats4[p, 0:1], norms[2]),
            lift(c6, i, stats6[p, 0:1], norms[3]),
        ]
        lines[i] = matmul_t(class_t3[...], jnp.concatenate(acts, axis=1))
    lines[0] = jnp.where(first, lines[1], lines[0])
    lines[count - 1] = jnp.where(last, lines[count - 2], lines[count - 1])
    for i in range(count):
        value = lines[i]
        high = value.astype(BF16)
        low = (value - high.astype(F32)).astype(BF16)
        both = matmul(jnp.concatenate([high, low], axis=0), up_cols[...])
        doubled[i] = both[:SLOT] + both[SLOT:]
    for r in range(rows):
        if r % chunk == 0:
            waits0[r // chunk].wait()
        p = r // 2
        value = matmul_t(class_t[...], lift(c0, r, totals0[p], norms[0]))
        value = value + (0.75 * doubled[p + 1] + 0.25 * doubled[p + 2 * (r % 2)])
        for i in range(scores.shape[0]):
            scores[i, r * SLOT : (r + 1) * SLOT] = value[:, i * HEAD : (i + 1) * HEAD]
    label_map = labels[...]
    exps = jnp.zeros(label_map.shape, F32)
    picked = jnp.zeros(label_map.shape, F32)
    for c in range(logits.shape[0]):
        tiles = [scores.at[i][pl.ds(c, rows, stride=SLOT), :] for i in range(scores.shape[0])]
        score = jnp.concatenate(tiles, axis=1) + bias[c]
        logits[c] = score.astype(BF16)
        exps = exps + jnp.exp(score)
        picked = picked + jnp.where(label_map == c, score, 0.0)
    usable = label_map != 255
    terms = jnp.where(usable, jnp.log(exps) - picked, 0.0)
    counts = jnp.where(usable, 1.0, 0.0)
    out = []
    for v in (terms, counts):
        v = jnp.sum(v, axis=0, keepdims=True)
        out.append(sum(v[:, i * HEAD : (i + 1) * HEAD] for i in range(v.shape[1] // HEAD)))
    both = jnp.concatenate(out, axis=0)
    for i in range(pieces.shape[0]):
        pieces[i] = both


def params_of(**kw):
    return pltpu.CompilerParams(vmem_limit_bytes=VMEM_LIMIT, **kw)


def shaped(shape, dtype):
    return jax.ShapeDtypeStruct(shape, dtype)


VM = pl.BlockSpec(memory_space=pltpu.VMEM)
SM = pl.BlockSpec(memory_space=pltpu.SMEM)
ANY = pl.BlockSpec(memory_space=pl.ANY)


def device_step(
    feat_quarter,
    feat_eighth,
    feat_sixteenth,
    feat_thirty,
    labels,
    first_weights,
    inner_weights,
    norm_gain,
    norm_shift,
    class_weight,
    class_bias,
):
    position = lax.axis_index(ROWS)
    bands = lax.axis_size(ROWS)
    devices = bands * lax.axis_size(BATCH)
    place = position.astype(jnp.int32).reshape(1)
    up_pairs = [(i, i + 1) for i in range(bands - 1)]
    down_pairs = [(j, i) for i, j in up_pairs]
    feats = [feat_quarter[0], feat_eighth[0], feat_sixteenth[0], feat_thirty[0]]
    quarter, eighth, sixteenth, thirty = feats
    q_rows, q_cols, depth = quarter.shape
    e_rows, e_cols, _ = eighth.shape
    s_rows, s_cols, _ = sixteenth.shape
    t_rows, t_cols, _ = thirty.shape
    small = shaped((SMALL[0] * s_cols + SMALL[1] * t_cols, depth), BF16)
    big = shaped((BIG[0] * q_cols + BIG[1] * e_cols, depth), BF16)
    small_before, small_after, big_before, big_after = pl.pallas_call(
        edges_kernel,
        out_shape=[small, small, big, big],
        in_specs=[ANY] * 4,
        out_specs=[VM] * 4,
        scratch_shapes=[pltpu.SemaphoreType.DMA((2 * (sum(SMALL) + sum(BIG)),))],
        compiler_params=params_of(),
        name="edges",
    )(*feats)
    small_before = lax.ppermute(small_before, ROWS, up_pairs)
    small_after = lax.ppermute(small_after, ROWS, down_pairs)
    big_before = lax.ppermute(big_before, ROWS, up_pairs)
    big_after = lax.ppermute(big_after, ROWS, down_pairs)

    def fixed(a, *index):
        index = index or (0,) * len(a.shape)
        return pl.BlockSpec(a.shape, lambda i: index)

    def weight(level):
        return pl.BlockSpec((None,) + first_weights.shape[1:], lambda i: (level, 0, 0, 0, 0))

    deep = pltpu.VMEM((4 * depth, 4 * HEAD), BF16)
    raw = pltpu.VMEM(first_weights.shape[1:], BF16)
    pairs = q_rows // 2
    steps = e_rows // 2 + 1
    field0 = shaped((q_rows, q_cols, HEAD), BF16)
    field1 = shaped((e_rows + 2, e_cols, HEAD), BF16)
    stats_shape = lambda n: shaped((n, 8, 2 * HEAD), F32)
    room = lambda a: pltpu.VMEM(a.shape, a.dtype)
    piece = shaped((bands, STAT_ROWS + t_rows * t_cols, HEAD), BF16)
    y2_shape = shaped((s_rows + 4, s_cols, HEAD), F32)
    coarse_call = pl.pallas_call(
        coarse_kernel,
        grid=(1,),
        out_shape=[y2_shape, piece],
        in_specs=[fixed(small), fixed(small), fixed(sixteenth), fixed(thirty), weight(2), weight(3)],
        out_specs=[fixed(y2_shape), fixed(piece)],
        scratch_shapes=[deep, deep],
        compiler_params=params_of(),
        name="coarse",
    )
    y2, pieces = coarse_call(
        small_before, small_after, sixteenth, thirty, first_weights, first_weights
    )
    got = everyone(pieces, ROWS)
    inside0, inside1 = pairs - 2, steps - 2
    c0, c1, inner0, inner1 = pl.pallas_call(
        inner_kernel,
        out_shape=[field0, field1, stats_shape(inside0), stats_shape(inside1)],
        in_specs=[ANY] * 4,
        out_specs=[ANY, ANY, VM, VM],
        scratch_shapes=[
            room(quarter), room(eighth), raw, raw, deep, deep, room(field0), room(field1),
            pltpu.SemaphoreType.DMA((2 * inside0 + inside1 + 3,)),
        ],
        compiler_params=params_of(),
        name="inner",
    )(quarter, eighth, first_weights, y2)
    c0, c1, outer0, outer1 = pl.pallas_call(
        outer_kernel,
        out_shape=[field0, field1, stats_shape(2), stats_shape(2)],
        in_specs=[ANY] * 7,
        out_specs=[ANY, ANY, VM, VM],
        input_output_aliases={5: 0, 6: 1},
        scratch_shapes=[
            pltpu.VMEM((6, q_cols, depth), BF16), pltpu.VMEM((4, e_cols, depth), BF16), room(big), room(big),
            raw, raw, deep, deep,
            pltpu.VMEM((4, q_cols, HEAD), BF16), pltpu.VMEM((4, e_cols, HEAD), BF16),
            pltpu.SemaphoreType.DMA((12,)),
        ],
        compiler_params=params_of(),
        name="outer",
    )(quarter, eighth, big_before, big_after, first_weights, c0, c1)
    up_small = jnp.asarray(doubling(t_cols), BF16)
    up_big = jnp.asarray(doubling(s_cols), BF16)
    up_cols = jnp.asarray(doubling(e_cols).T, BF16)
    narrow = pltpu.VMEM((4 * HEAD, 6 * HEAD), BF16)
    c4, c6, stats4, stats6, pieces = pl.pallas_call(
        between_kernel,
        out_shape=[field1, field1, stats_shape(steps), stats_shape(steps), shaped((bands, 16, HEAD), F32)],
        in_specs=[SM, VM, ANY, ANY] + [VM] * 8,
        out_specs=[ANY, ANY, VM, VM, VM],
        scratch_shapes=[
            room(y2), room(inner_weights), room(field1), room(field1),
            pltpu.VMEM((e_rows + 4, e_cols, HEAD), BF16),
            pltpu.VMEM((2 * t_rows * bands + 2, 2 * t_cols, HEAD), BF16),
            pltpu.VMEM((2 * t_rows * bands, 2 * t_cols, HEAD), F32),
            pltpu.VMEM((t_rows * bands, 8, 2 * HEAD), F32),
            narrow, narrow, narrow,
            pltpu.SemaphoreType.DMA((2 * steps + 2,)),
        ],
        compiler_params=params_of(),
        name="between",
    )(
        place, got, y2, inner_weights, norm_gain, norm_shift, up_small, up_big,
        inner0, outer0, inner1, outer1,
    )
    got = everyone(pieces, ROWS)
    classes = class_weight.shape[1]
    class_t = jnp.pad(class_weight.T, ((0, SLOT - classes), (0, 0)))
    class_t3 = jnp.concatenate([class_t] * 3, axis=1)
    logits, pieces = pl.pallas_call(
        final_kernel,
        out_shape=[shaped((classes, q_rows, q_cols), BF16), shaped((devices, 2, HEAD), F32)],
        in_specs=[SM, SM] + [VM] * 13 + [ANY] * 4,
        out_specs=[VM, VM],
        scratch_shapes=[
            room(field0), room(field1), room(field1), room(field1),
            pltpu.VMEM((e_rows + 2, SLOT, e_cols), F32),
            pltpu.VMEM((e_rows + 2, SLOT, q_cols), F32),
            pltpu.VMEM((q_cols // HEAD, q_rows * SLOT, HEAD), F32),
            pltpu.SemaphoreType.DMA((7,)),
        ],
        compiler_params=params_of(),
        name="final",
    )(
        place, class_bias, got, norm_gain, norm_shift, inner0, outer0, inner1, outer1, stats4, stats6,
        labels[0], class_t, class_t3, up_cols, c0, c1, c4, c6,
    )
    loss_total, valid_count = jnp.sum(everyone(pieces, EVERY), axis=(0, 2))
    mean_loss = loss_total / jnp.maximum(valid_count, 1.0)
    return (logits[None], mean_loss)


def solution(mesh):
    split = Mesh(mesh.devices.reshape(4, 2, 4, 4), ("batch_0", "batch_1", "rows_0", "rows_1"))
    in_specs = (
        P(BATCH, ROWS, None, None),
        P(BATCH, ROWS, None, None),
        P(BATCH, ROWS, None, None),
        P(BATCH, ROWS, None, None),
        P(BATCH, ROWS, None),
        P(),
        P(),
        P(),
        P(),
        P(),
        P(),
    )
    out_specs = (P(BATCH, None, ROWS, None), P())
    return jax.shard_map(device_step, mesh=split, in_specs=in_specs, out_specs=out_specs, check_vma=False)
```

time: 124 us -> 113 us (0.911)
  Pallas kernels: 48.5 us -> 42.4 us
  waiting for transfers between devices: 21.8 us -> 16.6 us
    ppermute x1, waiting for transfers between devices: 12 us -> 0.83 us  [device_step(): big_before = lax.ppermute(big_before, ROWS, up_pairs)]
    pallas_call x6 -> x5, Pallas kernels: 45.8 us -> 39.7 us  [the longest x1 11.9 us: device_step(): pl.pallas_call(between_kernel, out_shape=[field1, field1, stats_shape(ste...]
    ppermute x1, waiting for transfers between devices: 0.01 us -> 3.12 us  [device_step(): small_before = lax.ppermute(small_before, ROWS, up_pairs)]
    ppermute x1, waiting for transfers between devices: 1.06 us -> 3.89 us  [device_step(): small_after = lax.ppermute(small_after, ROWS, down_pairs)]
  transfers between devices with their start and end apart: 6 -> 6, of which waited for: 4 -> 5; matrix products, arithmetic and copies ran while one was open for 0% -> 1% of each run, Pallas kernels for 17% -> 16%
where the time goes in v2:
time: 113 us; the launch traced here: 112 us
  Pallas kernels  42.4 us (38%)
  starting transfers between devices  25.7 us (23%)
  blocking collectives  19.7 us (17%)
  waiting for transfers between devices  16.6 us (15%)
  local copies, waits for them, and re-layouts  3.59 us (3%)
  between operations  3.22 us (3%)
    all_to_all x1, blocking collectives, everyone(): return lax.all_to_all(pieces, axes, 0, 0)  19.7 us
    all_to_all x2, starting transfers between devices, everyone(): return lax.all_to_all(pieces, axes, 0, 0)  15.7 us
    pallas_call x1, Pallas kernels, device_step(): pl.pallas_call(between_kernel, out_shape=[field1, field1, stats_shape(ste...  11.9 us
    pallas_call x1, Pallas kernels, device_step(): pl.pallas_call(inner_kernel, out_shape=[field0, field1, stats_shape(insid...  11.1 us
    pallas_call x1, Pallas kernels, device_step(): pl.pallas_call(outer_kernel, out_shape=[field0, field1, stats_shape(2), s...  6.55 us
    pallas_call x1, Pallas kernels, device_step(): pl.pallas_call(final_kernel, out_shape=[shaped((classes, q_rows, q_cols),...  6.46 us
    all_to_all x2, waiting for transfers between devices, everyone(): return lax.all_to_all(pieces, axes, 0, 0)  6.2 us
    ppermute x1, starting transfers between devices, device_step(): small_before = lax.ppermute(small_before, ROWS, up_pairs)  4.03 us
  transfers between devices with their start and end apart: 6, of which 5 were waited for; matrix products, arithmetic and copies ran while one was open for 1% of the time, Pallas kernels for 16%

profile of v2, /device:TPU:1, one launch (start us, length us, event | category | flops | bytes accessed | tf_op | source)
XLA Modules:
  0.0 112.0 jit_solution(18204236410114405327)
XLA Ops:
  0.6 2.7 %edges.1 = (bf16[448,256]{1,0:T(8,128)(2,1)}, bf16[448,256]{1,0:T(8,128)(2,1)}, bf16[1024,256]{1,0:T(8,128)(2,1)}, bf16[1024,256]{1,0:T(8,128)(2,1)}) custom-call(bf16[16,512,256]{2,1,0:T(8,128)(2,1)} %bitcast.9, bf16[8,256,256]{2,1,0:T(8,128)(2,1)} %bitcast.12, bf16[4,128,256]{2,1,0:T(8,128)(2,1)} %bitcast.15, bf16[2,64,256]{2,1,0:T(8,128)(2,1)} %bitcast.17), custom_call_target="tpu_custom_call" | custom-call | tf_op jit(solution)/shard_map/edges/pallas_call | solution.py:529
  3.3 4.0 %collective-permute-start = (bf16[448,256]{1,0:T(8,128)(2,1)}, bf16[448,256]{1,0:T(8,128)(2,1)S(1)}, u32[]{:S(2)}, u32[]{:S(2)}) collective-permute-start(bf16[448,256]{1,0:T(8,128)(2,1)} %get-tuple-element.23), channel_id=1, source_target_pairs={{0,1},{1,2},{2,3},{3,4},{4,5},{5,6},{6,7},{7,8},{8,9},{9,10},{10,1... | collective-permute-start | bytes 688136 | tf_op jit(solution)/shard_map/ppermute | solution.py:538
  7.4 0.0 copy-start.9
  7.4 0.0 copy-start.8
  7.4 1.4 %collective-permute-start.1 = (bf16[448,256]{1,0:T(8,128)(2,1)}, bf16[448,256]{1,0:T(8,128)(2,1)S(1)}, u32[]{:S(2)}, u32[]{:S(2)}) collective-permute-start(bf16[448,256]{1,0:T(8,128)(2,1)} %get-tuple-element.24), channel_id=1, source_target_pairs={{1,0},{2,1},{3,2},{4,3},{5,4},{6,5},{7,6},{8,7},{9,8},{10,9},{11,1... | collective-permute-start | bytes 688136 | tf_op jit(solution)/shard_map/ppermute | solution.py:539
  8.8 3.1 %collective-permute-done.before = bf16[448,256]{1,0:T(8,128)(2,1)S(1)} collective-permute-done((bf16[448,256]{1,0:T(8,128)(2,1)}, bf16[448,256]{1,0:T(8,128)(2,1)S(1)}, u32[]{:S(2)}, u32[]{:S(2)}) %collective-permute-start) | collective-permute-done | bytes 229408 | tf_op jit(solution)/shard_map/ppermute | solution.py:538
  11.9 0.0 copy-start.4
  11.9 3.9 %collective-permute-done.1.after = bf16[448,256]{1,0:T(8,128)(2,1)S(1)} collective-permute-done((bf16[448,256]{1,0:T(8,128)(2,1)}, bf16[448,256]{1,0:T(8,128)(2,1)S(1)}, u32[]{:S(2)}, u32[]{:S(2)}) %collective-permute-start.1) | collective-permute-done | bytes 229408 | tf_op jit(solution)/shard_map/ppermute | solution.py:539
  15.8 0.0 copy-done.4
  15.8 0.0 copy-start.5
  15.8 0.7 copy-done.5
  16.5 3.6 %coarse.1 = (f32[8,128,128]{2,1,0:T(8,128)}, bf16[16,160,128]{2,1,0:T(8,128)(2,1)}) custom-call(bf16[448,256]{1,0:T(8,128)(2,1)} %copy-done.4, bf16[448,256]{1,0:T(8,128)(2,1)} %copy-done.5, bf16[4,128,256]{2,1,0:T(8,128)(2,1)} %bitcast.16, bf16[2,64,256]{2,1,0:T(8,128)(2,1)} %bitcast.18, bf16[4,3,3,256,128]{4,3,2,1,0:T(8,128)(2,1)} %weights.3, ...), custom_call_target="tpu_custom_call" | custom-call | tf_op jit(solution)/shard_map/coarse/pallas_call | solution.py:570
  20.1 9.2 %all-to-all-start = ((bf16[16,160,128]{2,1,0:T(8,128)(2,1)}), bf16[16,160,128]{2,1,0:T(8,128)(2,1)S(1)}, u32[]{:S(2)}, u32[]{:S(2)}) async-start(bf16[16,160,128]{2,1,0:T(8,128)(2,1)} %get-tuple-element.25), calls=%async_computation | async-start | bytes 1310720 | tf_op jit(solution)/shard_map/all_to_all | solution.py:35
  29.4 0.0 copy-done.9
  29.4 3.3 %collective-permute-start.2 = (bf16[1024,256]{1,0:T(8,128)(2,1)S(1)}, bf16[1024,256]{1,0:T(8,128)(2,1)S(1)}, u32[]{:S(2)}, u32[]{:S(2)}) collective-permute-start(bf16[1024,256]{1,0:T(8,128)(2,1)S(1)} %copy-done.9), channel_id=1, source_target_pairs={{0,1},{1,2},{2,3},{3,4},{4,5},{5,6},{6,7},{7,8},{8,9},{9,10},{10,1... | collective-permute-start | bytes 1572872 | tf_op jit(solution)/shard_map/ppermute | solution.py:540
  32.7 0.0 copy-done.8
  32.7 1.3 %collective-permute-start.3 = (bf16[1024,256]{1,0:T(8,128)(2,1)S(1)}, bf16[1024,256]{1,0:T(8,128)(2,1)S(1)}, u32[]{:S(2)}, u32[]{:S(2)}) collective-permute-start(bf16[1024,256]{1,0:T(8,128)(2,1)S(1)} %copy-done.8), channel_id=1, source_target_pairs={{1,0},{2,1},{3,2},{4,3},{5,4},{6,5},{7,6},{8,7},{9,8},{10,9},{11,1... | collective-permute-start | bytes 1572872 | tf_op jit(solution)/shard_map/ppermute | solution.py:541
  34.0 11.1 %inner.1 = (bf16[16,512,128]{2,1,0:T(8,128)(2,1)}, bf16[10,256,128]{2,1,0:T(8,128)(2,1)}, f32[6,8,256]{2,1,0:T(8,128)}, f32[3,8,256]{2,1,0:T(8,128)}) custom-call(bf16[16,512,256]{2,1,0:T(8,128)(2,1)} %bitcast.10, bf16[8,256,256]{2,1,0:T(8,128)(2,1)} %bitcast.13, bf16[4,3,3,256,128]{4,3,2,1,0:T(8,128)(2,1)} %weights.3, f32[8,128,128]{2,1,0:T(8,128)} %get-tuple-element.26._.y2_in), custom_call_target="tpu_custom_call" | custom-call | tf_op jit(solution)/shard_map/inner/pallas_call | solution.py:575
  45.1 0.8 collective-permute-done.2.before
  46.0 0.0 copy-start.1
  46.0 2.6 %collective-permute-done.3.after = bf16[1024,256]{1,0:T(8,128)(2,1)S(1)} collective-permute-done((bf16[1024,256]{1,0:T(8,128)(2,1)S(1)}, bf16[1024,256]{1,0:T(8,128)(2,1)S(1)}, u32[]{:S(2)}, u32[]{:S(2)}) %collective-permute-start.3) | collective-permute-done | bytes 524320 | tf_op jit(solution)/shard_map/ppermute | solution.py:541
  48.5 0.0 copy-start.2
  48.5 0.0 copy-done.1
  48.5 0.8 copy-done.2
  49.3 6.6 %outer.1 = (bf16[16,512,128]{2,1,0:T(8,128)(2,1)}, bf16[10,256,128]{2,1,0:T(8,128)(2,1)}, f32[2,8,256]{2,1,0:T(8,128)}, f32[2,8,256]{2,1,0:T(8,128)}) custom-call(bf16[16,512,256]{2,1,0:T(8,128)(2,1)} %bitcast.11, bf16[8,256,256]{2,1,0:T(8,128)(2,1)} %bitcast.14, bf16[1024,256]{1,0:T(8,128)(2,1)} %copy-done.1, ...), custom_call_target="tpu_custom_call", output_to_operand_aliasing={{0}: (5, {}), {1}: (6, {})} | custom-call | tf_op jit(solution)/shard_map/outer/pallas_call | solution.py:587
  55.9 0.0 copy-start.7
  55.9 0.0 all-to-all-done.got
  55.9 0.0 copy-start
  55.9 0.8 copy-done
  56.8 11.9 %between.1 = (bf16[10,256,128]{2,1,0:T(8,128)(2,1)}, bf16[10,256,128]{2,1,0:T(8,128)(2,1)}, f32[5,8,256]{2,1,0:T(8,128)}, f32[5,8,256]{2,1,0:T(8,128)}, f32[16,16,128]{2,1,0:T(8,128)}) custom-call(s32[1]{0:T(128)} %bitcast.place, bf16[16,160,128]{2,1,0:T(8,128)(2,1)} %copy-done, f32[8,128,128]{2,1,0:T(8,128)} %get-tuple-element.26._.y2_in, ...), custom_call_target="tpu_custom_call" | custom-call | tf_op jit(solution)/shard_map/between/pallas_call | solution.py:606
  68.7 6.4 %all-to-all-start.1 = ((f32[16,16,128]{2,1,0:T(8,128)}), f32[16,16,128]{2,1,0:T(8,128)S(1)}, u32[]{:S(2)}, u32[]{:S(2)}) async-start(f32[16,16,128]{2,1,0:T(8,128)} %get-tuple-element.35), calls=%async_computation.1 | async-start | bytes 262144 | tf_op jit(solution)/shard_map/all_to_all | solution.py:35
  75.1 0.0 copy-done.7
  75.2 0.0 copy-start.6
  75.2 0.6 pad_maximum_fusion.class_t3
  75.8 6.2 %all-to-all-done.1.got = f32[16,16,128]{2,1,0:T(8,128)S(1)} async-done(((f32[16,16,128]{2,1,0:T(8,128)}), f32[16,16,128]{2,1,0:T(8,128)S(1)}, u32[]{:S(2)}, u32[]{:S(2)}) %all-to-all-start.1) | async-done | bytes 131104 | tf_op jit(solution)/shard_map/all_to_all | solution.py:35
  82.0 0.0 copy-start.3
  82.0 0.0 copy-done.6
  82.0 0.7 copy-done.3
  82.6 6.5 %final.1 = (bf16[19,16,512]{2,1,0:T(8,128)(2,1)}, f32[128,2,128]{2,1,0:T(2,128)}) custom-call(s32[1]{0:T(128)} %bitcast.place, f32[19]{0:T(128)} %bias.1, f32[16,16,128]{2,1,0:T(8,128)} %copy-done.3, f32[7,128]{1,0:T(8,128)} %gain.3, f32[7,128]{1,0:T(8,128)} %shift.3, f32[6,8,256]{2,1,0:T(8,128)} %get-tuple-element.27.inner0, ...), custom_call_target="tpu_custom_call" | custom-call | tf_op jit(solution)/shard_map/final/pallas_call | solution.py:630
  89.1 19.7 %all_to_all.15 = f32[128,2,128]{2,1,0:T(2,128)S(1)} all-to-all(f32[128,2,128]{2,1,0:T(2,128)} %get-tuple-element.43), channel_id=1, replica_groups=mesh['batch_0'=4,'batch_1'=2,'rows_0'=4,'rows_1'=4] {'batch_0','batch_1'..., dimensions={0} | all-to-all | bytes 262144 | tf_op jit(solution)/shard_map/all_to_all | solution.py:35
  108.8 0.3 reduce_sum.9
  109.0 0.6 fusion
  (1 shorter events, 0.0 us)
Async XLA Ops:
  3.3 8.6 %collective-permute-start = (bf16[448,256]{1,0:T(8,128)(2,1)}, bf16[448,256]{1,0:T(8,128)(2,1)S(1)}, u32[]{:S(2)}, u32[]{:S(2)}) collective-permute-start(bf16[448,256]{1,0:T(8,128)(2,1)} %get-tuple-element.23), channel_id=1, source_target_pairs={{0,1},{1,2},{2,3},{3,4},{4,5},{5,6},{6,7},{7,8},{8,9},{9,10},{10,1... | collective-permute-start | bytes 688136 | tf_op jit(solution)/shard_map/ppermute | solution.py:538
  7.4 22.0 %copy-start.9 = (bf16[1024,256]{1,0:T(8,128)(2,1)S(1)}, bf16[1024,256]{1,0:T(8,128)(2,1)}, u32[]{:S(2)}) copy-start(bf16[1024,256]{1,0:T(8,128)(2,1)} %get-tuple-element.28) | copy-start | bytes 1572868
  7.4 25.3 %copy-start.8 = (bf16[1024,256]{1,0:T(8,128)(2,1)S(1)}, bf16[1024,256]{1,0:T(8,128)(2,1)}, u32[]{:S(2)}) copy-start(bf16[1024,256]{1,0:T(8,128)(2,1)} %get-tuple-element.29) | copy-start | bytes 1572868
  7.4 8.4 %collective-permute-start.1 = (bf16[448,256]{1,0:T(8,128)(2,1)}, bf16[448,256]{1,0:T(8,128)(2,1)S(1)}, u32[]{:S(2)}, u32[]{:S(2)}) collective-permute-start(bf16[448,256]{1,0:T(8,128)(2,1)} %get-tuple-element.24), channel_id=1, source_target_pairs={{1,0},{2,1},{3,2},{4,3},{5,4},{6,5},{7,6},{8,7},{9,8},{10,9},{11,1... | collective-permute-start | bytes 688136 | tf_op jit(solution)/shard_map/ppermute | solution.py:539
  11.9 3.9 %copy-start.4 = (bf16[448,256]{1,0:T(8,128)(2,1)}, bf16[448,256]{1,0:T(8,128)(2,1)S(1)}, u32[]{:S(2)}) copy-start(bf16[448,256]{1,0:T(8,128)(2,1)S(1)} %collective-permute-done.before) | copy-start | bytes 688132
  15.8 0.7 copy-start.5
  20.1 35.8 %all-to-all-start = ((bf16[16,160,128]{2,1,0:T(8,128)(2,1)}), bf16[16,160,128]{2,1,0:T(8,128)(2,1)S(1)}, u32[]{:S(2)}, u32[]{:S(2)}) async-start(bf16[16,160,128]{2,1,0:T(8,128)(2,1)} %get-tuple-element.25), calls=%async_computation | async-start | bytes 1310720 | tf_op jit(solution)/shard_map/all_to_all | solution.py:35
  29.4 16.6 %collective-permute-start.2 = (bf16[1024,256]{1,0:T(8,128)(2,1)S(1)}, bf16[1024,256]{1,0:T(8,128)(2,1)S(1)}, u32[]{:S(2)}, u32[]{:S(2)}) collective-permute-start(bf16[1024,256]{1,0:T(8,128)(2,1)S(1)} %copy-done.9), channel_id=1, source_target_pairs={{0,1},{1,2},{2,3},{3,4},{4,5},{5,6},{6,7},{7,8},{8,9},{9,10},{10,1... | collective-permute-start | bytes 1572872 | tf_op jit(solution)/shard_map/ppermute | solution.py:540
  32.7 15.8 %collective-permute-start.3 = (bf16[1024,256]{1,0:T(8,128)(2,1)S(1)}, bf16[1024,256]{1,0:T(8,128)(2,1)S(1)}, u32[]{:S(2)}, u32[]{:S(2)}) collective-permute-start(bf16[1024,256]{1,0:T(8,128)(2,1)S(1)} %copy-done.8), channel_id=1, source_target_pairs={{1,0},{2,1},{3,2},{4,3},{5,4},{6,5},{7,6},{8,7},{9,8},{10,9},{11,1... | collective-permute-start | bytes 1572872 | tf_op jit(solution)/shard_map/ppermute | solution.py:541
  46.0 2.6 %copy-start.1 = (bf16[1024,256]{1,0:T(8,128)(2,1)}, bf16[1024,256]{1,0:T(8,128)(2,1)S(1)}, u32[]{:S(2)}) copy-start(bf16[1024,256]{1,0:T(8,128)(2,1)S(1)} %collective-permute-done.2.before) | copy-start | bytes 1572868
  48.5 0.8 copy-start.2
  55.9 19.2 %copy-start.7 = (bf16[128,19]{0,1:T(8,128)(2,1)S(1)}, bf16[128,19]{0,1:T(8,128)(2,1)}, u32[]{:S(2)}) copy-start(bf16[128,19]{0,1:T(8,128)(2,1)} %param.23) | copy-start | bytes 14596
  55.9 0.8 copy-start
  68.7 13.3 %all-to-all-start.1 = ((f32[16,16,128]{2,1,0:T(8,128)}), f32[16,16,128]{2,1,0:T(8,128)S(1)}, u32[]{:S(2)}, u32[]{:S(2)}) async-start(f32[16,16,128]{2,1,0:T(8,128)} %get-tuple-element.35), calls=%async_computation.1 | async-start | bytes 262144 | tf_op jit(solution)/shard_map/all_to_all | solution.py:35
  75.2 6.8 %copy-start.6 = (bf16[32,128]{1,0:T(8,128)(2,1)}, bf16[32,128]{1,0:T(8,128)(2,1)S(1)}, u32[]{:S(2)}) copy-start(bf16[32,128]{1,0:T(8,128)(2,1)S(1)} %pad.4.class_t) | copy-start | bytes 24580
  82.0 0.7 copy-start.3

commit v3 on v2

--- a/solution.py
+++ b/solution.py
@@ -15,7 +15,7 @@
 NORM_FLOOR = 0.05
 SMALL = (3, 1)
 BIG = (1, 2)
-STAT_ROWS = 32
+STAT_ROWS = 16
 SLOT = 32
 F32, BF16 = jnp.float32, jnp.bfloat16
 VMEM_LIMIT = 60 * 1024 * 1024
@@ -182,79 +182,69 @@
     quarter, eighth, weights, _, c0_out, c1_out, stats0, stats1, x0, x1, w0, w1, deep0, deep1, c0, c1, sems
 ):
     copies = Copies(sems)
-    inside = stats0.shape[0]
-    wait_w0 = copies.start(weights.at[0], w0)
-    rows_of = lambda r, n: copies.start(quarter.at[pl.ds(r, n)], x0.at[pl.ds(r, n)])
-    waits = [rows_of(1, 4), rows_of(5, 2)]
-    wait_w0.wait()
-    fill_deep(w0, deep0, 2 * HEAD)
+    rows0 = pl.ds(1, quarter.shape[0] - 2)
+    waits1 = [copies.start(weights.at[1], w1), copies.start(eighth, x1)]
+    waits0 = [copies.start(weights.at[0], w0), copies.start(quarter.at[rows0], x0.at[rows0])]
     out = []
-    for i in range(inside):
-        p = i + 1
-        waits[i].wait()
-        if i + 2 < inside:
-            waits.append(rows_of(2 * p + 5, 2))
-        elif i + 2 == inside:
-            wait_w1 = copies.start(weights.at[1], w1)
-            wait_x1 = copies.start(eighth, x1)
-        rows = [x0[2 * p - 1 + j] for j in range(4)]
-        keep_pair(conv_deep(rows, deep0), c0, stats0, i, p)
-        out.append(copies.start(c0.at[pl.ds(2 * p, 2)], c0_out.at[pl.ds(2 * p, 2)]))
-    wait_w1.wait()
+    for wait in waits1:
+        wait.wait()
     fill_deep(w1, deep1, 2 * HEAD)
-    wait_x1.wait()
     for i in range(stats1.shape[0]):
         p = i + 1
-        rows = [x1[2 * i + j] for j in range(4)]
-        keep_pair(conv_deep(rows, deep1), c1, stats1, i, p)
+        keep_pair(conv_deep([x1[2 * i + j] for j in range(4)], deep1), c1, stats1, i, p)
         out.append(copies.start(c1.at[pl.ds(2 * p, 2)], c1_out.at[pl.ds(2 * p, 2)]))
+    for wait in waits0:
+        wait.wait()
+    fill_deep(w0, deep0, 2 * HEAD)
+    for i in range(stats0.shape[0]):
+        p = i + 1
+        keep_pair(conv_deep([x0[2 * i + 1 + j] for j in range(4)], deep0), c0, stats0, i, p)
+        out.append(copies.start(c0.at[pl.ds(2 * p, 2)], c0_out.at[pl.ds(2 * p, 2)]))
     for copy in out:
         copy.wait()
 
 
-def outer_kernel(
-    quarter, eighth, before, after, weights, _, __, c0_out, c1_out, stats0, stats1,
-    x0, x1, low, high, w0, w1, deep0, deep1, c0, c1, sems,
-):
-    copies = Copies(sems)
-    q_rows, cols, _ = quarter.shape
-    e_rows, e_cols, _ = eighth.shape
-    wait_w0 = copies.start(weights.at[0], w0)
-    waits = [
-        copies.start(before, low),
-        copies.start(quarter.at[pl.ds(0, 3)], x0.at[pl.ds(0, 3)]),
-        copies.start(after, high),
-        copies.start(quarter.at[pl.ds(q_rows - 3, 3)], x0.at[pl.ds(3, 3)]),
-    ]
-    wait_w1 = copies.start(weights.at[1], w1)
-    waits1 = [
-        copies.start(eighth.at[pl.ds(0, 2)], x1.at[pl.ds(0, 2)]),
-        copies.start(eighth.at[pl.ds(e_rows - 2, 2)], x1.at[pl.ds(2, 2)]),
-    ]
-    wait_w0.wait()
-    fill_deep(w0, deep0, 2 * HEAD)
-    out = []
-    for i in range(2):
-        waits[2 * i].wait()
-        waits[2 * i + 1].wait()
-        rows = [x0[3 * i + j] for j in range(3)]
-        rows = rows + [high[:cols]] if i else [low[:cols]] + rows
-        keep_pair(conv_deep(rows, deep0), c0, stats0, i, i)
-        spot = pl.ds(i * (q_rows - 2), 2)
-        out.append(copies.start(c0.at[pl.ds(2 * i, 2)], c0_out.at[spot]))
-    wait_w1.wait()
-    fill_deep(w1, deep1, 2 * HEAD)
-    for i in range(2):
-        waits1[i].wait()
-        halo = (high if i else low)
-        rows = [x1[2 * i + j] for j in range(2)]
-        extra = [halo[cols + j * e_cols : cols + (j + 1) * e_cols] for j in range(2)]
-        rows = rows + extra if i else extra + rows
-        keep_pair(conv_deep(rows, deep1), c1, stats1, i, i)
-        spot = pl.ds(i * e_rows, 2)
-        out.append(copies.start(c1.at[pl.ds(2 * i, 2)], c1_out.at[spot]))
-    for copy in out:
-        copy.wait()
+class Outer:
+    def __init__(self, copies, inputs, outputs, room):
+        self.copies, self.outputs, self.room = copies, outputs, room
+        quarter, eighth, before, after, weights = inputs
+        x0, x1, low, high, w0, w1 = room[:6]
+        self.q_rows, self.cols, _ = quarter.shape
+        self.e_rows, self.e_cols, _ = eighth.shape
+        pairs = (
+            (weights.at[1], w1),
+            (weights.at[0], w0),
+            (before, low),
+            (after, high),
+            (eighth.at[pl.ds(0, 2)], x1.at[pl.ds(0, 2)]),
+            (eighth.at[pl.ds(self.e_rows - 2, 2)], x1.at[pl.ds(2, 2)]),
+            (quarter.at[pl.ds(0, 3)], x0.at[pl.ds(0, 3)]),
+            (quarter.at[pl.ds(self.q_rows - 3, 3)], x0.at[pl.ds(3, 3)]),
+        )
+        self.waits = [copies.start(*pair) for pair in pairs]
+
+    def work(self):
+        for wait in self.waits:
+            wait.wait()
+        c0_out, c1_out, stats0, stats1 = self.outputs
+        x0, x1, low, high, w0, w1, deep0, deep1, c0, c1 = self.room
+        fill_deep(w1, deep1, 2 * HEAD)
+        fill_deep(w0, deep0, 2 * HEAD)
+        cols, e_cols = self.cols, self.e_cols
+        for i in range(2):
+            rows = [x0[3 * i + j] for j in range(3)]
+            keep_pair(conv_deep(rows + [high[:cols]] if i else [low[:cols]] + rows, deep0), c0, stats0, i, i)
+        for i in range(2):
+            halo = high if i else low
+            rows = [x1[2 * i + j] for j in range(2)]
+            extra = [halo[cols + j * e_cols : cols + (j + 1) * e_cols] for j in range(2)]
+            keep_pair(conv_deep(rows + extra if i else extra + rows, deep1), c1, stats1, i, i)
+        out = []
+        for i in range(2):
+            spot = pl.ds(2 * i, 2)
+            out.append(self.copies.start(c0.at[spot], c0_out.at[pl.ds(i * (self.q_rows - 2), 2)]))
+            out.append(self.copies.start(c1.at[spot], c1_out.at[pl.ds(i * self.e_rows, 2)]))
+        return out
 
 
 def coarse_kernel(before, after, sixteenth, thirty, w2, w3, y2, pieces, wide2, wide3):
@@ -278,17 +268,18 @@
     total3, square3, coarse = centre(jnp.concatenate([out[:, :HEAD], out[:, HEAD:]], axis=0))
     coarse = coarse.astype(BF16)
     total, square = merge(parts, cols)
-    values = jnp.concatenate([total, square, total3, square3, jnp.zeros((4, HEAD), F32)], axis=0)
-    head = jnp.concatenate(split_rows(values) + [jnp.zeros((8, HEAD), F32)], axis=0).astype(BF16)
+    values = jnp.concatenate([total, square, total3, square3], axis=0)
+    head = jnp.concatenate(split_rows(values) + [jnp.zeros((4, HEAD), F32)], axis=0).astype(BF16)
     for i in range(pieces.shape[0]):
         pieces[i, :STAT_ROWS] = head
         pieces[i, STAT_ROWS:] = coarse
 
 
 def between_kernel(
-    place, got, y2_in, weights_in, gain, shift, up_small, up_big, inner0, outer0, inner1, outer1,
-    c4_out, c6_out, stats4, stats6, pieces,
-    y2, weights, c4, c6, fine, coarse, field5, stats5, wide0, wide1, wide2, sems,
+    place, got, y2_in, weights_in, gain, shift, up_small, up_big, inner0, inner1,
+    quarter, eighth, before, after, first_weights, _, __,
+    c0_out, c1_out, outer0, outer1, c4_out, c6_out, stats4, stats6, pieces,
+    y2, weights, c4, c6, fine, coarse, field5, stats5, wide0, wide1, wide2, sems, *room,
 ):
     members = got.shape[0]
     position = place[0]
@@ -296,6 +287,9 @@
     copies = Copies(sems)
     wait_w = copies.start(weights_in, weights)
     wait_y2 = copies.start(y2_in, y2)
+    outer = Outer(
+        copies, (quarter, eighth, before, after, first_weights), (c0_out, c1_out, outer0, outer1), room
+    )
     out = []
 
     def merged_norm(each, pixels, layer):
@@ -333,7 +327,7 @@
     lines, cols = coarse.shape[0] - 2, coarse.shape[1]
     small = cols // 2
     blocks = [got[i, :STAT_ROWS].astype(F32) for i in range(members)]
-    blocks = [b[0:8] + b[8:16] + b[16:24] for b in blocks]
+    blocks = [b[0:4] + b[4:8] + b[8:12] for b in blocks]
     norm3 = merged_norm([(b[2:3], b[3:4]) for b in blocks], 2 * small, 3)
     doubled = []
     for i in range(members):
@@ -368,7 +362,7 @@
         stats5[q, 1:2] = square
         return carry
 
-    lax.fori_loop(0, lines // (2 * fold), step, 0, unroll=2)
+    lax.fori_loop(0, lines // (2 * fold), step, 0, unroll=True)
     wait_y2.wait()
     norm2 = merged_norm([(b[0:1], b[1:2]) for b in blocks], y2.shape[1] * (y2.shape[0] - 4), 2)
     acts = [normed(y2[i], *norm2) for i in range(y2.shape[0])]
@@ -376,6 +370,7 @@
     acts[1] = jnp.where(first, acts[2], acts[1])
     acts[count - 2] = jnp.where(last, acts[count - 3], acts[count - 2])
     merged4 = up_conv(acts, wide0, c4, c4_out, stats4)
+    out += outer.work()
     parts5 = []
     for q in range(lines // (2 * fold)):
         parts5 += halves((stats5[q, 0:1], stats5[q, 1:2]))
@@ -412,10 +407,7 @@
     copies = Copies(sems)
     waits = [copies.start(a, b) for a, b in ((c1_in, c1), (c4_in, c4), (c6_in, c6))]
     rows = c0.shape[0]
-    chunk = rows // 4
-    waits0 = [
-        copies.start(c0_in.at[pl.ds(i * chunk, chunk)], c0.at[pl.ds(i * chunk, chunk)]) for i in range(4)
-    ]
+    wait0 = copies.start(c0_in, c0)
     count = c4.shape[0]
     first, last = place[0] == 0, place[0] == members - 1
     row = lax.broadcasted_iota(jnp.int32, (8, HEAD), 0)
@@ -457,9 +449,8 @@
         low = (value - high.astype(F32)).astype(BF16)
         both = matmul(jnp.concatenate([high, low], axis=0), up_cols[...])
         doubled[i] = both[:SLOT] + both[SLOT:]
+    wait0.wait()
     for r in range(rows):
-        if r % chunk == 0:
-            waits0[r // chunk].wait()
         p = r // 2
         value = matmul_t(class_t[...], lift(c0, r, totals0[p], norms[0]))
         value = value + (0.75 * doubled[p + 1] + 0.25 * doubled[p + 2 * (r % 2)])
@@ -564,7 +555,7 @@
         in_specs=[fixed(small), fixed(small), fixed(sixteenth), fixed(thirty), weight(2), weight(3)],
         out_specs=[fixed(y2_shape), fixed(piece)],
         scratch_shapes=[deep, deep],
-        compiler_params=params_of(),
+        compiler_params=pltpu.CompilerParams(vmem_limit_bytes=20*1024*1024),
         name="coarse",
     )
     y2, pieces = coarse_call(
@@ -584,30 +575,19 @@
         compiler_params=params_of(),
         name="inner",
     )(quarter, eighth, first_weights, y2)
-    c0, c1, outer0, outer1 = pl.pallas_call(
-        outer_kernel,
-        out_shape=[field0, field1, stats_shape(2), stats_shape(2)],
-        in_specs=[ANY] * 7,
-        out_specs=[ANY, ANY, VM, VM],
-        input_output_aliases={5: 0, 6: 1},
-        scratch_shapes=[
-            pltpu.VMEM((6, q_cols, depth), BF16), pltpu.VMEM((4, e_cols, depth), BF16), room(big), room(big),
-            raw, raw, deep, deep,
-            pltpu.VMEM((4, q_cols, HEAD), BF16), pltpu.VMEM((4, e_cols, HEAD), BF16),
-            pltpu.SemaphoreType.DMA((12,)),
-        ],
-        compiler_params=params_of(),
-        name="outer",
-    )(quarter, eighth, big_before, big_after, first_weights, c0, c1)
     up_small = jnp.asarray(doubling(t_cols), BF16)
     up_big = jnp.asarray(doubling(s_cols), BF16)
     up_cols = jnp.asarray(doubling(e_cols).T, BF16)
     narrow = pltpu.VMEM((4 * HEAD, 6 * HEAD), BF16)
-    c4, c6, stats4, stats6, pieces = pl.pallas_call(
+    c0, c1, outer0, outer1, c4, c6, stats4, stats6, pieces = pl.pallas_call(
         between_kernel,
-        out_shape=[field1, field1, stats_shape(steps), stats_shape(steps), shaped((bands, 16, HEAD), F32)],
-        in_specs=[SM, VM, ANY, ANY] + [VM] * 8,
-        out_specs=[ANY, ANY, VM, VM, VM],
+        out_shape=[
+            field0, field1, stats_shape(2), stats_shape(2),
+            field1, field1, stats_shape(steps), stats_shape(steps), shaped((bands, 16, HEAD), F32),
+        ],
+        in_specs=[SM, VM, ANY, ANY] + [VM] * 6 + [ANY] * 7,
+        out_specs=[ANY, ANY, VM, VM, ANY, ANY, VM, VM, VM],
+        input_output_aliases={15: 0, 16: 1},
         scratch_shapes=[
             room(y2), room(inner_weights), room(field1), room(field1),
             pltpu.VMEM((e_rows + 4, e_cols, HEAD), BF16),
@@ -615,13 +595,16 @@
             pltpu.VMEM((2 * t_rows * bands, 2 * t_cols, HEAD), F32),
             pltpu.VMEM((t_rows * bands, 8, 2 * HEAD), F32),
             narrow, narrow, narrow,
-            pltpu.SemaphoreType.DMA((2 * steps + 2,)),
+            pltpu.SemaphoreType.DMA((2 * steps + 14,)),
+            pltpu.VMEM((6, q_cols, depth), BF16), pltpu.VMEM((4, e_cols, depth), BF16), room(big), room(big),
+            raw, raw, deep, deep,
+            pltpu.VMEM((4, q_cols, HEAD), BF16), pltpu.VMEM((4, e_cols, HEAD), BF16),
         ],
         compiler_params=params_of(),
         name="between",
     )(
         place, got, y2, inner_weights, norm_gain, norm_shift, up_small, up_big,
-        inner0, outer0, inner1, outer1,
+        inner0, inner1, quarter, eighth, big_before, big_after, first_weights, c0, c1,
     )
     got = everyone(pieces, ROWS)
     classes = class_weight.shape[1]

time: 113 us -> 105 us (0.929)
  Pallas kernels: 42.4 us -> 33.7 us
  waiting for transfers between devices: 16.6 us -> 18.4 us
    pallas_call x2 -> x1, Pallas kernels: 18.5 us -> 13.8 us  [device_step(): pl.pallas_call(between_kernel, out_shape=[field0, field1, stats_shape(2),...]
    pallas_call x1, Pallas kernels: 11.1 us -> 8.77 us  [device_step(): pl.pallas_call(inner_kernel, out_shape=[field0, field1, stats_shape(insid...]
    ppermute x1, waiting for transfers between devices: 0.83 us -> 2.49 us  [device_step(): big_before = lax.ppermute(big_before, ROWS, up_pairs)]
    pallas_call x1, Pallas kernels: 3.63 us -> 2.01 us  [device_step(): coarse_call(small_before, small_after, sixteenth, thirty, first_weights,...]
    unnamed x20 -> x24, local copies, waits for them, and re-layouts: 2.99 us -> 2.45 us
  transfers between devices with their start and end apart: 6 -> 6, of which waited for: 5 -> 5; matrix products, arithmetic and copies ran while one was open for 1% -> 1% of each run, Pallas kernels for 16% -> 8%
where the time goes in v3:
time: 105 us
  Pallas kernels  33.7 us (32%)
  starting transfers between devices  25.6 us (24%)
  blocking collectives  20 us (19%)
  waiting for transfers between devices  18.4 us (18%)
  between operations  3.22 us (3%)
  local copies, waits for them, and re-layouts  3.04 us (3%)
    all_to_all x1, blocking collectives, everyone(): return lax.all_to_all(pieces, axes, 0, 0)  20 us
    all_to_all x2, starting transfers between devices, everyone(): return lax.all_to_all(pieces, axes, 0, 0)  15.6 us
    pallas_call x1, Pallas kernels, device_step(): pl.pallas_call(between_kernel, out_shape=[field0, field1, stats_shape(2),...  13.8 us
    pallas_call x1, Pallas kernels, device_step(): pl.pallas_call(inner_kernel, out_shape=[field0, field1, stats_shape(insid...  8.77 us
    pallas_call x1, Pallas kernels, device_step(): pl.pallas_call(final_kernel, out_shape=[shaped((classes, q_rows, q_cols),...  6.28 us
    all_to_all x2, waiting for transfers between devices, everyone(): return lax.all_to_all(pieces, axes, 0, 0)  6.21 us
    ppermute x1, starting transfers between devices, device_step(): small_before = lax.ppermute(small_before, ROWS, up_pairs)  4.03 us
    ppermute x1, waiting for transfers between devices, device_step(): small_after = lax.ppermute(small_after, ROWS, down_pairs)  3.89 us
  transfers between devices with their start and end apart: 6, of which 5 were waited for; matrix products, arithmetic and copies ran while one was open for 1% of the time, Pallas kernels for 8%

profile of v3, /device:TPU:1, one launch (start us, length us, event | category | flops | bytes accessed | tf_op | source)
XLA Modules:
  0.0 104.9 jit_solution(4268271337308446944)
XLA Ops:
  0.6 0.0 copy-start
  0.6 0.0 copy-start.2
  0.7 0.0 copy-start.3
  0.7 2.8 %edges.1 = (bf16[448,256]{1,0:T(8,128)(2,1)}, bf16[448,256]{1,0:T(8,128)(2,1)}, bf16[1024,256]{1,0:T(8,128)(2,1)}, bf16[1024,256]{1,0:T(8,128)(2,1)}) custom-call(bf16[16,512,256]{2,1,0:T(8,128)(2,1)} %bitcast.13, bf16[8,256,256]{2,1,0:T(8,128)(2,1)} %bitcast.16, bf16[4,128,256]{2,1,0:T(8,128)(2,1)} %bitcast.9, bf16[2,64,256]{2,1,0:T(8,128)(2,1)} %bitcast.11), custom_call_target="tpu_custom_call" | custom-call | tf_op jit(solution)/shard_map/edges/pallas_call | solution.py:520
  3.5 4.0 %collective-permute-start = (bf16[448,256]{1,0:T(8,128)(2,1)}, bf16[448,256]{1,0:T(8,128)(2,1)S(1)}, u32[]{:S(2)}, u32[]{:S(2)}) collective-permute-start(bf16[448,256]{1,0:T(8,128)(2,1)} %get-tuple-element.23), channel_id=1, source_target_pairs={{0,1},{1,2},{2,3},{3,4},{4,5},{5,6},{6,7},{7,8},{8,9},{9,10},{10,1... | collective-permute-start | bytes 688136 | tf_op jit(solution)/shard_map/ppermute | solution.py:529
  7.5 0.0 copy-start.11
  7.5 0.0 copy-start.10
  7.5 1.4 %collective-permute-start.1 = (bf16[448,256]{1,0:T(8,128)(2,1)}, bf16[448,256]{1,0:T(8,128)(2,1)S(1)}, u32[]{:S(2)}, u32[]{:S(2)}) collective-permute-start(bf16[448,256]{1,0:T(8,128)(2,1)} %get-tuple-element.24), channel_id=1, source_target_pairs={{1,0},{2,1},{3,2},{4,3},{5,4},{6,5},{7,6},{8,7},{9,8},{10,9},{11,1... | collective-permute-start | bytes 688136 | tf_op jit(solution)/shard_map/ppermute | solution.py:530
  9.0 3.1 %collective-permute-done.before = bf16[448,256]{1,0:T(8,128)(2,1)S(1)} collective-permute-done((bf16[448,256]{1,0:T(8,128)(2,1)}, bf16[448,256]{1,0:T(8,128)(2,1)S(1)}, u32[]{:S(2)}, u32[]{:S(2)}) %collective-permute-start) | collective-permute-done | bytes 229408 | tf_op jit(solution)/shard_map/ppermute | solution.py:529
  12.1 3.9 %collective-permute-done.1.after = bf16[448,256]{1,0:T(8,128)(2,1)S(1)} collective-permute-done((bf16[448,256]{1,0:T(8,128)(2,1)}, bf16[448,256]{1,0:T(8,128)(2,1)S(1)}, u32[]{:S(2)}, u32[]{:S(2)}) %collective-permute-start.1) | collective-permute-done | bytes 229408 | tf_op jit(solution)/shard_map/ppermute | solution.py:530
  16.0 0.0 copy-done
  16.0 0.0 copy-done.2
  16.0 0.0 copy-done.3
  16.0 2.0 %coarse.1 = (f32[8,128,128]{2,1,0:T(8,128)S(1)}, bf16[16,144,128]{2,1,0:T(8,128)(2,1)}) custom-call(bf16[448,256]{1,0:T(8,128)(2,1)S(1)} %collective-permute-done.before, bf16[448,256]{1,0:T(8,128)(2,1)S(1)} %collective-permute-done.1.after, bf16[4,128,256]{2,1,0:T(8,128)(2,1)S(1)} %bitcast.10, bf16[2,64,256]{2,1,0:T(8,128)(2,1)S(1)} %bitcast.12, ...), custom_call_target="tpu_custom_call" | custom-call | tf_op jit(solution)/shard_map/coarse/pallas_call | solution.py:561
  18.0 0.0 copy-start.1
  18.0 0.8 copy-done.1
  18.8 9.2 %all-to-all-start = ((bf16[16,144,128]{2,1,0:T(8,128)(2,1)}), bf16[16,144,128]{2,1,0:T(8,128)(2,1)S(1)}, u32[]{:S(2)}, u32[]{:S(2)}) async-start(bf16[16,144,128]{2,1,0:T(8,128)(2,1)} %get-tuple-element.25), calls=%async_computation | async-start | bytes 1179648 | tf_op jit(solution)/shard_map/all_to_all | solution.py:35
  28.0 0.0 copy-done.11
  28.0 3.3 %collective-permute-start.2 = (bf16[1024,256]{1,0:T(8,128)(2,1)S(1)}, bf16[1024,256]{1,0:T(8,128)(2,1)S(1)}, u32[]{:S(2)}, u32[]{:S(2)}) collective-permute-start(bf16[1024,256]{1,0:T(8,128)(2,1)S(1)} %copy-done.11), channel_id=1, source_target_pairs={{0,1},{1,2},{2,3},{3,4},{4,5},{5,6},{6,7},{7,8},{8,9},{9,10},{10,1... | collective-permute-start | bytes 1572872 | tf_op jit(solution)/shard_map/ppermute | solution.py:531
  31.3 0.0 copy-done.10
  31.4 1.3 %collective-permute-start.3 = (bf16[1024,256]{1,0:T(8,128)(2,1)S(1)}, bf16[1024,256]{1,0:T(8,128)(2,1)S(1)}, u32[]{:S(2)}, u32[]{:S(2)}) collective-permute-start(bf16[1024,256]{1,0:T(8,128)(2,1)S(1)} %copy-done.10), channel_id=1, source_target_pairs={{1,0},{2,1},{3,2},{4,3},{5,4},{6,5},{7,6},{8,7},{9,8},{10,9},{11,1... | collective-permute-start | bytes 1572872 | tf_op jit(solution)/shard_map/ppermute | solution.py:532
  32.7 8.8 %inner.1 = (bf16[16,512,128]{2,1,0:T(8,128)(2,1)}, bf16[10,256,128]{2,1,0:T(8,128)(2,1)}, f32[6,8,256]{2,1,0:T(8,128)}, f32[3,8,256]{2,1,0:T(8,128)}) custom-call(bf16[16,512,256]{2,1,0:T(8,128)(2,1)} %bitcast.14, bf16[8,256,256]{2,1,0:T(8,128)(2,1)} %bitcast.17, bf16[4,3,3,256,128]{4,3,2,1,0:T(8,128)(2,1)} %first_weights.1, f32[8,128,128]{2,1,0:T(8,128)} %copy-done.1), custom_call_target="tpu_custom_call" | custom-call | tf_op jit(solution)/shard_map/inner/pallas_call | solution.py:566
  41.4 2.5 %collective-permute-done.2.before = bf16[1024,256]{1,0:T(8,128)(2,1)S(1)} collective-permute-done((bf16[1024,256]{1,0:T(8,128)(2,1)S(1)}, bf16[1024,256]{1,0:T(8,128)(2,1)S(1)}, u32[]{:S(2)}, u32[]{:S(2)}) %collective-permute-start.2) | collective-permute-done | bytes 524320 | tf_op jit(solution)/shard_map/ppermute | solution.py:531
  43.9 0.0 copy-start.6
  43.9 2.7 %collective-permute-done.3.after = bf16[1024,256]{1,0:T(8,128)(2,1)S(1)} collective-permute-done((bf16[1024,256]{1,0:T(8,128)(2,1)S(1)}, bf16[1024,256]{1,0:T(8,128)(2,1)S(1)}, u32[]{:S(2)}, u32[]{:S(2)}) %collective-permute-start.3) | collective-permute-done | bytes 524320 | tf_op jit(solution)/shard_map/ppermute | solution.py:532
  46.7 0.0 copy-start.7
  46.7 0.0 all-to-all-done.got
  46.7 0.0 copy-start.4
  46.7 0.0 copy-done.6
  46.7 0.8 copy-done.7
  47.5 0.2 copy-done.4
  47.6 0.0 copy-start.9
  47.6 13.8 %between.1 = (bf16[16,512,128]{2,1,0:T(8,128)(2,1)}, bf16[10,256,128]{2,1,0:T(8,128)(2,1)}, f32[2,8,256]{2,1,0:T(8,128)}, f32[2,8,256]{2,1,0:T(8,128)}, bf16[10,...) custom-call(s32[1]{0:T(128)} %bitcast.place, ...), custom_call_target="tpu_custom_call", output_to_operand_aliasing={{0}: (15, {}), {1}: (16, {})} | custom-call | tf_op jit(solution)/shard_map/between/pallas_call | solution.py:582
  61.5 6.3 %all-to-all-start.1 = ((f32[16,16,128]{2,1,0:T(8,128)}), f32[16,16,128]{2,1,0:T(8,128)S(1)}, u32[]{:S(2)}, u32[]{:S(2)}) async-start(f32[16,16,128]{2,1,0:T(8,128)} %get-tuple-element.33), calls=%async_computation.1 | async-start | bytes 262144 | tf_op jit(solution)/shard_map/all_to_all | solution.py:35
  67.8 0.0 copy-done.9
  67.9 0.0 copy-start.8
  67.9 0.6 pad_maximum_fusion.class_t3
  68.5 6.2 %all-to-all-done.1.got = f32[16,16,128]{2,1,0:T(8,128)S(1)} async-done(((f32[16,16,128]{2,1,0:T(8,128)}), f32[16,16,128]{2,1,0:T(8,128)S(1)}, u32[]{:S(2)}, u32[]{:S(2)}) %all-to-all-start.1) | async-done | bytes 131104 | tf_op jit(solution)/shard_map/all_to_all | solution.py:35
  74.7 0.0 copy-start.5
  74.7 0.0 copy-done.8
  74.7 0.6 copy-done.5
  75.3 6.3 %final.1 = (bf16[19,16,512]{2,1,0:T(8,128)(2,1)}, f32[128,2,128]{2,1,0:T(2,128)}) custom-call(s32[1]{0:T(128)} %bitcast.place, f32[19]{0:T(128)} %bias.1, f32[16,16,128]{2,1,0:T(8,128)} %copy-done.5, f32[7,128]{1,0:T(8,128)} %gain.3, f32[7,128]{1,0:T(8,128)} %shift.3, f32[6,8,256]{2,1,0:T(8,128)} %get-tuple-element.27.inner0, ...), custom_call_target="tpu_custom_call" | custom-call | tf_op jit(solution)/shard_map/final/pallas_call | solution.py:613
  81.6 20.0 %all_to_all.15 = f32[128,2,128]{2,1,0:T(2,128)S(1)} all-to-all(f32[128,2,128]{2,1,0:T(2,128)} %get-tuple-element.43), channel_id=1, replica_groups=mesh['batch_0'=4,'batch_1'=2,'rows_0'=4,'rows_1'=4] {'batch_0','batch_1'..., dimensions={0} | all-to-all | bytes 262144 | tf_op jit(solution)/shard_map/all_to_all | solution.py:35
  101.6 0.3 reduce_sum.9
  101.9 0.6 fusion
  (1 shorter events, 0.0 us)
Async XLA Ops:
  0.6 15.3 %copy-start = (bf16[4,3,3,256,128]{4,3,2,1,0:T(8,128)(2,1)S(1)}, bf16[4,3,3,256,128]{4,3,2,1,0:T(8,128)(2,1)}, u32[]{:S(2)}) copy-start(bf16[4,3,3,256,128]{4,3,2,1,0:T(8,128)(2,1)} %first_weights.1) | copy-start | bytes 7077892
  0.6 15.3 %copy-start.2 = (bf16[1,4,128,256]{3,2,1,0:T(8,128)(2,1)S(1)}, bf16[1,4,128,256]{3,2,1,0:T(8,128)(2,1)}, u32[]{:S(2)}) copy-start(bf16[1,4,128,256]{3,2,1,0:T(8,128)(2,1)} %param.16) | copy-start | bytes 786436
  0.7 15.3 %copy-start.3 = (bf16[1,2,64,256]{3,2,1,0:T(8,128)(2,1)S(1)}, bf16[1,2,64,256]{3,2,1,0:T(8,128)(2,1)}, u32[]{:S(2)}) copy-start(bf16[1,2,64,256]{3,2,1,0:T(8,128)(2,1)} %param.17) | copy-start | bytes 196612
  3.5 8.6 %collective-permute-start = (bf16[448,256]{1,0:T(8,128)(2,1)}, bf16[448,256]{1,0:T(8,128)(2,1)S(1)}, u32[]{:S(2)}, u32[]{:S(2)}) collective-permute-start(bf16[448,256]{1,0:T(8,128)(2,1)} %get-tuple-element.23), channel_id=1, source_target_pairs={{0,1},{1,2},{2,3},{3,4},{4,5},{5,6},{6,7},{7,8},{8,9},{9,10},{10,1... | collective-permute-start | bytes 688136 | tf_op jit(solution)/shard_map/ppermute | solution.py:529
  7.5 20.5 %copy-start.11 = (bf16[1024,256]{1,0:T(8,128)(2,1)S(1)}, bf16[1024,256]{1,0:T(8,128)(2,1)}, u32[]{:S(2)}) copy-start(bf16[1024,256]{1,0:T(8,128)(2,1)} %get-tuple-element.29) | copy-start | bytes 1572868
  7.5 23.8 %copy-start.10 = (bf16[1024,256]{1,0:T(8,128)(2,1)S(1)}, bf16[1024,256]{1,0:T(8,128)(2,1)}, u32[]{:S(2)}) copy-start(bf16[1024,256]{1,0:T(8,128)(2,1)} %get-tuple-element.30) | copy-start | bytes 1572868
  7.5 8.4 %collective-permute-start.1 = (bf16[448,256]{1,0:T(8,128)(2,1)}, bf16[448,256]{1,0:T(8,128)(2,1)S(1)}, u32[]{:S(2)}, u32[]{:S(2)}) collective-permute-start(bf16[448,256]{1,0:T(8,128)(2,1)} %get-tuple-element.24), channel_id=1, source_target_pairs={{1,0},{2,1},{3,2},{4,3},{5,4},{6,5},{7,6},{8,7},{9,8},{10,9},{11,1... | collective-permute-start | bytes 688136 | tf_op jit(solution)/shard_map/ppermute | solution.py:530
  18.0 0.8 copy-start.1
  18.8 27.9 %all-to-all-start = ((bf16[16,144,128]{2,1,0:T(8,128)(2,1)}), bf16[16,144,128]{2,1,0:T(8,128)(2,1)S(1)}, u32[]{:S(2)}, u32[]{:S(2)}) async-start(bf16[16,144,128]{2,1,0:T(8,128)(2,1)} %get-tuple-element.25), calls=%async_computation | async-start | bytes 1179648 | tf_op jit(solution)/shard_map/all_to_all | solution.py:35
  28.0 15.9 %collective-permute-start.2 = (bf16[1024,256]{1,0:T(8,128)(2,1)S(1)}, bf16[1024,256]{1,0:T(8,128)(2,1)S(1)}, u32[]{:S(2)}, u32[]{:S(2)}) collective-permute-start(bf16[1024,256]{1,0:T(8,128)(2,1)S(1)} %copy-done.11), channel_id=1, source_target_pairs={{0,1},{1,2},{2,3},{3,4},{4,5},{5,6},{6,7},{7,8},{8,9},{9,10},{10,1... | collective-permute-start | bytes 1572872 | tf_op jit(solution)/shard_map/ppermute | solution.py:531
  31.4 15.3 %collective-permute-start.3 = (bf16[1024,256]{1,0:T(8,128)(2,1)S(1)}, bf16[1024,256]{1,0:T(8,128)(2,1)S(1)}, u32[]{:S(2)}, u32[]{:S(2)}) collective-permute-start(bf16[1024,256]{1,0:T(8,128)(2,1)S(1)} %copy-done.10), channel_id=1, source_target_pairs={{1,0},{2,1},{3,2},{4,3},{5,4},{6,5},{7,6},{8,7},{9,8},{10,9},{11,1... | collective-permute-start | bytes 1572872 | tf_op jit(solution)/shard_map/ppermute | solution.py:532
  43.9 2.7 %copy-start.6 = (bf16[1024,256]{1,0:T(8,128)(2,1)}, bf16[1024,256]{1,0:T(8,128)(2,1)S(1)}, u32[]{:S(2)}) copy-start(bf16[1024,256]{1,0:T(8,128)(2,1)S(1)} %collective-permute-done.2.before) | copy-start | bytes 1572868
  46.7 0.8 copy-start.7
  46.7 1.0 copy-start.4
  47.6 20.2 %copy-start.9 = (bf16[128,19]{0,1:T(8,128)(2,1)S(1)}, bf16[128,19]{0,1:T(8,128)(2,1)}, u32[]{:S(2)}) copy-start(bf16[128,19]{0,1:T(8,128)(2,1)} %param.23) | copy-start | bytes 14596
  61.5 13.2 %all-to-all-start.1 = ((f32[16,16,128]{2,1,0:T(8,128)}), f32[16,16,128]{2,1,0:T(8,128)S(1)}, u32[]{:S(2)}, u32[]{:S(2)}) async-start(f32[16,16,128]{2,1,0:T(8,128)} %get-tuple-element.33), calls=%async_computation.1 | async-start | bytes 262144 | tf_op jit(solution)/shard_map/all_to_all | solution.py:35
  67.9 6.8 %copy-start.8 = (bf16[32,128]{1,0:T(8,128)(2,1)}, bf16[32,128]{1,0:T(8,128)(2,1)S(1)}, u32[]{:S(2)}) copy-start(bf16[32,128]{1,0:T(8,128)(2,1)S(1)} %pad.4.class_t) | copy-start | bytes 24580
  74.7 0.7 copy-start.5

commit v4 on v3

--- a/solution.py
+++ b/solution.py
@@ -363,6 +363,7 @@
         return carry
 
     lax.fori_loop(0, lines // (2 * fold), step, 0, unroll=True)
+    out += outer.work()
     wait_y2.wait()
     norm2 = merged_norm([(b[0:1], b[1:2]) for b in blocks], y2.shape[1] * (y2.shape[0] - 4), 2)
     acts = [normed(y2[i], *norm2) for i in range(y2.shape[0])]
@@ -370,7 +371,6 @@
     acts[1] = jnp.where(first, acts[2], acts[1])
     acts[count - 2] = jnp.where(last, acts[count - 3], acts[count - 2])
     merged4 = up_conv(acts, wide0, c4, c4_out, stats4)
-    out += outer.work()
     parts5 = []
     for q in range(lines // (2 * fold)):
         parts5 += halves((stats5[q, 0:1], stats5[q, 1:2]))
@@ -391,8 +391,7 @@
         parts1.append(halves((outer1[p, 0:1], outer1[p, 1:2]))[1 - p])
     eighth_cols = c4.shape[1]
     merged = [merge(parts0, 2 * eighth_cols), merge(parts1, eighth_cols), merged4, merged6]
-    pad = [jnp.zeros((4, HEAD), F32)]
-    block = jnp.concatenate([m[0] for m in merged] + pad + [m[1] for m in merged] + pad, axis=0)
+    block = jnp.concatenate([m[0] for m in merged] + [m[1] for m in merged], axis=0)
     for i in range(members):
         pieces[i] = block
     for copy in out:
@@ -401,21 +400,20 @@
 
 def final_kernel(
     place, bias, got, gain, shift, inner0, outer0, inner1, outer1, stats4, stats6, labels, class_t, class_t3, up_cols,
-    c0_in, c1_in, c4_in, c6_in, logits, pieces, c0, c1, c4, c6, lines, doubled, scores, sems,
+    c1, c4, c6, c0_in, logits, pieces, c0, lines, doubled, scores, sems,
 ):
     members = got.shape[0]
     copies = Copies(sems)
-    waits = [copies.start(a, b) for a, b in ((c1_in, c1), (c4_in, c4), (c6_in, c6))]
     rows = c0.shape[0]
     wait0 = copies.start(c0_in, c0)
     count = c4.shape[0]
     first, last = place[0] == 0, place[0] == members - 1
-    row = lax.broadcasted_iota(jnp.int32, (8, HEAD), 0)
+    row = lax.broadcasted_iota(jnp.int32, (4, HEAD), 0)
     own = float((count - 2) * c4.shape[1])
     pixels = jnp.where(row == 0, 4.0 * own, own)
-    total = sum(got[i, 0:8] for i in range(members))
+    total = sum(got[i, 0:4] for i in range(members))
     mean = group_sum(total) / (pixels * (members * GROUP))
-    square = sum(got[i, 8:16] + pixels * jnp.square(got[i, 0:8] / pixels - mean) for i in range(members))
+    square = sum(got[i, 4:8] + pixels * jnp.square(got[i, 0:4] / pixels - mean) for i in range(members))
     scale = lax.rsqrt(group_sum(square) / (pixels * (members * GROUP)) + NORM_FLOOR)
     norms = [
         (mean[j : j + 1], gain[layer : layer + 1] * scale[j : j + 1], shift[layer : layer + 1])
@@ -431,8 +429,6 @@
         return [outer[0, 0:1]] + pairs + [outer[1, 0:1]]
 
     totals0, totals1 = joined(inner0, outer0), joined(inner1, outer1)
-    for wait in waits:
-        wait.wait()
     for i in range(count):
         p = i // 2
         acts = [
@@ -583,7 +579,7 @@
         between_kernel,
         out_shape=[
             field0, field1, stats_shape(2), stats_shape(2),
-            field1, field1, stats_shape(steps), stats_shape(steps), shaped((bands, 16, HEAD), F32),
+            field1, field1, stats_shape(steps), stats_shape(steps), shaped((bands, 8, HEAD), F32),
         ],
         in_specs=[SM, VM, ANY, ANY] + [VM] * 6 + [ANY] * 7,
         out_specs=[ANY, ANY, VM, VM, ANY, ANY, VM, VM, VM],
@@ -613,20 +609,20 @@
     logits, pieces = pl.pallas_call(
         final_kernel,
         out_shape=[shaped((classes, q_rows, q_cols), BF16), shaped((devices, 2, HEAD), F32)],
-        in_specs=[SM, SM] + [VM] * 13 + [ANY] * 4,
+        in_specs=[SM, SM] + [VM] * 16 + [ANY],
         out_specs=[VM, VM],
         scratch_shapes=[
-            room(field0), room(field1), room(field1), room(field1),
+            room(field0),
             pltpu.VMEM((e_rows + 2, SLOT, e_cols), F32),
             pltpu.VMEM((e_rows + 2, SLOT, q_cols), F32),
             pltpu.VMEM((q_cols // HEAD, q_rows * SLOT, HEAD), F32),
-            pltpu.SemaphoreType.DMA((7,)),
+            pltpu.SemaphoreType.DMA((1,)),
         ],
         compiler_params=params_of(),
         name="final",
     )(
         place, class_bias, got, norm_gain, norm_shift, inner0, outer0, inner1, outer1, stats4, stats6,
-        labels[0], class_t, class_t3, up_cols, c0, c1, c4, c6,
+        labels[0], class_t, class_t3, up_cols, c1, c4, c6, c0,
     )
     loss_total, valid_count = jnp.sum(everyone(pieces, EVERY), axis=(0, 2))
     mean_loss = loss_total / jnp.maximum(valid_count, 1.0)

time: 105 us -> 104 us (level)
  no operation moved by 1% of the time
where the time goes in v4:
time: 104 us
  Pallas kernels  32.8 us (32%)
  starting transfers between devices  25.6 us (25%)
  blocking collectives  20.1 us (19%)
  waiting for transfers between devices  18.1 us (17%)
  between operations  3.23 us (3%)
  local copies, waits for them, and re-layouts  3.01 us (3%)
    all_to_all x1, blocking collectives, everyone(): return lax.all_to_all(pieces, axes, 0, 0)  20.1 us
    all_to_all x2, starting transfers between devices, everyone(): return lax.all_to_all(pieces, axes, 0, 0)  15.6 us
    pallas_call x1, Pallas kernels, device_step(): pl.pallas_call(between_kernel, out_shape=[field0, field1, stats_shape(2),...  13.6 us
    pallas_call x1, Pallas kernels, device_step(): pl.pallas_call(inner_kernel, out_shape=[field0, field1, stats_shape(insid...  8.78 us
    all_to_all x2, waiting for transfers between devices, everyone(): return lax.all_to_all(pieces, axes, 0, 0)  5.91 us
    pallas_call x1, Pallas kernels, device_step(): pl.pallas_call(final_kernel, out_shape=[shaped((classes, q_rows, q_cols),...  5.6 us
    ppermute x1, starting transfers between devices, device_step(): small_before = lax.ppermute(small_before, ROWS, up_pairs)  4.03 us
    ppermute x1, waiting for transfers between devices, device_step(): small_after = lax.ppermute(small_after, ROWS, down_pairs)  3.9 us
  transfers between devices with their start and end apart: 6, of which 5 were waited for; matrix products, arithmetic and copies ran while one was open for 1% of the time, Pallas kernels for 8%

profile of v4, /device:TPU:1, one launch (start us, length us, event | category | flops | bytes accessed | tf_op | source)
XLA Modules:
  0.0 103.7 jit_solution(69907242949324985)
XLA Ops:
  0.6 0.0 copy-start
  0.6 0.0 copy-start.2
  0.7 0.0 copy-start.3
  0.7 2.8 %edges.1 = (bf16[448,256]{1,0:T(8,128)(2,1)}, bf16[448,256]{1,0:T(8,128)(2,1)}, bf16[1024,256]{1,0:T(8,128)(2,1)}, bf16[1024,256]{1,0:T(8,128)(2,1)}) custom-call(bf16[16,512,256]{2,1,0:T(8,128)(2,1)} %bitcast.13, bf16[8,256,256]{2,1,0:T(8,128)(2,1)} %bitcast.16, bf16[4,128,256]{2,1,0:T(8,128)(2,1)} %bitcast.9, bf16[2,64,256]{2,1,0:T(8,128)(2,1)} %bitcast.11), custom_call_target="tpu_custom_call" | custom-call | tf_op jit(solution)/shard_map/edges/pallas_call | solution.py:516
  3.5 4.0 %collective-permute-start = (bf16[448,256]{1,0:T(8,128)(2,1)}, bf16[448,256]{1,0:T(8,128)(2,1)S(1)}, u32[]{:S(2)}, u32[]{:S(2)}) collective-permute-start(bf16[448,256]{1,0:T(8,128)(2,1)} %get-tuple-element.23), channel_id=1, source_target_pairs={{0,1},{1,2},{2,3},{3,4},{4,5},{5,6},{6,7},{7,8},{8,9},{9,10},{10,1... | collective-permute-start | bytes 688136 | tf_op jit(solution)/shard_map/ppermute | solution.py:525
  7.5 0.0 copy-start.11
  7.5 0.0 copy-start.10
  7.5 0.0 copy-start.9
  7.5 1.4 %collective-permute-start.1 = (bf16[448,256]{1,0:T(8,128)(2,1)}, bf16[448,256]{1,0:T(8,128)(2,1)S(1)}, u32[]{:S(2)}, u32[]{:S(2)}) collective-permute-start(bf16[448,256]{1,0:T(8,128)(2,1)} %get-tuple-element.24), channel_id=1, source_target_pairs={{1,0},{2,1},{3,2},{4,3},{5,4},{6,5},{7,6},{8,7},{9,8},{10,9},{11,1... | collective-permute-start | bytes 688136 | tf_op jit(solution)/shard_map/ppermute | solution.py:526
  9.0 3.1 %collective-permute-done.before = bf16[448,256]{1,0:T(8,128)(2,1)S(1)} collective-permute-done((bf16[448,256]{1,0:T(8,128)(2,1)}, bf16[448,256]{1,0:T(8,128)(2,1)S(1)}, u32[]{:S(2)}, u32[]{:S(2)}) %collective-permute-start) | collective-permute-done | bytes 229408 | tf_op jit(solution)/shard_map/ppermute | solution.py:525
  12.1 3.9 %collective-permute-done.1.after = bf16[448,256]{1,0:T(8,128)(2,1)S(1)} collective-permute-done((bf16[448,256]{1,0:T(8,128)(2,1)}, bf16[448,256]{1,0:T(8,128)(2,1)S(1)}, u32[]{:S(2)}, u32[]{:S(2)}) %collective-permute-start.1) | collective-permute-done | bytes 229408 | tf_op jit(solution)/shard_map/ppermute | solution.py:526
  16.0 0.0 copy-done
  16.0 0.0 copy-done.2
  16.0 0.0 copy-done.3
  16.0 2.0 %coarse.1 = (f32[8,128,128]{2,1,0:T(8,128)S(1)}, bf16[16,144,128]{2,1,0:T(8,128)(2,1)}) custom-call(bf16[448,256]{1,0:T(8,128)(2,1)S(1)} %collective-permute-done.before, bf16[448,256]{1,0:T(8,128)(2,1)S(1)} %collective-permute-done.1.after, bf16[4,128,256]{2,1,0:T(8,128)(2,1)S(1)} %bitcast.10, bf16[2,64,256]{2,1,0:T(8,128)(2,1)S(1)} %bitcast.12, ...), custom_call_target="tpu_custom_call" | custom-call | tf_op jit(solution)/shard_map/coarse/pallas_call | solution.py:557
  18.0 0.0 copy-start.1
  18.0 0.8 copy-done.1
  18.8 9.2 %all-to-all-start = ((bf16[16,144,128]{2,1,0:T(8,128)(2,1)}), bf16[16,144,128]{2,1,0:T(8,128)(2,1)S(1)}, u32[]{:S(2)}, u32[]{:S(2)}) async-start(bf16[16,144,128]{2,1,0:T(8,128)(2,1)} %get-tuple-element.25), calls=%async_computation | async-start | bytes 1179648 | tf_op jit(solution)/shard_map/all_to_all | solution.py:35
  28.0 0.0 copy-done.11
  28.0 3.3 %collective-permute-start.2 = (bf16[1024,256]{1,0:T(8,128)(2,1)S(1)}, bf16[1024,256]{1,0:T(8,128)(2,1)S(1)}, u32[]{:S(2)}, u32[]{:S(2)}) collective-permute-start(bf16[1024,256]{1,0:T(8,128)(2,1)S(1)} %copy-done.11), channel_id=1, source_target_pairs={{0,1},{1,2},{2,3},{3,4},{4,5},{5,6},{6,7},{7,8},{8,9},{9,10},{10,1... | collective-permute-start | bytes 1572872 | tf_op jit(solution)/shard_map/ppermute | solution.py:527
  31.4 0.0 copy-done.10
  31.4 1.3 %collective-permute-start.3 = (bf16[1024,256]{1,0:T(8,128)(2,1)S(1)}, bf16[1024,256]{1,0:T(8,128)(2,1)S(1)}, u32[]{:S(2)}, u32[]{:S(2)}) collective-permute-start(bf16[1024,256]{1,0:T(8,128)(2,1)S(1)} %copy-done.10), channel_id=1, source_target_pairs={{1,0},{2,1},{3,2},{4,3},{5,4},{6,5},{7,6},{8,7},{9,8},{10,9},{11,1... | collective-permute-start | bytes 1572872 | tf_op jit(solution)/shard_map/ppermute | solution.py:528
  32.7 0.0 copy-done.9
  32.7 0.0 copy-start.8
  32.7 8.8 %inner.1 = (bf16[16,512,128]{2,1,0:T(8,128)(2,1)}, bf16[10,256,128]{2,1,0:T(8,128)(2,1)}, f32[6,8,256]{2,1,0:T(8,128)}, f32[3,8,256]{2,1,0:T(8,128)}) custom-call(bf16[16,512,256]{2,1,0:T(8,128)(2,1)} %bitcast.14, bf16[8,256,256]{2,1,0:T(8,128)(2,1)} %bitcast.17, bf16[4,3,3,256,128]{4,3,2,1,0:T(8,128)(2,1)} %first_weights.1, f32[8,128,128]{2,1,0:T(8,128)} %copy-done.1), custom_call_target="tpu_custom_call" | custom-call | tf_op jit(solution)/shard_map/inner/pallas_call | solution.py:562
  41.5 2.5 %collective-permute-done.2.before = bf16[1024,256]{1,0:T(8,128)(2,1)S(1)} collective-permute-done((bf16[1024,256]{1,0:T(8,128)(2,1)S(1)}, bf16[1024,256]{1,0:T(8,128)(2,1)S(1)}, u32[]{:S(2)}, u32[]{:S(2)}) %collective-permute-start.2) | collective-permute-done | bytes 524320 | tf_op jit(solution)/shard_map/ppermute | solution.py:527
  43.9 0.0 copy-start.5
  43.9 2.7 %collective-permute-done.3.after = bf16[1024,256]{1,0:T(8,128)(2,1)S(1)} collective-permute-done((bf16[1024,256]{1,0:T(8,128)(2,1)S(1)}, bf16[1024,256]{1,0:T(8,128)(2,1)S(1)}, u32[]{:S(2)}, u32[]{:S(2)}) %collective-permute-start.3) | collective-permute-done | bytes 524320 | tf_op jit(solution)/shard_map/ppermute | solution.py:528
  46.7 0.0 copy-start.6
  46.7 0.0 all-to-all-done.got
  46.7 0.0 copy-start.4
  46.7 0.0 copy-done.5
  46.7 0.8 copy-done.6
  47.5 0.2 copy-done.4
  47.7 13.6 %between.1 = (bf16[16,512,128]{2,1,0:T(8,128)(2,1)}, bf16[10,256,128]{2,1,0:T(8,128)(2,1)}, f32[2,8,256]{2,1,0:T(8,128)}, f32[2,8,256]{2,1,0:T(8,128)}, bf16[10,...) custom-call(s32[1]{0:T(128)} %bitcast.place, ...), custom_call_target="tpu_custom_call", output_to_operand_aliasing={{0}: (15, {}), {1}: (16, {})} | custom-call | tf_op jit(solution)/shard_map/between/pallas_call | solution.py:578
  61.3 6.3 %all-to-all-start.1 = ((f32[16,8,128]{2,1,0:T(8,128)}), f32[16,8,128]{2,1,0:T(8,128)S(1)}, u32[]{:S(2)}, u32[]{:S(2)}) async-start(f32[16,8,128]{2,1,0:T(8,128)} %get-tuple-element.33), calls=%async_computation.1 | async-start | bytes 131072 | tf_op jit(solution)/shard_map/all_to_all | solution.py:35
  67.6 0.0 copy-done.8
  67.7 0.6 pad_maximum_fusion.class_t3
  68.3 5.9 %all-to-all-done.1.got = f32[16,8,128]{2,1,0:T(8,128)S(1)} async-done(((f32[16,8,128]{2,1,0:T(8,128)}), f32[16,8,128]{2,1,0:T(8,128)S(1)}, u32[]{:S(2)}, u32[]{:S(2)}) %all-to-all-start.1) | async-done | bytes 65568 | tf_op jit(solution)/shard_map/all_to_all | solution.py:35
  74.2 0.0 copy-start.7
  74.2 0.6 copy-done.7
  74.8 5.6 %final.1 = (bf16[19,16,512]{2,1,0:T(8,128)(2,1)}, f32[128,2,128]{2,1,0:T(2,128)}) custom-call(s32[1]{0:T(128)} %bitcast.place, f32[19]{0:T(128)} %bias.1, f32[16,8,128]{2,1,0:T(8,128)} %copy-done.7, f32[7,128]{1,0:T(8,128)} %gain.3, f32[7,128]{1,0:T(8,128)} %shift.3, f32[6,8,256]{2,1,0:T(8,128)} %get-tuple-element.27.inner0, ...), custom_call_target="tpu_custom_call" | custom-call | tf_op jit(solution)/shard_map/final/pallas_call | solution.py:609
  80.4 20.1 %all_to_all.15 = f32[128,2,128]{2,1,0:T(2,128)S(1)} all-to-all(f32[128,2,128]{2,1,0:T(2,128)} %get-tuple-element.43), channel_id=1, replica_groups=mesh['batch_0'=4,'batch_1'=2,'rows_0'=4,'rows_1'=4] {'batch_0','batch_1'..., dimensions={0} | all-to-all | bytes 262144 | tf_op jit(solution)/shard_map/all_to_all | solution.py:35
  100.5 0.3 reduce_sum.9
  100.7 0.6 fusion
  (1 shorter events, 0.0 us)
Async XLA Ops:
  0.6 15.3 %copy-start = (bf16[4,3,3,256,128]{4,3,2,1,0:T(8,128)(2,1)S(1)}, bf16[4,3,3,256,128]{4,3,2,1,0:T(8,128)(2,1)}, u32[]{:S(2)}) copy-start(bf16[4,3,3,256,128]{4,3,2,1,0:T(8,128)(2,1)} %first_weights.1) | copy-start | bytes 7077892
  0.6 15.3 %copy-start.2 = (bf16[1,4,128,256]{3,2,1,0:T(8,128)(2,1)S(1)}, bf16[1,4,128,256]{3,2,1,0:T(8,128)(2,1)}, u32[]{:S(2)}) copy-start(bf16[1,4,128,256]{3,2,1,0:T(8,128)(2,1)} %param.16) | copy-start | bytes 786436
  0.7 15.3 %copy-start.3 = (bf16[1,2,64,256]{3,2,1,0:T(8,128)(2,1)S(1)}, bf16[1,2,64,256]{3,2,1,0:T(8,128)(2,1)}, u32[]{:S(2)}) copy-start(bf16[1,2,64,256]{3,2,1,0:T(8,128)(2,1)} %param.17) | copy-start | bytes 196612
  3.5 8.6 %collective-permute-start = (bf16[448,256]{1,0:T(8,128)(2,1)}, bf16[448,256]{1,0:T(8,128)(2,1)S(1)}, u32[]{:S(2)}, u32[]{:S(2)}) collective-permute-start(bf16[448,256]{1,0:T(8,128)(2,1)} %get-tuple-element.23), channel_id=1, source_target_pairs={{0,1},{1,2},{2,3},{3,4},{4,5},{5,6},{6,7},{7,8},{8,9},{9,10},{10,1... | collective-permute-start | bytes 688136 | tf_op jit(solution)/shard_map/ppermute | solution.py:525
  7.5 20.5 %copy-start.11 = (bf16[1024,256]{1,0:T(8,128)(2,1)S(1)}, bf16[1024,256]{1,0:T(8,128)(2,1)}, u32[]{:S(2)}) copy-start(bf16[1024,256]{1,0:T(8,128)(2,1)} %get-tuple-element.29) | copy-start | bytes 1572868
  7.5 23.8 %copy-start.10 = (bf16[1024,256]{1,0:T(8,128)(2,1)S(1)}, bf16[1024,256]{1,0:T(8,128)(2,1)}, u32[]{:S(2)}) copy-start(bf16[1024,256]{1,0:T(8,128)(2,1)} %get-tuple-element.30) | copy-start | bytes 1572868
  7.5 25.2 %copy-start.9 = (bf16[128,19]{0,1:T(8,128)(2,1)S(1)}, bf16[128,19]{0,1:T(8,128)(2,1)}, u32[]{:S(2)}) copy-start(bf16[128,19]{0,1:T(8,128)(2,1)} %param.23) | copy-start | bytes 14596
  7.5 8.4 %collective-permute-start.1 = (bf16[448,256]{1,0:T(8,128)(2,1)}, bf16[448,256]{1,0:T(8,128)(2,1)S(1)}, u32[]{:S(2)}, u32[]{:S(2)}) collective-permute-start(bf16[448,256]{1,0:T(8,128)(2,1)} %get-tuple-element.24), channel_id=1, source_target_pairs={{1,0},{2,1},{3,2},{4,3},{5,4},{6,5},{7,6},{8,7},{9,8},{10,9},{11,1... | collective-permute-start | bytes 688136 | tf_op jit(solution)/shard_map/ppermute | solution.py:526
  18.0 0.8 copy-start.1
  18.8 27.9 %all-to-all-start = ((bf16[16,144,128]{2,1,0:T(8,128)(2,1)}), bf16[16,144,128]{2,1,0:T(8,128)(2,1)S(1)}, u32[]{:S(2)}, u32[]{:S(2)}) async-start(bf16[16,144,128]{2,1,0:T(8,128)(2,1)} %get-tuple-element.25), calls=%async_computation | async-start | bytes 1179648 | tf_op jit(solution)/shard_map/all_to_all | solution.py:35
  28.0 15.9 %collective-permute-start.2 = (bf16[1024,256]{1,0:T(8,128)(2,1)S(1)}, bf16[1024,256]{1,0:T(8,128)(2,1)S(1)}, u32[]{:S(2)}, u32[]{:S(2)}) collective-permute-start(bf16[1024,256]{1,0:T(8,128)(2,1)S(1)} %copy-done.11), channel_id=1, source_target_pairs={{0,1},{1,2},{2,3},{3,4},{4,5},{5,6},{6,7},{7,8},{8,9},{9,10},{10,1... | collective-permute-start | bytes 1572872 | tf_op jit(solution)/shard_map/ppermute | solution.py:527
  31.4 15.3 %collective-permute-start.3 = (bf16[1024,256]{1,0:T(8,128)(2,1)S(1)}, bf16[1024,256]{1,0:T(8,128)(2,1)S(1)}, u32[]{:S(2)}, u32[]{:S(2)}) collective-permute-start(bf16[1024,256]{1,0:T(8,128)(2,1)S(1)} %copy-done.10), channel_id=1, source_target_pairs={{1,0},{2,1},{3,2},{4,3},{5,4},{6,5},{7,6},{8,7},{9,8},{10,9},{11,1... | collective-permute-start | bytes 1572872 | tf_op jit(solution)/shard_map/ppermute | solution.py:528
  32.7 34.9 %copy-start.8 = (bf16[32,128]{1,0:T(8,128)(2,1)}, bf16[32,128]{1,0:T(8,128)(2,1)S(1)}, u32[]{:S(2)}) copy-start(bf16[32,128]{1,0:T(8,128)(2,1)S(1)} %pad.4.class_t) | copy-start | bytes 24580
  43.9 2.7 %copy-start.5 = (bf16[1024,256]{1,0:T(8,128)(2,1)}, bf16[1024,256]{1,0:T(8,128)(2,1)S(1)}, u32[]{:S(2)}) copy-start(bf16[1024,256]{1,0:T(8,128)(2,1)S(1)} %collective-permute-done.2.before) | copy-start | bytes 1572868
  46.7 0.8 copy-start.6
  46.7 1.0 copy-start.4
  61.3 12.9 %all-to-all-start.1 = ((f32[16,8,128]{2,1,0:T(8,128)}), f32[16,8,128]{2,1,0:T(8,128)S(1)}, u32[]{:S(2)}, u32[]{:S(2)}) async-start(f32[16,8,128]{2,1,0:T(8,128)} %get-tuple-element.33), calls=%async_computation.1 | async-start | bytes 131072 | tf_op jit(solution)/shard_map/all_to_all | solution.py:35
  74.2 0.6 copy-start.7

commit v5 on v4

--- a/solution.py
+++ b/solution.py
@@ -342,7 +342,7 @@
     wait_w.wait()
     for i, wide in enumerate((wide0, wide1, wide2)):
         fill_pair(weights.at[i], wide, HEAD)
-    fold = 4
+    fold = 2
 
     def step(q, carry):
         base = q * (2 * fold)
@@ -468,7 +468,9 @@
     for v in (terms, counts):
         v = jnp.sum(v, axis=0, keepdims=True)
         out.append(sum(v[:, i * HEAD : (i + 1) * HEAD] for i in range(v.shape[1] // HEAD)))
-    both = jnp.concatenate(out, axis=0)
+    lane = lax.broadcasted_iota(jnp.int32, out[0].shape, 1)
+    folded = [v + pltpu.roll(v, HEAD // 2, 1) for v in out]
+    both = jnp.where(lane < HEAD // 2, folded[0], folded[1])
     for i in range(pieces.shape[0]):
         pieces[i] = both
 
@@ -608,7 +610,7 @@
     class_t3 = jnp.concatenate([class_t] * 3, axis=1)
     logits, pieces = pl.pallas_call(
         final_kernel,
-        out_shape=[shaped((classes, q_rows, q_cols), BF16), shaped((devices, 2, HEAD), F32)],
+        out_shape=[shaped((classes, q_rows, q_cols), BF16), shaped((devices, 1, HEAD), F32)],
         in_specs=[SM, SM] + [VM] * 16 + [ANY],
         out_specs=[VM, VM],
         scratch_shapes=[
@@ -624,7 +626,8 @@
         place, class_bias, got, norm_gain, norm_shift, inner0, outer0, inner1, outer1, stats4, stats6,
         labels[0], class_t, class_t3, up_cols, c1, c4, c6, c0,
     )
-    loss_total, valid_count = jnp.sum(everyone(pieces, EVERY), axis=(0, 2))
+    sums_of = jnp.sum(everyone(pieces, EVERY), axis=(0, 1))
+    loss_total, valid_count = jnp.sum(sums_of[: HEAD // 2]), jnp.sum(sums_of[HEAD // 2 :])
     mean_loss = loss_total / jnp.maximum(valid_count, 1.0)
     return (logits[None], mean_loss)
 

time: 104 us -> 104 us (level)
  transfers between devices with their start and end apart: 6 -> 6, of which waited for: 5 -> 5; matrix products, arithmetic and copies ran while one was open for 1% -> 1% of each run, Pallas kernels for 8% -> 9%
where the time goes in v5:
time: 104 us; the launch traced here: 103 us
  Pallas kernels  32.6 us (31%)
  starting transfers between devices  25.6 us (25%)
  blocking collectives  19.7 us (19%)
  waiting for transfers between devices  18.1 us (17%)
  between operations  3.15 us (3%)
  local copies, waits for them, and re-layouts  2.42 us (2%)
  other arithmetic  1.43 us (1%)
    all_to_all x1, blocking collectives, everyone(): return lax.all_to_all(pieces, axes, 0, 0)  19.7 us
    all_to_all x2, starting transfers between devices, everyone(): return lax.all_to_all(pieces, axes, 0, 0)  15.5 us
    pallas_call x1, Pallas kernels, device_step(): pl.pallas_call(between_kernel, out_shape=[field0, field1, stats_shape(2),...  13.5 us
    pallas_call x1, Pallas kernels, device_step(): pl.pallas_call(inner_kernel, out_shape=[field0, field1, stats_shape(insid...  8.78 us
    all_to_all x2, waiting for transfers between devices, everyone(): return lax.all_to_all(pieces, axes, 0, 0)  5.9 us
    pallas_call x1, Pallas kernels, device_step(): pl.pallas_call(final_kernel, out_shape=[shaped((classes, q_rows, q_cols),...  5.53 us
    ppermute x1, starting transfers between devices, device_step(): small_before = lax.ppermute(small_before, ROWS, up_pairs)  4.03 us
    ppermute x1, waiting for transfers between devices, device_step(): small_after = lax.ppermute(small_after, ROWS, down_pairs)  3.9 us
  transfers between devices with their start and end apart: 6, of which 5 were waited for; matrix products, arithmetic and copies ran while one was open for 1% of the time, Pallas kernels for 9%

profile of v5, /device:TPU:1, one launch (start us, length us, event | category | flops | bytes accessed | tf_op | source)
XLA Modules:
  0.0 103.0 jit_solution(2315967577915374478)
XLA Ops:
  0.6 0.0 copy-start
  0.6 0.0 copy-start.2
  0.7 0.0 copy-start.3
  0.7 2.8 %edges.1 = (bf16[448,256]{1,0:T(8,128)(2,1)}, bf16[448,256]{1,0:T(8,128)(2,1)}, bf16[1024,256]{1,0:T(8,128)(2,1)}, bf16[1024,256]{1,0:T(8,128)(2,1)}) custom-call(bf16[16,512,256]{2,1,0:T(8,128)(2,1)} %bitcast.12, bf16[8,256,256]{2,1,0:T(8,128)(2,1)} %bitcast.15, bf16[4,128,256]{2,1,0:T(8,128)(2,1)} %bitcast.8, bf16[2,64,256]{2,1,0:T(8,128)(2,1)} %bitcast.10), custom_call_target="tpu_custom_call" | custom-call | tf_op jit(solution)/shard_map/edges/pallas_call | solution.py:518
  3.5 4.0 %collective-permute-start = (bf16[448,256]{1,0:T(8,128)(2,1)}, bf16[448,256]{1,0:T(8,128)(2,1)S(1)}, u32[]{:S(2)}, u32[]{:S(2)}) collective-permute-start(bf16[448,256]{1,0:T(8,128)(2,1)} %get-tuple-element.23), channel_id=1, source_target_pairs={{0,1},{1,2},{2,3},{3,4},{4,5},{5,6},{6,7},{7,8},{8,9},{9,10},{10,1... | collective-permute-start | bytes 688136 | tf_op jit(solution)/shard_map/ppermute | solution.py:527
  7.5 0.0 copy-start.11
  7.5 0.0 copy-start.10
  7.5 0.0 copy-start.9
  7.5 1.4 %collective-permute-start.1 = (bf16[448,256]{1,0:T(8,128)(2,1)}, bf16[448,256]{1,0:T(8,128)(2,1)S(1)}, u32[]{:S(2)}, u32[]{:S(2)}) collective-permute-start(bf16[448,256]{1,0:T(8,128)(2,1)} %get-tuple-element.24), channel_id=1, source_target_pairs={{1,0},{2,1},{3,2},{4,3},{5,4},{6,5},{7,6},{8,7},{9,8},{10,9},{11,1... | collective-permute-start | bytes 688136 | tf_op jit(solution)/shard_map/ppermute | solution.py:528
  9.0 3.1 %collective-permute-done.before = bf16[448,256]{1,0:T(8,128)(2,1)S(1)} collective-permute-done((bf16[448,256]{1,0:T(8,128)(2,1)}, bf16[448,256]{1,0:T(8,128)(2,1)S(1)}, u32[]{:S(2)}, u32[]{:S(2)}) %collective-permute-start) | collective-permute-done | bytes 229408 | tf_op jit(solution)/shard_map/ppermute | solution.py:527
  12.1 3.9 %collective-permute-done.1.after = bf16[448,256]{1,0:T(8,128)(2,1)S(1)} collective-permute-done((bf16[448,256]{1,0:T(8,128)(2,1)}, bf16[448,256]{1,0:T(8,128)(2,1)S(1)}, u32[]{:S(2)}, u32[]{:S(2)}) %collective-permute-start.1) | collective-permute-done | bytes 229408 | tf_op jit(solution)/shard_map/ppermute | solution.py:528
  16.0 0.0 copy-done
  16.0 0.0 copy-done.2
  16.0 0.0 copy-done.3
  16.0 2.0 %coarse.1 = (f32[8,128,128]{2,1,0:T(8,128)S(1)}, bf16[16,144,128]{2,1,0:T(8,128)(2,1)}) custom-call(bf16[448,256]{1,0:T(8,128)(2,1)S(1)} %collective-permute-done.before, bf16[448,256]{1,0:T(8,128)(2,1)S(1)} %collective-permute-done.1.after, bf16[4,128,256]{2,1,0:T(8,128)(2,1)S(1)} %bitcast.9, bf16[2,64,256]{2,1,0:T(8,128)(2,1)S(1)} %bitcast.11, ...), custom_call_target="tpu_custom_call" | custom-call | tf_op jit(solution)/shard_map/coarse/pallas_call | solution.py:559
  18.0 0.0 copy-start.1
  18.0 0.8 copy-done.1
  18.8 9.2 %all-to-all-start = ((bf16[16,144,128]{2,1,0:T(8,128)(2,1)}), bf16[16,144,128]{2,1,0:T(8,128)(2,1)S(1)}, u32[]{:S(2)}, u32[]{:S(2)}) async-start(bf16[16,144,128]{2,1,0:T(8,128)(2,1)} %get-tuple-element.25), calls=%async_computation | async-start | bytes 1179648 | tf_op jit(solution)/shard_map/all_to_all | solution.py:35
  28.0 0.0 copy-done.11
  28.0 3.3 %collective-permute-start.2 = (bf16[1024,256]{1,0:T(8,128)(2,1)S(1)}, bf16[1024,256]{1,0:T(8,128)(2,1)S(1)}, u32[]{:S(2)}, u32[]{:S(2)}) collective-permute-start(bf16[1024,256]{1,0:T(8,128)(2,1)S(1)} %copy-done.11), channel_id=1, source_target_pairs={{0,1},{1,2},{2,3},{3,4},{4,5},{5,6},{6,7},{7,8},{8,9},{9,10},{10,1... | collective-permute-start | bytes 1572872 | tf_op jit(solution)/shard_map/ppermute | solution.py:529
  31.3 0.0 copy-done.10
  31.3 1.3 %collective-permute-start.3 = (bf16[1024,256]{1,0:T(8,128)(2,1)S(1)}, bf16[1024,256]{1,0:T(8,128)(2,1)S(1)}, u32[]{:S(2)}, u32[]{:S(2)}) collective-permute-start(bf16[1024,256]{1,0:T(8,128)(2,1)S(1)} %copy-done.10), channel_id=1, source_target_pairs={{1,0},{2,1},{3,2},{4,3},{5,4},{6,5},{7,6},{8,7},{9,8},{10,9},{11,1... | collective-permute-start | bytes 1572872 | tf_op jit(solution)/shard_map/ppermute | solution.py:530
  32.6 0.0 copy-done.9
  32.7 0.0 copy-start.8
  32.7 8.8 %inner.1 = (bf16[16,512,128]{2,1,0:T(8,128)(2,1)}, bf16[10,256,128]{2,1,0:T(8,128)(2,1)}, f32[6,8,256]{2,1,0:T(8,128)}, f32[3,8,256]{2,1,0:T(8,128)}) custom-call(bf16[16,512,256]{2,1,0:T(8,128)(2,1)} %bitcast.13, bf16[8,256,256]{2,1,0:T(8,128)(2,1)} %bitcast.16, bf16[4,3,3,256,128]{4,3,2,1,0:T(8,128)(2,1)} %first_weights.1, f32[8,128,128]{2,1,0:T(8,128)} %copy-done.1), custom_call_target="tpu_custom_call" | custom-call | tf_op jit(solution)/shard_map/inner/pallas_call | solution.py:564
  41.5 2.4 %collective-permute-done.2.before = bf16[1024,256]{1,0:T(8,128)(2,1)S(1)} collective-permute-done((bf16[1024,256]{1,0:T(8,128)(2,1)S(1)}, bf16[1024,256]{1,0:T(8,128)(2,1)S(1)}, u32[]{:S(2)}, u32[]{:S(2)}) %collective-permute-start.2) | collective-permute-done | bytes 524320 | tf_op jit(solution)/shard_map/ppermute | solution.py:529
  43.9 0.0 copy-start.5
  43.9 2.7 %collective-permute-done.3.after = bf16[1024,256]{1,0:T(8,128)(2,1)S(1)} collective-permute-done((bf16[1024,256]{1,0:T(8,128)(2,1)S(1)}, bf16[1024,256]{1,0:T(8,128)(2,1)S(1)}, u32[]{:S(2)}, u32[]{:S(2)}) %collective-permute-start.3) | collective-permute-done | bytes 524320 | tf_op jit(solution)/shard_map/ppermute | solution.py:530
  46.7 0.0 copy-start.6
  46.7 0.0 all-to-all-done.got
  46.7 0.0 copy-start.4
  46.7 0.0 copy-done.5
  46.7 0.8 copy-done.6
  47.5 0.2 copy-done.4
  47.6 13.5 %between.1 = (bf16[16,512,128]{2,1,0:T(8,128)(2,1)}, bf16[10,256,128]{2,1,0:T(8,128)(2,1)}, f32[2,8,256]{2,1,0:T(8,128)}, f32[2,8,256]{2,1,0:T(8,128)}, bf16[10,...) custom-call(s32[1]{0:T(128)} %bitcast.place, ...), custom_call_target="tpu_custom_call", output_to_operand_aliasing={{0}: (15, {}), {1}: (16, {})} | custom-call | tf_op jit(solution)/shard_map/between/pallas_call | solution.py:580
  61.2 6.3 %all-to-all-start.1 = ((f32[16,8,128]{2,1,0:T(8,128)}), f32[16,8,128]{2,1,0:T(8,128)S(1)}, u32[]{:S(2)}, u32[]{:S(2)}) async-start(f32[16,8,128]{2,1,0:T(8,128)} %get-tuple-element.33), calls=%async_computation.1 | async-start | bytes 131072 | tf_op jit(solution)/shard_map/all_to_all | solution.py:35
  67.5 0.0 copy-done.8
  67.5 0.6 pad_maximum_fusion.class_t3
  68.1 5.9 %all-to-all-done.1.got = f32[16,8,128]{2,1,0:T(8,128)S(1)} async-done(((f32[16,8,128]{2,1,0:T(8,128)}), f32[16,8,128]{2,1,0:T(8,128)S(1)}, u32[]{:S(2)}, u32[]{:S(2)}) %all-to-all-start.1) | async-done | bytes 65568 | tf_op jit(solution)/shard_map/all_to_all | solution.py:35
  74.0 0.0 copy-start.7
  74.0 0.6 copy-done.7
  74.6 5.5 %final.1 = (bf16[19,16,512]{2,1,0:T(8,128)(2,1)}, f32[128,1,128]{2,1,0:T(1,128)}) custom-call(s32[1]{0:T(128)} %bitcast.place, f32[19]{0:T(128)} %bias.1, f32[16,8,128]{2,1,0:T(8,128)} %copy-done.7, f32[7,128]{1,0:T(8,128)} %gain.3, f32[7,128]{1,0:T(8,128)} %shift.3, f32[6,8,256]{2,1,0:T(8,128)} %get-tuple-element.27.inner0, ...), custom_call_target="tpu_custom_call" | custom-call | tf_op jit(solution)/shard_map/final/pallas_call | solution.py:611
  80.2 19.7 %all_to_all.15 = f32[128,1,128]{2,1,0:T(1,128)S(1)} all-to-all(f32[128,1,128]{2,1,0:T(1,128)} %get-tuple-element.43), channel_id=1, replica_groups=mesh['batch_0'=4,'batch_1'=2,'rows_0'=4,'rows_1'=4] {'batch_0','batch_1'..., dimensions={0} | all-to-all | bytes 131072 | tf_op jit(solution)/shard_map/all_to_all | solution.py:35
  99.9 0.2 reduce_sum.27
  100.0 0.7 slice_reduce_fusion
  (1 shorter events, 0.0 us)
Async XLA Ops:
  0.6 15.3 %copy-start = (bf16[4,3,3,256,128]{4,3,2,1,0:T(8,128)(2,1)S(1)}, bf16[4,3,3,256,128]{4,3,2,1,0:T(8,128)(2,1)}, u32[]{:S(2)}) copy-start(bf16[4,3,3,256,128]{4,3,2,1,0:T(8,128)(2,1)} %first_weights.1) | copy-start | bytes 7077892
  0.6 15.3 %copy-start.2 = (bf16[1,4,128,256]{3,2,1,0:T(8,128)(2,1)S(1)}, bf16[1,4,128,256]{3,2,1,0:T(8,128)(2,1)}, u32[]{:S(2)}) copy-start(bf16[1,4,128,256]{3,2,1,0:T(8,128)(2,1)} %param.16) | copy-start | bytes 786436
  0.7 15.3 %copy-start.3 = (bf16[1,2,64,256]{3,2,1,0:T(8,128)(2,1)S(1)}, bf16[1,2,64,256]{3,2,1,0:T(8,128)(2,1)}, u32[]{:S(2)}) copy-start(bf16[1,2,64,256]{3,2,1,0:T(8,128)(2,1)} %param.17) | copy-start | bytes 196612
  3.5 8.6 %collective-permute-start = (bf16[448,256]{1,0:T(8,128)(2,1)}, bf16[448,256]{1,0:T(8,128)(2,1)S(1)}, u32[]{:S(2)}, u32[]{:S(2)}) collective-permute-start(bf16[448,256]{1,0:T(8,128)(2,1)} %get-tuple-element.23), channel_id=1, source_target_pairs={{0,1},{1,2},{2,3},{3,4},{4,5},{5,6},{6,7},{7,8},{8,9},{9,10},{10,1... | collective-permute-start | bytes 688136 | tf_op jit(solution)/shard_map/ppermute | solution.py:527
  7.5 20.5 %copy-start.11 = (bf16[1024,256]{1,0:T(8,128)(2,1)S(1)}, bf16[1024,256]{1,0:T(8,128)(2,1)}, u32[]{:S(2)}) copy-start(bf16[1024,256]{1,0:T(8,128)(2,1)} %get-tuple-element.29) | copy-start | bytes 1572868
  7.5 23.8 %copy-start.10 = (bf16[1024,256]{1,0:T(8,128)(2,1)S(1)}, bf16[1024,256]{1,0:T(8,128)(2,1)}, u32[]{:S(2)}) copy-start(bf16[1024,256]{1,0:T(8,128)(2,1)} %get-tuple-element.30) | copy-start | bytes 1572868
  7.5 25.1 %copy-start.9 = (bf16[128,19]{0,1:T(8,128)(2,1)S(1)}, bf16[128,19]{0,1:T(8,128)(2,1)}, u32[]{:S(2)}) copy-start(bf16[128,19]{0,1:T(8,128)(2,1)} %param.23) | copy-start | bytes 14596
  7.5 8.4 %collective-permute-start.1 = (bf16[448,256]{1,0:T(8,128)(2,1)}, bf16[448,256]{1,0:T(8,128)(2,1)S(1)}, u32[]{:S(2)}, u32[]{:S(2)}) collective-permute-start(bf16[448,256]{1,0:T(8,128)(2,1)} %get-tuple-element.24), channel_id=1, source_target_pairs={{1,0},{2,1},{3,2},{4,3},{5,4},{6,5},{7,6},{8,7},{9,8},{10,9},{11,1... | collective-permute-start | bytes 688136 | tf_op jit(solution)/shard_map/ppermute | solution.py:528
  18.0 0.8 copy-start.1
  18.8 27.9 %all-to-all-start = ((bf16[16,144,128]{2,1,0:T(8,128)(2,1)}), bf16[16,144,128]{2,1,0:T(8,128)(2,1)S(1)}, u32[]{:S(2)}, u32[]{:S(2)}) async-start(bf16[16,144,128]{2,1,0:T(8,128)(2,1)} %get-tuple-element.25), calls=%async_computation | async-start | bytes 1179648 | tf_op jit(solution)/shard_map/all_to_all | solution.py:35
  28.0 15.9 %collective-permute-start.2 = (bf16[1024,256]{1,0:T(8,128)(2,1)S(1)}, bf16[1024,256]{1,0:T(8,128)(2,1)S(1)}, u32[]{:S(2)}, u32[]{:S(2)}) collective-permute-start(bf16[1024,256]{1,0:T(8,128)(2,1)S(1)} %copy-done.11), channel_id=1, source_target_pairs={{0,1},{1,2},{2,3},{3,4},{4,5},{5,6},{6,7},{7,8},{8,9},{9,10},{10,1... | collective-permute-start | bytes 1572872 | tf_op jit(solution)/shard_map/ppermute | solution.py:529
  31.3 15.3 %collective-permute-start.3 = (bf16[1024,256]{1,0:T(8,128)(2,1)S(1)}, bf16[1024,256]{1,0:T(8,128)(2,1)S(1)}, u32[]{:S(2)}, u32[]{:S(2)}) collective-permute-start(bf16[1024,256]{1,0:T(8,128)(2,1)S(1)} %copy-done.10), channel_id=1, source_target_pairs={{1,0},{2,1},{3,2},{4,3},{5,4},{6,5},{7,6},{8,7},{9,8},{10,9},{11,1... | collective-permute-start | bytes 1572872 | tf_op jit(solution)/shard_map/ppermute | solution.py:530
  32.7 34.8 %copy-start.8 = (bf16[32,128]{1,0:T(8,128)(2,1)}, bf16[32,128]{1,0:T(8,128)(2,1)S(1)}, u32[]{:S(2)}) copy-start(bf16[32,128]{1,0:T(8,128)(2,1)S(1)} %pad.4.class_t) | copy-start | bytes 24580
  43.9 2.7 %copy-start.5 = (bf16[1024,256]{1,0:T(8,128)(2,1)}, bf16[1024,256]{1,0:T(8,128)(2,1)S(1)}, u32[]{:S(2)}) copy-start(bf16[1024,256]{1,0:T(8,128)(2,1)S(1)} %collective-permute-done.2.before) | copy-start | bytes 1572868
  46.7 0.8 copy-start.6
  46.7 1.0 copy-start.4
  61.2 12.8 %all-to-all-start.1 = ((f32[16,8,128]{2,1,0:T(8,128)}), f32[16,8,128]{2,1,0:T(8,128)S(1)}, u32[]{:S(2)}, u32[]{:S(2)}) async-start(f32[16,8,128]{2,1,0:T(8,128)} %get-tuple-element.33), calls=%async_computation.1 | async-start | bytes 131072 | tf_op jit(solution)/shard_map/all_to_all | solution.py:35
  74.0 0.6 copy-start.7
